TPU v7x, 32 devices: a whole 2x2x4 slice. The times are simulated.
32 devices in a mesh: dp: 8 (over z, y), mp: 4 (over x, core).
Axes of the slice: x: 2, y: 2, z: 4, core: 2. Of those that a mesh axis runs over, the one named last changes fastest.
Arguments:
- pixels: bfloat16 [128, 256, 768], P('dp', 'mp'), may hold values from -6 to 6
- selection: int32 [128], P('dp'), may hold values from 0 to 1, as said below
- destination: int32 [128], P('dp'), may hold values from 0 to 7, as said below
- patch_weight: bfloat16 [768, 1024], replicated, may hold values from -0.21875 to 0.21875
- position: bfloat16 [256, 1024], P('mp'), may hold values from -6 to 6
- query_key_value: bfloat16 [3, 1024, 1024], P(None, None, 'mp'), may hold values from -1 to 1
- output_weight: bfloat16 [1024, 1024], P('mp'), may hold values from -0.1875 to 0.1875
- up_weight: bfloat16 [1024, 4096], P(None, 'mp'), may hold values from -0.1875 to 0.1875
- down_weight: bfloat16 [4096, 1024], P('mp'), may hold values from -0.09375 to 0.09375
- norm_gains: float32 [3, 1024], replicated, may hold values from 0.25 to 1.75
- embedding_weight: bfloat16 [1024, 1024], replicated, may hold values from -0.1875 to 0.1875
- caption_vectors: bfloat16 [128, 1024], P('dp'), may hold values from -6 to 6
- loss_params: float32 [2], replicated, may hold values from -1 to 1
Outputs:
- image_embedding: float32 [32, 1024], P('dp')
- pair_loss: float32 [32], P('dp')
Inputs may be any that keep to these rules, and one draw needn't show every extreme that they name: `selection`: exactly 16 examples are selected in all; each index of dp holds between 1 and 3 of them, and some holds exactly 3. Among selected examples, at most 4 have the same destination, some destination has exactly 4, and no index of dp holds two selected examples with the same destination. Destinations of unselected examples are arbitrary.
All inputs are finite; a program needn't handle non-finite values.
Results may differ from a plain program's by a relative error of at most 0.0031.
Values may be sent and summed in bfloat16 or wider, within the bound.
No kernel may reach another device: no remote copies, remote signals or barrier semaphores. Data moves between devices by JAX's collectives and lax.ppermute only.
A program may use at most 128 MiB of HBM per device.

v0:
```python
import jax
import jax.numpy as jnp
from jax import lax
from jax.sharding import PartitionSpec as P

HEAD_DIM = 64
PATCHES = 256
SEL_DEV = 2
SEND_MOST = 3
RECV_MOST = 4


EPS = 1e-06


def layer_norm(values, gain):
    center = jnp.mean(values, axis=-1, keepdims=True)
    centred = values - center
    spread = jnp.mean(centred * centred, axis=-1, keepdims=True)
    return centred * lax.rsqrt(spread + EPS) * gain


def unit_rows(values):
    scale = lax.rsqrt(jnp.mean(values * values, axis=-1, keepdims=True) + EPS)
    return values * scale * values.shape[-1] ** (-0.5)


def compact(members, labels, capacity):
    present = (labels > 0).astype(jnp.int32)
    running = jnp.cumsum(present)
    wanted = jnp.arange(capacity, dtype=jnp.int32)
    source = jnp.sum((running[None, :] <= wanted[:, None]).astype(jnp.int32), axis=1)
    source = jnp.minimum(source, labels.shape[0] - 1)
    filled = wanted < running[-1]
    picked = tuple((member[source] for member in members))
    return (picked, jnp.where(filled, labels[source] - 1, -1).astype(jnp.int32))


def encode(
    images,
    patch_weight,
    position,
    query_key_value,
    output_weight,
    up_weight,
    down_weight,
    norm_gains,
):
    hidden = jnp.einsum("rpc,cd->prd", images, patch_weight, preferred_element_type=jnp.float32)
    hidden = hidden + position.astype(jnp.float32)[:, None, :]
    normed = layer_norm(hidden, norm_gains[0]).astype(jnp.bfloat16)
    projected = jnp.einsum(
        "prd,tdk->rptk",
        lax.all_gather(normed, "mp", axis=0, tiled=True),
        query_key_value,
        preferred_element_type=jnp.float32,
    ).astype(jnp.bfloat16)
    image_count = projected.shape[0]
    length = projected.shape[1]
    heads_here = projected.shape[3] // HEAD_DIM
    shaped = projected.reshape(image_count, length, 3, heads_here, HEAD_DIM)
    scores = jnp.einsum(
        "rqhd,rkhd->rhqk", shaped[:, :, 0], shaped[:, :, 1], preferred_element_type=jnp.float32
    ) * HEAD_DIM ** (-0.5)
    weights = jax.nn.softmax(scores, axis=-1).astype(jnp.bfloat16)
    context = jnp.einsum(
        "rhqk,rkhd->rqhd", weights, shaped[:, :, 2], preferred_element_type=jnp.float32
    ).astype(jnp.bfloat16)
    context = context.reshape(image_count, length, heads_here * HEAD_DIM)
    segment = context
    hidden = hidden + lax.psum_scatter(
        jnp.einsum("rpk,kd->prd", segment, output_weight, preferred_element_type=jnp.float32),
        "mp",
        scatter_dimension=0,
        tiled=True,
    )
    normed = layer_norm(hidden, norm_gains[1]).astype(jnp.bfloat16)
    expanded = jax.nn.gelu(
        jnp.einsum(
            "prd,df->prf",
            lax.all_gather(normed, "mp", axis=0, tiled=True),
            up_weight,
            preferred_element_type=jnp.float32,
        )
    ).astype(jnp.bfloat16)
    segment = expanded
    hidden = hidden + lax.psum_scatter(
        jnp.einsum("prf,fd->prd", segment, down_weight, preferred_element_type=jnp.float32),
        "mp",
        scatter_dimension=0,
        tiled=True,
    )
    return lax.psum(jnp.sum(hidden, axis=0), "mp") / PATCHES


def per_device(
    pixels,
    selection,
    destination,
    patch_weight,
    position,
    query_key_value,
    output_weight,
    up_weight,
    down_weight,
    norm_gains,
    embedding_weight,
    caption_vectors,
    loss_params,
):
    devices_dp = lax.axis_size("dp")
    local_count = selection.shape[0]
    example_ids = lax.axis_index("dp") * local_count + jnp.arange(local_count, dtype=jnp.int32)
    chosen = selection > 0
    local_rank = jnp.cumsum(selection) - 1
    layer_weights = (
        patch_weight,
        position,
        query_key_value,
        output_weight,
        up_weight,
        down_weight,
        norm_gains,
    )
    picker = chosen[None, :] & (
        local_rank[None, :] == jnp.arange(SEND_MOST, dtype=jnp.int32)[:, None]
    )
    caption_rows = jnp.dot(
        picker.astype(jnp.bfloat16), caption_vectors, preferred_element_type=jnp.float32
    ).astype(jnp.bfloat16)
    caption_ids = jnp.sum(jnp.where(picker, example_ids[None, :] + 1, 0), axis=1) - 1
    all_captions, all_caption_ids = (
        lax.all_gather(caption_rows, "dp", axis=0, tiled=True),
        lax.all_gather(caption_ids, "dp", axis=0, tiled=True),
    )
    sorter = (destination[None, :] == jnp.arange(devices_dp, dtype=jnp.int32)[:, None]) & chosen[
        None, :
    ]
    outgoing = jnp.einsum(
        "se,epc->spc", sorter.astype(jnp.bfloat16), pixels, preferred_element_type=jnp.float32
    ).astype(jnp.bfloat16)
    tagged_ids = jnp.sum(jnp.where(sorter, example_ids[None, :] + 1, 0), axis=1)
    arrived, arrived_ids = (
        lax.all_to_all(outgoing, "dp", split_axis=0, concat_axis=0, tiled=True),
        lax.all_to_all(tagged_ids, "dp", split_axis=0, concat_axis=0, tiled=True),
    )
    picked, slot_ids = compact((arrived,), arrived_ids, RECV_MOST)
    pooled = encode(picked[0], *layer_weights)
    live = slot_ids >= 0
    normed = layer_norm(pooled, norm_gains[2]).astype(jnp.bfloat16)
    embedded = jnp.dot(normed, embedding_weight, preferred_element_type=jnp.float32)
    embedded = jnp.where(live[:, None], embedded, 0.0)
    images_unit = unit_rows(embedded)
    captions_unit = unit_rows(all_captions.astype(jnp.float32))
    scale = 10.0 * jnp.exp(loss_params[0])
    shift = 2.0 * loss_params[1]
    logits = scale * jnp.dot(images_unit, captions_unit.T, precision=lax.Precision.HIGHEST) + shift
    signs = jnp.where(slot_ids[:, None] == all_caption_ids[None, :], 1.0, -1.0).astype(jnp.float32)
    caption_live = (all_caption_ids >= 0).astype(jnp.float32)
    terms = jax.nn.softplus(-signs * logits) * caption_live[None, :]
    losses = jnp.where(live, jnp.sum(terms, axis=1) / float(devices_dp * SEL_DEV), 0.0)
    return (embedded, losses)


def solution(mesh):
    in_specs = (
        P("dp", "mp", None),
        P("dp"),
        P("dp"),
        P(),
        P("mp", None),
        P(None, None, "mp"),
        P("mp", None),
        P(None, "mp"),
        P("mp", None),
        P(),
        P(),
        P("dp", None),
        P(),
    )
    out_specs = (P("dp", None), P("dp"))
    return jax.shard_map(
        per_device, mesh=mesh, in_specs=in_specs, out_specs=out_specs, check_vma=False
    )
```

profile of v0, /device:TPU:0, one launch (start us, length us, event | category | flops | bytes accessed | tf_op | source)
XLA Modules:
  0.0 234.0 jit_solution(14146244724643054699)
XLA Ops:
  7.2 0.8 broadcast_compare_fusion.1
  8.0 0.5 copy-done.10
  8.5 0.8 select_reduce_fusion
  9.3 0.7 copy.59
  10.0 7.3 %all-to-all-start = ((s32[8,1,1]{2,1,0:T(1,128)}), s32[8,1,1]{2,1,0:T(1,128)S(1)}, u32[]{:S(2)}, u32[]{:S(2)}) async-start(s32[8,1,1]{2,1,0:T(1,128)} %copy.59), calls=%async_computation | async-start | bytes 8192 | tf_op jit(solution)/shard_map/all_to_all | solution.py:145
  17.3 2.4 %fusion.33 = bf16[8,64,768]{2,0,1:T(8,128)(2,1)S(1)} fusion(bf16[16,64,768]{2,1,0:T(8,128)(2,1)} %param.13, s32[16]{0:T(128)} %param.15, pred[16]{0:T(512)(128)(4,1)S(1)} %broadcast_compare_fusion.1), kind=kOutput, calls=%fused_computation.35 | convolution fusion | flops 12976384 | bytes 2359376 | tf_op jit(solution)/shard_map/se,epc->spc/dot_general | solution.py:139
  19.7 1.0 copy.61
  20.7 3.0 %all-to-all-done = s32[8,1,1]{2,1,0:T(1,128)S(1)} async-done(((s32[8,1,1]{2,1,0:T(1,128)}), s32[8,1,1]{2,1,0:T(1,128)S(1)}, u32[]{:S(2)}, u32[]{:S(2)}) %all-to-all-start) | async-done | bytes 64 | tf_op jit(solution)/shard_map/all_to_all | solution.py:145
  23.7 3.5 %all-to-all-start.1 = ((bf16[8,64,768]{2,1,0:T(8,128)(2,1)}), bf16[8,64,768]{2,1,0:T(8,128)(2,1)S(1)}, u32[]{:S(2)}, u32[]{:S(2)}) async-start(bf16[8,64,768]{2,1,0:T(8,128)(2,1)} %copy.61), calls=%async_computation.1 | async-start | bytes 1572864 | tf_op jit(solution)/shard_map/all_to_all | solution.py:144
  27.4 0.4 fusion.88
  27.8 0.2 reduce-window.13
  28.1 0.6 pad_clamp_fusion
  28.7 17.7 %all-to-all-done.1 = bf16[8,64,768]{2,1,0:T(8,128)(2,1)S(1)} async-done(((bf16[8,64,768]{2,1,0:T(8,128)(2,1)}), bf16[8,64,768]{2,1,0:T(8,128)(2,1)S(1)}, u32[]{:S(2)}, u32[]{:S(2)}) %all-to-all-start.1) | async-done | bytes 786464 | tf_op jit(solution)/shard_map/all_to_all | solution.py:144
  46.4 0.7 gather_fusion.1
  47.1 2.1 fusion.92
  49.2 0.3 multiply_reduce_fusion.2
  49.5 0.7 copy-done.1
  50.2 1.0 multiply_convert_fusion.1
  51.3 21.6 %all-gather.4.cloned.1.call-done = bf16[256,4,1024]{2,0,1:T(8,128)(2,1)} async-done(((bf16[64,4,1024]{2,0,1:T(8,128)(2,1)}), bf16[256,4,1024]{2,0,1:T(8,128)(2,1)}) %all-gather.4.cloned.1.call-update) | async-done | bytes 2097168 | tf_op jit(solution)/shard_map/all_gather | solution.py:54
  72.9 3.9 %fusion.25 = bf16[256,4,3,256]{0,3,2,1:T(8,128)(2,1)S(1)} fusion(bf16[256,4,1024]{2,0,1:T(8,128)(2,1)} %all-gather.4.cloned.1.call-done, bf16[3,1024,256]{2,1,0:T(8,128)(2,1)} %param.18), kind=kOutput, calls=%fused_computation.29 | convolution fusion | flops 1611399168 | bytes 5242880 | tf_op jit(solution)/shard_map/prd,tdk->rptk/dot_general | solution.py:52
  76.8 0.8 fusion.50
  77.5 3.2 %fusion.93 = (f32[4,4,256]{2,1,0:T(4,128)S(1)}, f32[4,4,256,256]{2,3,1,0:T(8,128)S(1)}) fusion(f32[4,4,256,256]{2,3,1,0:T(8,128)S(1)} %fusion.50), kind=kOutput, calls=%fused_computation.121 | output fusion | flops 4194559 | bytes 8404992 | tf_op jit(solution)/shard_map/sub | solution.py:65
  80.8 0.5 fusion.42
  81.3 0.5 copy-done.2
  81.8 2.7 %convolution_bitcast_fusion = f32[256,4,1024]{2,0,1:T(8,128)} fusion(bf16[4,256,256]{1,2,0:T(8,128)(2,1)S(1)} %bitcast.84, bf16[256,1024]{1,0:T(8,128)(2,1)S(1)} %copy-done.2), kind=kOutput, calls=%fused_computation.16 | convolution fusion | flops 536870912 | bytes 5242880 | tf_op jit(solution)/shard_map/rpk,kd->prd/dot_general | solution.py:72
  84.6 44.6 %reduce-scatter.3.cloned.1.call-done = f32[64,4,1024]{2,0,1:T(8,128)} async-done(((f32[256,4,1024]{2,0,1:T(8,128)}), f32[64,4,1024]{2,0,1:T(8,128)}) %reduce-scatter.3.cloned.1.call-update) | async-done | bytes 1048592 | tf_op jit(solution)/shard_map/reduce_scatter | solution.py:71
  129.1 1.7 fusion.89
  130.9 0.3 multiply_reduce_fusion.1
  131.1 1.0 multiply_convert_fusion
  132.2 22.7 %all-gather.6.cloned.1.call-done = bf16[256,4,1024]{2,0,1:T(8,128)(2,1)} async-done(((bf16[64,4,1024]{2,0,1:T(8,128)(2,1)}), bf16[256,4,1024]{2,0,1:T(8,128)(2,1)}) %all-gather.6.cloned.1.call-update) | async-done | bytes 2097168 | tf_op jit(solution)/shard_map/all_gather | solution.py:81
  154.9 8.7 %fusion.12 = f32[256,4,1024]{2,0,1:T(8,128)} fusion(bf16[1024,1024]{1,0:T(8,128)(2,1)S(1)} %copy-done, bf16[256,4,1024]{2,0,1:T(8,128)(2,1)} %all-gather.6.cloned.1.call-done, bf16[1024,1024]{1,0:T(8,128)(2,1)} %param.20), kind=kOutput, calls=%fused_computation.17 | convolution fusion | flops 4304404480 | bytes 10485760 | tf_op jit(solution)/shard_map/prf,fd->prd/dot_general | solution.py:88
  163.7 0.6 copy-done.12
  164.4 0.6 dynamic-slice
  166.0 11.3 %all-reduce = s32[24]{0:T(128)S(1)} all-reduce(s32[24]{0:T(128)S(1)} %add_dynamic-update-slice_fusion), channel_id=1, replica_groups=mesh['dp'=8,'mp'=4] {'dp'}, use_global_device_ids=true, to_apply=%add | all-reduce | flops 24 | bytes 192
  177.4 0.1 fusion.43
  177.5 30.5 %all-gather = bf16[8,3,1024]{2,1,0:T(4,128)(2,1)S(1)} all-gather(bf16[1,3,1024]{2,1,0:T(4,128)(2,1)S(1)} %fusion.43), channel_id=1, replica_groups=mesh['dp'=8,'mp'=4] {'dp'}, dimensions={0}, use_global_device_ids=true | all-gather | bytes 55296 | tf_op jit(solution)/shard_map/all_gather | solution.py:133
  208.1 0.7 fusion.91
  210.1 0.1 multiply_reduce_fusion.3
  210.2 0.6 slice.28
  210.8 0.8 gather_fusion
  211.6 0.7 broadcast_compare_fusion
  212.3 1.5 add_reduce_fusion
  213.8 10.3 %psum.7 = f32[4,1024]{1,0:T(4,128)S(1)} all-reduce(f32[4,1024]{1,0:T(4,128)S(1)} %add_reduce_fusion), channel_id=1, replica_groups=mesh['dp'=8,'mp'=4] {'mp'}, use_global_device_ids=true, to_apply=%region_12.13 | all-reduce | flops 4096 | bytes 32768 | tf_op jit(solution)/shard_map/psum | solution.py:93
  224.0 0.1 multiply_reduce_fusion.6
  224.1 0.2 multiply_reduce_fusion.5
  224.3 2.1 multiply_reduce_fusion.4
  226.5 0.4 fusion.69
  226.9 0.5 multiply_select_fusion
  (58 shorter events, 1.0 us)
Async XLA Ops:
  7.2 147.7 %copy-start = (bf16[1024,1024]{1,0:T(8,128)(2,1)S(1)}, bf16[1024,1024]{1,0:T(8,128)(2,1)}, u32[]{:S(2)}) copy-start(bf16[1024,1024]{1,0:T(8,128)(2,1)} %param.21) | copy-start | bytes 6291460
  8.0 15.7 %copy-start.7 = (pred[16]{0:T(512)(128)(4,1)}, pred[16]{0:T(512)(128)(4,1)S(1)}, u32[]{:S(2)}) copy-start(pred[16]{0:T(512)(128)(4,1)S(1)} %broadcast_compare_fusion.1) | copy-start | bytes 52
  8.0 0.5 copy-start.10
  10.0 13.7 %all-to-all-start = ((s32[8,1,1]{2,1,0:T(1,128)}), s32[8,1,1]{2,1,0:T(1,128)S(1)}, u32[]{:S(2)}, u32[]{:S(2)}) async-start(s32[8,1,1]{2,1,0:T(1,128)} %copy.59), calls=%async_computation | async-start | bytes 8192 | tf_op jit(solution)/shard_map/all_to_all | solution.py:145
  19.7 7.6 %copy-start.3 = (bf16[64,1024]{1,0:T(8,128)(2,1)S(1)}, bf16[64,1024]{1,0:T(8,128)(2,1)}, u32[]{:S(2)}) copy-start(bf16[64,1024]{1,0:T(8,128)(2,1)} %param.17) | copy-start | bytes 393220
  19.7 7.7 %copy-start.6 = (f32[3,1024]{1,0:T(4,128)S(1)}, f32[3,1024]{1,0:T(4,128)}, u32[]{:S(2)}) copy-start(f32[3,1024]{1,0:T(4,128)} %param.22) | copy-start | bytes 36868
  23.7 22.7 %all-to-all-start.1 = ((bf16[8,64,768]{2,1,0:T(8,128)(2,1)}), bf16[8,64,768]{2,1,0:T(8,128)(2,1)S(1)}, u32[]{:S(2)}, u32[]{:S(2)}) async-start(bf16[8,64,768]{2,1,0:T(8,128)(2,1)} %copy.61), calls=%async_computation.1 | async-start | bytes 1572864 | tf_op jit(solution)/shard_map/all_to_all | solution.py:144
  27.3 45.6 %all-gather.4.cloned.1.call-start = ((), (), s32[]{:S(2)}) async-start(), calls=%async_computation.4 | async-start | bytes 2621440 | tf_op jit(solution)/shard_map/all_gather | solution.py:54
  28.0 0.7 copy-start.14
  49.2 1.0 copy-start.1
  51.2 77.9 %reduce-scatter.3.cloned.1.call-start = ((), (), s32[]{:S(2)}) async-start(), calls=%async_computation.5 | async-start | bytes 5242880 | tf_op jit(solution)/shard_map/reduce_scatter | solution.py:71
  80.8 1.0 copy-start.2
  84.5 70.4 %all-gather.6.cloned.1.call-start = ((), (), s32[]{:S(2)}) async-start(), calls=%async_computation.6 | async-start | bytes 2621440 | tf_op jit(solution)/shard_map/all_gather | solution.py:81
  132.2 80.1 %reduce-scatter.5.cloned.1.call-start = ((), (), s32[]{:S(2)}) async-start(), calls=%async_computation.7 | async-start | bytes 5242880 | tf_op jit(solution)/shard_map/reduce_scatter | solution.py:87
  163.6 0.7 copy-start.12
  163.6 0.8 copy-start.13
  163.6 2.1 copy-start.8
  163.6 2.1 copy-start.11
  163.6 13.7 %copy-start.4 = (bf16[16,1024]{1,0:T(8,128)(2,1)S(1)}, bf16[16,1024]{1,0:T(8,128)(2,1)}, u32[]{:S(2)}) copy-start(bf16[16,1024]{1,0:T(8,128)(2,1)} %param.24) | copy-start | bytes 98308
  163.6 44.4 %copy-start.9 = (f32[2]{0:T(128)S(1)}, f32[2]{0:T(128)}, u32[]{:S(2)}) copy-start(f32[2]{0:T(128)} %param.25) | copy-start | bytes 28
  163.7 46.6 %copy-start.15 = (s32[8,1]{0,1:T(1,128)S(1)}, s32[8,1]{0,1:T(1,128)}, u32[]{:S(2)}) copy-start(s32[8,1]{0,1:T(1,128)} %copy-done.14) | copy-start | bytes 100
  226.5 1.0 copy-start.5
Sparse Core Ops, SparseCore 0:
  51.3 21.5 all-gather.3
  84.6 44.4 reduce-scatter.2
  132.3 22.5 all-gather.5
  163.8 44.4 reduce-scatter.4
where the time goes:
time: 235 us; the launch traced here: 234 us
  waiting for transfers between devices  110 us (47%)
  blocking collectives  52.1 us (22%)
  matrix products  23.6 us (10%)
  between operations  16.1 us (7%)
  other arithmetic  13.9 us (6%)
  starting transfers between devices  11 us (5%)
  local copies, waits for them, and re-layouts  7.55 us (3%)
    reduce_scatter x1, waiting for transfers between devices, encode(): lax.psum_scatter(jnp.einsum('rpk,kd->prd', segment, output_weight, prefer...  44.6 us
    all_gather x2, waiting for transfers between devices, encode(): lax.all_gather(normed, 'mp', axis=0, tiled=True)  44.3 us
    all_gather x1, blocking collectives, per_device(): lax.all_gather(caption_rows, 'dp', axis=0, tiled=True)  30.5 us
    all_to_all x1, waiting for transfers between devices, per_device(): lax.all_to_all(outgoing, 'dp', split_axis=0, concat_axis=0, tiled=True)  17.7 us
    unnamed x1, blocking collectives  11.3 us
    psum x1, blocking collectives, encode(): return lax.psum(jnp.sum(hidden, axis=0), 'mp') / PATCHES  10.3 us
    dot_general x1, matrix products, encode(): jnp.einsum('prf,fd->prd', segment, down_weight, preferred_element_type=jn...  8.73 us
    all_to_all x1, starting transfers between devices, per_device(): lax.all_to_all(tagged_ids, 'dp', split_axis=0, concat_axis=0, tiled=True)  7.31 us
  transfers between devices with their start and end apart: 6, of which 5 were waited for; matrix products, arithmetic and copies ran while one was open for 4% of the time, Pallas kernels for 0%

commit v1 on v0

v1 whole, which is shorter than its diff:
```python
import functools

import jax
import jax.numpy as jnp
from jax import lax
from jax.experimental import pallas as pl
from jax.experimental.pallas import tpu as pltpu
from jax.sharding import PartitionSpec as P

HEAD_DIM = 64
SEL_DEV = 2
SEND_MOST = 3
RECV_MOST = 4
META = 128
EPS = 1e-06

VMEM = pltpu.MemorySpace.VMEM
SMEM = pltpu.MemorySpace.SMEM
F32 = jnp.float32
BF16 = jnp.bfloat16


def vmem():
    return pl.BlockSpec(memory_space=VMEM)


def smem():
    return pl.BlockSpec(memory_space=SMEM)


def layer_norm(values, gain):
    center = jnp.mean(values, axis=-1, keepdims=True)
    centred = values - center
    spread = jnp.mean(centred * centred, axis=-1, keepdims=True)
    return centred * lax.rsqrt(spread + EPS) * gain


def unit_rows(values):
    scale = lax.rsqrt(jnp.mean(values * values, axis=-1, keepdims=True) + EPS)
    return values * scale * values.shape[-1] ** (-0.5)


def swap(values, axis, bit):
    size = lax.axis_size(axis)
    return lax.ppermute(values, axis, [(i, i ^ bit) for i in range(size)])


def bits_down(size):
    bits = []
    bit = size // 2
    while bit:
        bits.append(bit)
        bit //= 2
    return bits


def gather_blocks(values, axis):
    blocks, order = [values], [0]
    for bit in bits_down(lax.axis_size(axis)):
        blocks = blocks + [swap(block, axis, bit) for block in blocks]
        order = order + [other ^ bit for other in order]
    return blocks, order


def double_stack(values, axis):
    stacked = values[None]
    bit = 1
    while bit < lax.axis_size(axis):
        stacked = jnp.concatenate([stacked, swap(stacked, axis, bit)], axis=0)
        bit *= 2
    return stacked


def pick_kernel(sel_ref, dest_ref, pixels_ref, cap_ref, rows_ref, meta_ref, sems):
    count = jnp.int32(0)
    index = [jnp.int32(0)] * SEND_MOST
    target = [jnp.int32(0)] * SEND_MOST
    for e in range(sel_ref.shape[0]):
        here = sel_ref[e] > 0
        for r in range(SEND_MOST):
            take = here & (count == r)
            index[r] = jnp.where(take, e, index[r])
            target[r] = jnp.where(take, dest_ref[e], target[r])
        count = count + here.astype(jnp.int32)
    copies = []
    for r in range(SEND_MOST):
        copies.append(
            pltpu.make_async_copy(pixels_ref.at[index[r]], rows_ref.at[r], sems.at[r])
        )
        copies[-1].start()
    captions = cap_ref[...].astype(F32)
    width = captions.shape[1]
    example = lax.broadcasted_iota(jnp.int32, captions.shape, 0)
    lane = lax.broadcasted_iota(jnp.int32, (1, META), 1)
    for r in range(SEND_MOST):
        row = jnp.sum(jnp.where(example == index[r], captions, 0.0), axis=0, keepdims=True)
        live = (count > r).astype(F32)
        extra = jnp.where(lane == 0, live, jnp.where(lane == 1, target[r].astype(F32), 0.0))
        meta_ref[r : r + 1, :width] = row.astype(BF16)
        meta_ref[r : r + 1, width:] = extra.astype(BF16)
    for copy in copies:
        copy.wait()


def pick(selection, destination, pixels, captions):
    _, length, depth = pixels.shape
    return pl.pallas_call(
        pick_kernel,
        out_shape=(
            jax.ShapeDtypeStruct((SEND_MOST, length, depth), BF16),
            jax.ShapeDtypeStruct((SEND_MOST, captions.shape[1] + META), BF16),
        ),
        in_specs=[smem(), smem(), pl.BlockSpec(memory_space=pl.ANY), vmem()],
        out_specs=(vmem(), vmem()),
        scratch_shapes=[pltpu.SemaphoreType.DMA((SEND_MOST,))],
        name="pick",
    )(selection, destination, pixels, captions)


def attend_kernel(shards, gains_ref, patch_ref, qkv_ref, *refs):
    pixel_refs = refs[:shards]
    position_refs = refs[shards : 2 * shards]
    hidden_ref, context_ref = refs[2 * shards :]
    pixels = jnp.concatenate([ref[...] for ref in pixel_refs], axis=0)
    position = jnp.concatenate([ref[...] for ref in position_refs], axis=0)
    hidden = jnp.dot(pixels, patch_ref[...], preferred_element_type=F32)
    hidden = hidden + position.astype(F32)
    hidden_ref[...] = hidden
    normed = layer_norm(hidden, gains_ref[0:1, :]).astype(BF16)
    query, key, value = [
        jnp.dot(normed, qkv_ref[t], preferred_element_type=F32).astype(BF16) for t in range(3)
    ]
    query = query * jnp.asarray(HEAD_DIM ** (-0.5), BF16)
    parts = []
    for h in range(query.shape[1] // HEAD_DIM):
        cols = slice(h * HEAD_DIM, (h + 1) * HEAD_DIM)
        scores = lax.dot_general(
            query[:, cols], key[:, cols], (((1,), (1,)), ((), ())), preferred_element_type=F32
        )
        weights = jnp.exp(scores - jnp.max(scores, axis=-1, keepdims=True))
        weights = weights * (1.0 / jnp.sum(weights, axis=-1, keepdims=True))
        parts.append(jnp.dot(weights.astype(BF16), value[:, cols], preferred_element_type=F32))
    context_ref[...] = jnp.concatenate(parts, axis=1).astype(BF16)


def attend(pixels, positions, gains, patch_weight, qkv):
    shards = len(pixels)
    length = shards * pixels[0].shape[0]
    width = patch_weight.shape[1]
    return pl.pallas_call(
        functools.partial(attend_kernel, shards),
        out_shape=(
            jax.ShapeDtypeStruct((length, width), F32),
            jax.ShapeDtypeStruct((length, qkv.shape[2]), BF16),
        ),
        in_specs=[vmem()] * (3 + 2 * shards),
        out_specs=(vmem(), vmem()),
        name="attend",
    )(gains, patch_weight, qkv, *pixels, *positions)


def expand_kernel(order, gains_ref, up_ref, hidden_ref, *refs):
    shards = len(order)
    context_refs = refs[:shards]
    output_refs = refs[shards : 2 * shards]
    sums_ref = refs[2 * shards]
    block = hidden_ref.shape[0] // shards
    hidden = hidden_ref[...]
    for j, ref in enumerate(context_refs):
        places = [order.index(order[p] ^ order[j]) for p in range(shards)]
        context = jnp.concatenate([ref[q * block : (q + 1) * block, :] for q in places], axis=0)
        hidden = hidden + jnp.dot(context, output_refs[j][...], preferred_element_type=F32)
    normed = layer_norm(hidden, gains_ref[1:2, :]).astype(BF16)
    expanded = jax.nn.gelu(jnp.dot(normed, up_ref[...], preferred_element_type=F32)).astype(BF16)
    sums_ref[0:1, :] = jnp.sum(hidden, axis=0, keepdims=True)
    sums_ref[1:2, :] = jnp.sum(expanded.astype(F32), axis=0, keepdims=True)


def expand(contexts, order, outputs, hidden, gains, up_weight):
    width = hidden.shape[1]
    return pl.pallas_call(
        functools.partial(expand_kernel, tuple(order)),
        out_shape=jax.ShapeDtypeStruct((2, width), F32),
        in_specs=[vmem()] * (3 + 2 * len(order)),
        out_specs=vmem(),
        name="expand",
    )(gains, up_weight, hidden, *contexts, *outputs)


def reduce_kernel(scale, own_ref, down_ref, *refs):
    out_ref = refs[-1]
    sums = refs[:-1]
    units = jnp.concatenate([ref[1:2, :] for ref in sums], axis=0) * scale
    residual = jnp.concatenate([ref[0:1, :] for ref in sums], axis=0) * scale
    high = units.astype(BF16)
    low = (units - high.astype(F32)).astype(BF16)
    both = jnp.concatenate([high, low], axis=0)
    product = jnp.dot(both, down_ref[...], preferred_element_type=F32)
    count = len(sums)
    own = own_ref[0].astype(F32)
    out_ref[...] = product[:count] + product[count:] + residual * own


def reduce_units(sums, own, down_weight, patches):
    return pl.pallas_call(
        functools.partial(reduce_kernel, 1.0 / patches),
        out_shape=jax.ShapeDtypeStruct((len(sums), down_weight.shape[1]), F32),
        in_specs=[smem()] + [vmem()] * (1 + len(sums)),
        out_specs=vmem(),
        name="reduce",
    )(own, down_weight, *sums)


def finish_kernel(total, params_ref, gains_ref, weight_ref, cap_ref, meta_ref, pooled_ref, out_ref, loss_ref):
    count = meta_ref.shape[0]
    rows = [
        pooled_ref[c // SEND_MOST, c % SEND_MOST : c % SEND_MOST + 1, :] for c in range(count)
    ]
    meta = meta_ref[...]
    live = meta[:, 0:1]
    slots = []
    for k in range(RECV_MOST):
        acc = None
        for c in range(count):
            term = jnp.where(meta[c : c + 1, k + 1 : k + 2] > 0.0, rows[c], 0.0)
            acc = term if acc is None else acc + term
        slots.append(acc)
    pooled = jnp.concatenate(slots, axis=0)
    filled = jnp.max(meta[:, 1 : RECV_MOST + 1], axis=0, keepdims=True)
    normed = layer_norm(pooled, gains_ref[2:3, :]).astype(BF16)
    embedded = jnp.dot(normed, weight_ref[...], preferred_element_type=F32)
    captions = cap_ref[...]
    scale = 10.0 * jnp.exp(jnp.full((1, 1), params_ref[0], F32))
    shift = 2.0 * params_ref[1]
    for k in range(RECV_MOST):
        used = filled[:, k : k + 1] > 0.0
        row = jnp.where(used, embedded[k : k + 1, :], 0.0)
        out_ref[k : k + 1, :] = row
        logits = scale * jnp.sum(captions * unit_rows(row), axis=1, keepdims=True) + shift
        signs = jnp.where(meta[:, k + 1 : k + 2] > 0.0, 1.0, -1.0)
        value = -signs * logits
        terms = jnp.maximum(value, 0.0) + jnp.log1p(jnp.exp(-jnp.abs(value)))
        lost = jnp.sum(terms * live) / total
        loss_ref[k] = jnp.where(jnp.max(jnp.where(used, 1.0, 0.0)) > 0.0, lost, 0.0)


def finish(pooled, captions, meta, params, gains, weight, total):
    return pl.pallas_call(
        functools.partial(finish_kernel, total),
        out_shape=(
            jax.ShapeDtypeStruct((RECV_MOST, weight.shape[1]), F32),
            jax.ShapeDtypeStruct((RECV_MOST,), F32),
        ),
        in_specs=[smem()] + [vmem()] * 5,
        out_specs=(vmem(), smem()),
        name="finish",
    )(params, gains, weight, captions, meta, pooled)


def per_device(
    pixels,
    selection,
    destination,
    patch_weight,
    position,
    query_key_value,
    output_weight,
    up_weight,
    down_weight,
    norm_gains,
    embedding_weight,
    caption_vectors,
    loss_params,
):
    devices_dp = lax.axis_size("dp")
    rows, caption_meta = pick(selection, destination, pixels, caption_vectors)
    positions, order = gather_blocks(position, "mp")
    pixel_blocks = [gather_blocks(rows[r], "mp")[0] for r in range(SEND_MOST)]
    outputs, _ = gather_blocks(output_weight, "mp")

    me = lax.axis_index("dp")
    width = caption_vectors.shape[1]
    gathered = double_stack(caption_meta, "dp").reshape(devices_dp * SEND_MOST, width + META)
    captions = unit_rows(gathered[:, :width].astype(F32))
    live = gathered[:, width] > 0
    target = gathered[:, width + 1].astype(jnp.int32)
    spot = (me ^ jnp.arange(devices_dp, dtype=jnp.int32))[:, None] * SEND_MOST
    spot = (spot + jnp.arange(SEND_MOST, dtype=jnp.int32)).reshape(-1)
    mine = live & (target == me)
    ahead = mine[None, :] & (spot[None, :] < spot[:, None])
    place = jnp.sum(ahead.astype(jnp.int32), axis=1)
    slot = mine[:, None] & (place[:, None] == jnp.arange(RECV_MOST, dtype=jnp.int32))
    meta = jnp.concatenate([live[:, None], slot], axis=1).astype(F32)

    sums = []
    for r in range(SEND_MOST):
        hidden, context = attend(pixel_blocks[r], positions, norm_gains, patch_weight, query_key_value)
        contexts, _ = gather_blocks(context, "mp")
        sums.append(expand(contexts, order, outputs, hidden, norm_gains, up_weight))
    own = (lax.axis_index("mp") == 0).astype(jnp.int32).reshape(1)
    patches = position.shape[0] * len(order)
    pooled = reduce_units(sums, own, down_weight, patches)
    for bit in reversed(bits_down(lax.axis_size("mp"))):
        pooled = pooled + swap(pooled, "mp", bit)
    pooled = double_stack(pooled, "dp")
    return finish(
        pooled, captions, meta, loss_params, norm_gains, embedding_weight, float(devices_dp * SEL_DEV)
    )


def solution(mesh):
    in_specs = (
        P("dp", "mp", None),
        P("dp"),
        P("dp"),
        P(),
        P("mp", None),
        P(None, None, "mp"),
        P("mp", None),
        P(None, "mp"),
        P("mp", None),
        P(),
        P(),
        P("dp", None),
        P(),
    )
    out_specs = (P("dp", None), P("dp"))
    return jax.shard_map(
        per_device, mesh=mesh, in_specs=in_specs, out_specs=out_specs, check_vma=False
    )
```

time: 235 us -> 108 us (0.46)
  waiting for transfers between devices: 110 us -> 35.2 us
  blocking collectives: 52.1 us -> 0 us
  Pallas kernels: 0 us -> 39.8 us
  matrix products: 23.6 us -> 0 us
  between operations: 16.1 us -> 1.17 us
  starting transfers between devices: 11 us -> 22.7 us
  other arithmetic: 13.9 us -> 4.97 us
  local copies, waits for them, and re-layouts: 7.55 us -> 3.47 us
    reduce_scatter x2 -> x0, waiting for transfers between devices: 44.6 us -> none  [the longest x1 44.6 us: encode(): lax.psum_scatter(jnp.einsum('rpk,kd->prd', segment, output_weight, prefer...]
    all_gather x2 -> x0, waiting for transfers between devices: 44.3 us -> none  [encode(): lax.all_gather(normed, 'mp', axis=0, tiled=True)]
    pallas_call x0 -> x9, Pallas kernels: none -> 39.8 us  [the longest x3 15.6 us: expand(): pl.pallas_call(functools.partial(expand_kernel, tuple(order)), out_shape=...]
    ppermute x0 -> x32, waiting for transfers between devices: none -> 35.2 us  [swap(): return lax.ppermute(values, axis, [(i, i ^ bit) for i in range(size)])]
    all_gather x1 -> x0, blocking collectives: 30.5 us -> none  [per_device(): lax.all_gather(caption_rows, 'dp', axis=0, tiled=True)]
    dot_general x10 -> x0, matrix products: 23.6 us -> none  [the longest x1 8.73 us: encode(): jnp.einsum('prf,fd->prd', segment, down_weight, preferred_element_type=jn...]
    ppermute x0 -> x32, starting transfers between devices: none -> 22.7 us  [swap(): return lax.ppermute(values, axis, [(i, i ^ bit) for i in range(size)])]
    all_to_all x2 -> x0, waiting for transfers between devices: 20.7 us -> none  [the longest x1 17.7 us: per_device(): lax.all_to_all(outgoing, 'dp', split_axis=0, concat_axis=0, tiled=True)]
  transfers between devices with their start and end apart: 6 -> 32, of which waited for: 5 -> 9; matrix products, arithmetic and copies ran while one was open for 4% -> 4% of each run, Pallas kernels for 0% -> 24%
where the time goes in v1:
time: 108 us; the launch traced here: 107 us
  Pallas kernels  39.8 us (37%)
  waiting for transfers between devices  35.2 us (33%)
  starting transfers between devices  22.7 us (21%)
  other arithmetic  4.97 us (5%)
  local copies, waits for them, and re-layouts  3.47 us (3%)
  between operations  1.17 us (1%)
    ppermute x32, waiting for transfers between devices, swap(): return lax.ppermute(values, axis, [(i, i ^ bit) for i in range(size)])  35.2 us
    ppermute x32, starting transfers between devices, swap(): return lax.ppermute(values, axis, [(i, i ^ bit) for i in range(size)])  22.7 us
    pallas_call x3, Pallas kernels, expand(): pl.pallas_call(functools.partial(expand_kernel, tuple(order)), out_shape=...  15.6 us
    pallas_call x3, Pallas kernels, attend(): pl.pallas_call(functools.partial(attend_kernel, shards), out_shape=(jax.S...  15.5 us
    pallas_call x1, Pallas kernels, finish(): pl.pallas_call(functools.partial(finish_kernel, total), out_shape=(jax.Sh...  3.44 us
    pallas_call x1, Pallas kernels, pick(): pl.pallas_call(pick_kernel, out_shape=(jax.ShapeDtypeStruct((SEND_MOST, l...  2.66 us
    pallas_call x1, Pallas kernels, reduce_units(): pl.pallas_call(functools.partial(reduce_kernel, 1.0 / patches), out_shape...  2.61 us
    unnamed x62, local copies, waits for them, and re-layouts  2.34 us
  transfers between devices with their start and end apart: 32, of which 9 were waited for; matrix products, arithmetic and copies ran while one was open for 4% of the time, Pallas kernels for 24%

profile of v1, /device:TPU:0, one launch (start us, length us, event | category | flops | bytes accessed | tf_op | source)
XLA Modules:
  0.0 107.4 jit_solution(5480076308381883864)
XLA Ops:
  0.7 2.7 %pick.1 = (bf16[3,64,768]{2,1,0:T(8,128)(2,1)}, bf16[3,1152]{1,0:T(4,128)(2,1)}) custom-call(s32[16]{0:T(128)} %sel_ref.1, s32[16]{0:T(128)} %dest_ref.1, bf16[16,64,768]{2,1,0:T(8,128)(2,1)} %pixels_ref.1, bf16[16,1024]{1,0:T(8,128)(2,1)} %cap_ref.1), custom_call_target="tpu_custom_call" | custom-call | tf_op jit(solution)/shard_map/pick/pallas_call | solution.py:107
  3.3 3.1 %collective-permute-start = (bf16[1,3,1152]{2,1,0:T(4,128)(2,1)}, bf16[1,3,1152]{2,1,0:T(4,128)(2,1)S(1)}, u32[]{:S(2)}, u32[]{:S(2)}) collective-permute-start(bf16[1,3,1152]{2,1,0:T(4,128)(2,1)} %bitcast.10), channel_id=1, source_target_pairs={{0,4},{4,0},{8,12},{12,8},{16,20},{20,16},{24,28},{28,24},{1,5},{5... | collective-permute-start | bytes 20744 | tf_op jit(solution)/shard_map/ppermute | solution.py:45
  6.4 1.0 slice_bitcast_fusion
  7.4 1.6 %collective-permute-start.21 = (bf16[64,768]{1,0:T(8,128)(2,1)S(1)}, bf16[64,768]{1,0:T(8,128)(2,1)S(1)}, u32[]{:S(2)}, u32[]{:S(2)}) collective-permute-start(bf16[64,768]{1,0:T(8,128)(2,1)S(1)} %get-tuple-element.20.refs_0_), channel_id=1, source_target_pairs={{0,2},{1,3},{2,0},{3,1},{4,6},{5,7},{6,4},{7,5},{8,10},{9,11},{10,... | collective-permute-start | bytes 294920 | tf_op jit(solution)/shard_map/ppermute | solution.py:45
  9.0 0.5 collective-permute-start.6
  9.5 1.5 %collective-permute-start.15 = (bf16[64,768]{1,0:T(8,128)(2,1)S(1)}, bf16[64,768]{1,0:T(8,128)(2,1)S(1)}, u32[]{:S(2)}, u32[]{:S(2)}) collective-permute-start(bf16[64,768]{1,0:T(8,128)(2,1)S(1)} %get-tuple-element.21.refs_0_), channel_id=1, source_target_pairs={{0,2},{1,3},{2,0},{3,1},{4,6},{5,7},{6,4},{7,5},{8,10},{9,11},{10,... | collective-permute-start | bytes 294920 | tf_op jit(solution)/shard_map/ppermute | solution.py:45
  11.0 0.7 pad_maximum_fusion.5
  11.7 1.6 %collective-permute-start.1 = (bf16[2,3,1152]{2,1,0:T(4,128)(2,1)S(1)}, bf16[2,3,1152]{2,1,0:T(4,128)(2,1)S(1)}, u32[]{:S(2)}, u32[]{:S(2)}) collective-permute-start(bf16[2,3,1152]{2,1,0:T(4,128)(2,1)S(1)} %pad_maximum_fusion.5), channel_id=1, source_target_pairs={{0,8},{4,12},{8,0},{12,4},{16,24},{20,28},{24,16},{28,20},{1,9},{5... | collective-permute-start | bytes 41480 | tf_op jit(solution)/shard_map/ppermute | solution.py:45
  13.4 2.2 %collective-permute-done.1 = bf16[2,3,1152]{2,1,0:T(4,128)(2,1)S(1)} collective-permute-done((bf16[2,3,1152]{2,1,0:T(4,128)(2,1)S(1)}, bf16[2,3,1152]{2,1,0:T(4,128)(2,1)S(1)}, u32[]{:S(2)}, u32[]{:S(2)}) %collective-permute-start.1) | collective-permute-done | bytes 13856 | tf_op jit(solution)/shard_map/ppermute | solution.py:45
  15.6 0.5 collective-permute-start.8
  16.1 1.4 %collective-permute-start.12 = (bf16[256,1024]{1,0:T(8,128)(2,1)S(1)}, bf16[256,1024]{1,0:T(8,128)(2,1)S(1)}, u32[]{:S(2)}, u32[]{:S(2)}) collective-permute-start(bf16[256,1024]{1,0:T(8,128)(2,1)S(1)} %copy-done), channel_id=1, source_target_pairs={{0,2},{1,3},{2,0},{3,1},{4,6},{5,7},{6,4},{7,5},{8,10},{9,11},{10,... | collective-permute-start | bytes 1572872 | tf_op jit(solution)/shard_map/ppermute | solution.py:45
  17.5 0.7 collective-permute-start.3
  18.2 13.9 %collective-permute-done.3.refs_1_ = bf16[64,768]{1,0:T(8,128)(2,1)S(1)} collective-permute-done((bf16[64,768]{1,0:T(8,128)(2,1)S(1)}, bf16[64,768]{1,0:T(8,128)(2,1)S(1)}, u32[]{:S(2)}, u32[]{:S(2)}) %collective-permute-start.3) | collective-permute-done | bytes 98336 | tf_op jit(solution)/shard_map/ppermute | solution.py:45
  32.2 0.5 collective-permute-start.4
  32.8 0.4 collective-permute-start.5
  33.2 0.7 pad_maximum_fusion.3
  34.0 5.2 %attend.5 = (f32[256,1024]{1,0:T(8,128)}, bf16[256,256]{1,0:T(8,128)(2,1)}) custom-call(f32[3,1024]{1,0:T(4,128)} %gains_ref.13, bf16[768,1024]{1,0:T(8,128)(2,1)} %patch_ref.5, bf16[3,1024,256]{2,1,0:T(8,128)(2,1)} %qkv_ref.5, bf16[64,768]{1,0:T(8,128)(2,1)} %copy-done.10, bf16[64,768]{1,0:T(8,128)(2,1)} %copy-done.23, bf16[64,768]{1,0:T(8,128)(2,1)} %copy-done.24, ...), custom_call_target="tpu_custom_call" | custom-call | tf_op jit(solution)/shard_map/attend/pallas_call | solution.py:150
  39.3 2.6 %collective-permute-start.2 = (bf16[4,3,1152]{2,1,0:T(4,128)(2,1)S(1)}, bf16[4,3,1152]{2,1,0:T(4,128)(2,1)S(1)}, u32[]{:S(2)}, u32[]{:S(2)}) collective-permute-start(bf16[4,3,1152]{2,1,0:T(4,128)(2,1)S(1)} %pad_maximum_fusion.3), channel_id=1, source_target_pairs={{0,16},{4,20},{8,24},{12,28},{16,0},{20,4},{24,8},{28,12},{1,17},{... | collective-permute-start | bytes 82952 | tf_op jit(solution)/shard_map/ppermute | solution.py:45
  41.9 1.7 %collective-permute-start.24 = (bf16[256,256]{1,0:T(8,128)(2,1)}, bf16[256,256]{1,0:T(8,128)(2,1)S(1)}, u32[]{:S(2)}, u32[]{:S(2)}) collective-permute-start(bf16[256,256]{1,0:T(8,128)(2,1)} %get-tuple-element.17.refs_0_), channel_id=1, source_target_pairs={{0,2},{1,3},{2,0},{3,1},{4,6},{5,7},{6,4},{7,5},{8,10},{9,11},{10,... | collective-permute-start | bytes 393224 | tf_op jit(solution)/shard_map/ppermute | solution.py:45
  43.9 5.1 %attend.4 = (f32[256,1024]{1,0:T(8,128)}, bf16[256,256]{1,0:T(8,128)(2,1)}) custom-call(f32[3,1024]{1,0:T(4,128)} %gains_ref.13, bf16[768,1024]{1,0:T(8,128)(2,1)} %patch_ref.5, bf16[3,1024,256]{2,1,0:T(8,128)(2,1)} %qkv_ref.5, bf16[64,768]{1,0:T(8,128)(2,1)} %copy-done.9, bf16[64,768]{1,0:T(8,128)(2,1)} %copy-done.21, bf16[64,768]{1,0:T(8,128)(2,1)} %copy-done.26, ...), custom_call_target="tpu_custom_call" | custom-call | tf_op jit(solution)/shard_map/attend/pallas_call | solution.py:150
  49.0 5.2 %attend.3 = (f32[256,1024]{1,0:T(8,128)}, bf16[256,256]{1,0:T(8,128)(2,1)}) custom-call(f32[3,1024]{1,0:T(4,128)} %gains_ref.13, bf16[768,1024]{1,0:T(8,128)(2,1)} %patch_ref.5, bf16[3,1024,256]{2,1,0:T(8,128)(2,1)} %qkv_ref.5, bf16[64,768]{1,0:T(8,128)(2,1)} %copy-done.8, bf16[64,768]{1,0:T(8,128)(2,1)} %copy-done.22, bf16[64,768]{1,0:T(8,128)(2,1)} %copy-done.25, ...), custom_call_target="tpu_custom_call" | custom-call | tf_op jit(solution)/shard_map/attend/pallas_call | solution.py:150
  54.2 0.5 collective-permute-start.18
  54.8 1.6 %collective-permute-start.9 = (bf16[256,256]{1,0:T(8,128)(2,1)}, bf16[256,256]{1,0:T(8,128)(2,1)S(1)}, u32[]{:S(2)}, u32[]{:S(2)}) collective-permute-start(bf16[256,256]{1,0:T(8,128)(2,1)} %get-tuple-element.13.refs_0_), channel_id=1, source_target_pairs={{0,2},{1,3},{2,0},{3,1},{4,6},{5,7},{6,4},{7,5},{8,10},{9,11},{10,... | collective-permute-start | bytes 393224 | tf_op jit(solution)/shard_map/ppermute | solution.py:45
  56.4 0.5 collective-permute-start.14
  57.1 3.6 %collective-permute-done.18.refs_1_ = bf16[256,256]{1,0:T(8,128)(2,1)S(1)} collective-permute-done((bf16[256,256]{1,0:T(8,128)(2,1)S(1)}, bf16[256,256]{1,0:T(8,128)(2,1)S(1)}, u32[]{:S(2)}, u32[]{:S(2)}) %collective-permute-start.18) | collective-permute-done | bytes 131104 | tf_op jit(solution)/shard_map/ppermute | solution.py:45
  60.7 2.3 %collective-permute-done.9.refs_1_ = bf16[256,256]{1,0:T(8,128)(2,1)S(1)} collective-permute-done((bf16[256,256]{1,0:T(8,128)(2,1)}, bf16[256,256]{1,0:T(8,128)(2,1)S(1)}, u32[]{:S(2)}, u32[]{:S(2)}) %collective-permute-start.9) | collective-permute-done | bytes 131104 | tf_op jit(solution)/shard_map/ppermute | solution.py:45
  63.0 0.5 collective-permute-start.20
  63.7 0.6 copy-done.2
  64.6 5.2 %expand.5.refs_2_ = f32[2,1024]{1,0:T(2,128)} custom-call(f32[3,1024]{1,0:T(4,128)} %gains_ref.13, bf16[1024,1024]{1,0:T(8,128)(2,1)} %up_ref.5, f32[256,1024]{1,0:T(8,128)} %get-tuple-element.16.hidden_ref, bf16[256,256]{1,0:T(8,128)(2,1)} %get-tuple-element.17.refs_0_, bf16[256,256]{1,0:T(8,128)(2,1)} %copy-done.11, bf16[256,256]{1,0:T(8,128)(2,1)} %copy-done.12, ...), custom_call_target="tpu_custom_call" | custom-call | tf_op jit(solution)/shard_map/expand/pallas_call | solution.py:181
  69.8 0.6 copy-done.18
  70.4 5.2 %expand.4.refs_1_ = f32[2,1024]{1,0:T(2,128)} custom-call(f32[3,1024]{1,0:T(4,128)} %gains_ref.13, bf16[1024,1024]{1,0:T(8,128)(2,1)} %up_ref.5, f32[256,1024]{1,0:T(8,128)} %get-tuple-element.14.hidden_ref, bf16[256,256]{1,0:T(8,128)(2,1)} %get-tuple-element.15.refs_0_, bf16[256,256]{1,0:T(8,128)(2,1)} %copy-done.15, bf16[256,256]{1,0:T(8,128)(2,1)} %copy-done.18, ...), custom_call_target="tpu_custom_call" | custom-call | tf_op jit(solution)/shard_map/expand/pallas_call | solution.py:181
  75.6 0.6 copy-done.17
  76.3 5.3 %expand.3.refs_0_ = f32[2,1024]{1,0:T(2,128)} custom-call(f32[3,1024]{1,0:T(4,128)} %gains_ref.13, bf16[1024,1024]{1,0:T(8,128)(2,1)} %up_ref.5, f32[256,1024]{1,0:T(8,128)} %get-tuple-element.12.hidden_ref, bf16[256,256]{1,0:T(8,128)(2,1)} %get-tuple-element.13.refs_0_, bf16[256,256]{1,0:T(8,128)(2,1)} %copy-done.14, bf16[256,256]{1,0:T(8,128)(2,1)} %copy-done.17, ...), custom_call_target="tpu_custom_call" | custom-call | tf_op jit(solution)/shard_map/expand/pallas_call | solution.py:181
  81.6 2.6 %reduce.3 = f32[3,1024]{1,0:T(4,128)} custom-call(s32[1]{0:T(128)} %bitcast.1.own_ref, bf16[1024,1024]{1,0:T(8,128)(2,1)} %down_ref.1, f32[2,1024]{1,0:T(2,128)} %expand.3.refs_0_, f32[2,1024]{1,0:T(2,128)} %expand.4.refs_1_, f32[2,1024]{1,0:T(2,128)} %expand.5.refs_2_), custom_call_target="tpu_custom_call" | custom-call | tf_op jit(solution)/shard_map/reduce/pallas_call | solution.py:205
  84.2 0.3 collective-permute-start.27
  84.5 0.7 fusion.1.cap_ref
  85.3 0.4 collective-permute-done.27
  85.6 0.7 add.43
  86.8 3.3 %collective-permute-done.28 = f32[3,1024]{1,0:T(4,128)S(1)} collective-permute-done((f32[3,1024]{1,0:T(4,128)S(1)}, f32[3,1024]{1,0:T(4,128)S(1)}, u32[]{:S(2)}, u32[]{:S(2)}) %collective-permute-start.28) | collective-permute-done | bytes 12320 | tf_op jit(solution)/shard_map/ppermute | solution.py:45
  90.1 0.5 collective-permute-start.29
  90.8 3.1 %collective-permute-done.29 = f32[1,3,1024]{2,1,0:T(4,128)S(1)} collective-permute-done((f32[1,3,1024]{2,1,0:T(4,128)S(1)}, f32[1,3,1024]{2,1,0:T(4,128)S(1)}, u32[]{:S(2)}, u32[]{:S(2)}) %collective-permute-start.29) | collective-permute-done | bytes 12320 | tf_op jit(solution)/shard_map/ppermute | solution.py:45
  93.8 1.6 %collective-permute-start.30 = (f32[2,3,1024]{2,1,0:T(4,128)S(1)}, f32[2,3,1024]{2,1,0:T(4,128)S(1)}, u32[]{:S(2)}, u32[]{:S(2)}) collective-permute-start(f32[2,3,1024]{2,1,0:T(4,128)S(1)} %pad_maximum_fusion.4), channel_id=1, source_target_pairs={{0,8},{4,12},{8,0},{12,4},{16,24},{20,28},{24,16},{28,20},{1,9},{5... | collective-permute-start | bytes 73736 | tf_op jit(solution)/shard_map/ppermute | solution.py:45
  95.6 2.3 %collective-permute-done.30 = f32[2,3,1024]{2,1,0:T(4,128)S(1)} collective-permute-done((f32[2,3,1024]{2,1,0:T(4,128)S(1)}, f32[2,3,1024]{2,1,0:T(4,128)S(1)}, u32[]{:S(2)}, u32[]{:S(2)}) %collective-permute-start.30) | collective-permute-done | bytes 24608 | tf_op jit(solution)/shard_map/ppermute | solution.py:45
  97.9 0.4 collective-permute-start.31
  98.3 0.7 add_convert_fusion.meta_ref
  98.9 4.2 %collective-permute-done.31 = f32[4,3,1024]{2,1,0:T(4,128)S(1)} collective-permute-done((f32[4,3,1024]{2,1,0:T(4,128)S(1)}, f32[4,3,1024]{2,1,0:T(4,128)S(1)}, u32[]{:S(2)}, u32[]{:S(2)}) %collective-permute-start.31) | collective-permute-done | bytes 49184 | tf_op jit(solution)/shard_map/ppermute | solution.py:45
  103.1 0.7 pad_maximum_fusion.pooled_ref
  103.8 3.4 %finish.1 = (f32[4,1024]{1,0:T(4,128)}, f32[4]{0:T(128)}) custom-call(f32[2]{0:T(128)} %params_ref.1, f32[3,1024]{1,0:T(4,128)} %gains_ref.13, bf16[1024,1024]{1,0:T(8,128)(2,1)} %weight_ref.1, f32[24,1024]{1,0:T(8,128)} %fusion.1.cap_ref, f32[24,5]{1,0:T(8,128)} %add_convert_fusion.meta_ref, f32[8,3,1024]{2,1,0:T(4,128)} %pad_maximum_fusion.pooled_ref), custom_call_target="tpu_custom_call" | custom-call | tf_op jit(solution)/shard_map/finish/pallas_call | solution.py:248
  (107 shorter events, 2.0 us)
Async XLA Ops:
  0.6 8.4 %copy-start.4 = (bf16[64,1024]{1,0:T(8,128)(2,1)S(1)}, bf16[64,1024]{1,0:T(8,128)(2,1)}, u32[]{:S(2)}) copy-start(bf16[64,1024]{1,0:T(8,128)(2,1)} %refs_4_.10) | copy-start | bytes 393220
  0.6 15.4 %copy-start = (bf16[256,1024]{1,0:T(8,128)(2,1)S(1)}, bf16[256,1024]{1,0:T(8,128)(2,1)}, u32[]{:S(2)}) copy-start(bf16[256,1024]{1,0:T(8,128)(2,1)} %refs_4_.11) | copy-start | bytes 1572868
  3.3 7.7 %collective-permute-start = (bf16[1,3,1152]{2,1,0:T(4,128)(2,1)}, bf16[1,3,1152]{2,1,0:T(4,128)(2,1)S(1)}, u32[]{:S(2)}, u32[]{:S(2)}) collective-permute-start(bf16[1,3,1152]{2,1,0:T(4,128)(2,1)} %bitcast.10), channel_id=1, source_target_pairs={{0,4},{4,0},{8,12},{12,8},{16,20},{20,16},{24,28},{28,24},{1,5},{5... | collective-permute-start | bytes 20744 | tf_op jit(solution)/shard_map/ppermute | solution.py:45
  7.4 26.5 %copy-start.10 = (bf16[64,768]{1,0:T(8,128)(2,1)}, bf16[64,768]{1,0:T(8,128)(2,1)S(1)}, u32[]{:S(2)}) copy-start(bf16[64,768]{1,0:T(8,128)(2,1)S(1)} %get-tuple-element.20.refs_0_) | copy-start | bytes 294916
  7.4 31.8 %copy-start.8 = (bf16[64,768]{1,0:T(8,128)(2,1)}, bf16[64,768]{1,0:T(8,128)(2,1)S(1)}, u32[]{:S(2)}) copy-start(bf16[64,768]{1,0:T(8,128)(2,1)S(1)} %get-tuple-element.22.refs_0_) | copy-start | bytes 294916
  7.4 36.4 %copy-start.9 = (bf16[64,768]{1,0:T(8,128)(2,1)}, bf16[64,768]{1,0:T(8,128)(2,1)S(1)}, u32[]{:S(2)}) copy-start(bf16[64,768]{1,0:T(8,128)(2,1)S(1)} %get-tuple-element.21.refs_0_) | copy-start | bytes 294916
  7.4 8.7 %collective-permute-start.21 = (bf16[64,768]{1,0:T(8,128)(2,1)S(1)}, bf16[64,768]{1,0:T(8,128)(2,1)S(1)}, u32[]{:S(2)}, u32[]{:S(2)}) collective-permute-start(bf16[64,768]{1,0:T(8,128)(2,1)S(1)} %get-tuple-element.20.refs_0_), channel_id=1, source_target_pairs={{0,2},{1,3},{2,0},{3,1},{4,6},{5,7},{6,4},{7,5},{8,10},{9,11},{10,... | collective-permute-start | bytes 294920 | tf_op jit(solution)/shard_map/ppermute | solution.py:45
  9.0 8.5 %collective-permute-start.22 = (bf16[64,768]{1,0:T(8,128)(2,1)S(1)}, bf16[64,768]{1,0:T(8,128)(2,1)S(1)}, u32[]{:S(2)}, u32[]{:S(2)}) collective-permute-start(bf16[64,768]{1,0:T(8,128)(2,1)S(1)} %get-tuple-element.20.refs_0_), channel_id=1, source_target_pairs={{0,1},{1,0},{2,3},{3,2},{4,5},{5,4},{6,7},{7,6},{8,9},{9,8},{10,11... | collective-permute-start | bytes 294920 | tf_op jit(solution)/shard_map/ppermute | solution.py:45
  9.0 6.6 %collective-permute-start.6 = (bf16[64,1024]{1,0:T(8,128)(2,1)S(1)}, bf16[64,1024]{1,0:T(8,128)(2,1)S(1)}, u32[]{:S(2)}, u32[]{:S(2)}) collective-permute-start(bf16[64,1024]{1,0:T(8,128)(2,1)S(1)} %copy-done.4), channel_id=1, source_target_pairs={{0,2},{1,3},{2,0},{3,1},{4,6},{5,7},{6,4},{7,5},{8,10},{9,11},{10,... | collective-permute-start | bytes 393224 | tf_op jit(solution)/shard_map/ppermute | solution.py:45
  9.5 8.7 %collective-permute-start.15 = (bf16[64,768]{1,0:T(8,128)(2,1)S(1)}, bf16[64,768]{1,0:T(8,128)(2,1)S(1)}, u32[]{:S(2)}, u32[]{:S(2)}) collective-permute-start(bf16[64,768]{1,0:T(8,128)(2,1)S(1)} %get-tuple-element.21.refs_0_), channel_id=1, source_target_pairs={{0,2},{1,3},{2,0},{3,1},{4,6},{5,7},{6,4},{7,5},{8,10},{9,11},{10,... | collective-permute-start | bytes 294920 | tf_op jit(solution)/shard_map/ppermute | solution.py:45
  11.7 3.8 %collective-permute-start.1 = (bf16[2,3,1152]{2,1,0:T(4,128)(2,1)S(1)}, bf16[2,3,1152]{2,1,0:T(4,128)(2,1)S(1)}, u32[]{:S(2)}, u32[]{:S(2)}) collective-permute-start(bf16[2,3,1152]{2,1,0:T(4,128)(2,1)S(1)} %pad_maximum_fusion.5), channel_id=1, source_target_pairs={{0,8},{4,12},{8,0},{12,4},{16,24},{20,28},{24,16},{28,20},{1,9},{5... | collective-permute-start | bytes 41480 | tf_op jit(solution)/shard_map/ppermute | solution.py:45
  15.6 16.6 %collective-permute-start.7 = (bf16[64,1024]{1,0:T(8,128)(2,1)S(1)}, bf16[64,1024]{1,0:T(8,128)(2,1)S(1)}, u32[]{:S(2)}, u32[]{:S(2)}) collective-permute-start(bf16[64,1024]{1,0:T(8,128)(2,1)S(1)} %copy-done.4), channel_id=1, source_target_pairs={{0,1},{1,0},{2,3},{3,2},{4,5},{5,4},{6,7},{7,6},{8,9},{9,8},{10,11... | collective-permute-start | bytes 393224 | tf_op jit(solution)/shard_map/ppermute | solution.py:45
  15.6 18.4 %copy-start.5 = (bf16[64,1024]{1,0:T(8,128)(2,1)}, bf16[64,1024]{1,0:T(8,128)(2,1)S(1)}, u32[]{:S(2)}) copy-start(bf16[64,1024]{1,0:T(8,128)(2,1)S(1)} %collective-permute-done.6.refs_5_) | copy-start | bytes 393220
  15.6 17.2 %collective-permute-start.8 = (bf16[64,1024]{1,0:T(8,128)(2,1)S(1)}, bf16[64,1024]{1,0:T(8,128)(2,1)S(1)}, u32[]{:S(2)}, u32[]{:S(2)}) collective-permute-start(bf16[64,1024]{1,0:T(8,128)(2,1)S(1)} %collective-permute-done.6.refs_5_), channel_id=1, source_target_pairs={{0,1},{1,0},{2,3},{3,2},{4,5},{5,4},{6,7},{7,6},{8,9},{9,8},{10,11... | collective-permute-start | bytes 393224 | tf_op jit(solution)/shard_map/ppermute | solution.py:45
  16.1 17.9 %copy-start.23 = (bf16[64,768]{1,0:T(8,128)(2,1)}, bf16[64,768]{1,0:T(8,128)(2,1)S(1)}, u32[]{:S(2)}) copy-start(bf16[64,768]{1,0:T(8,128)(2,1)S(1)} %collective-permute-done.21.refs_1_) | copy-start | bytes 294916
  16.1 40.3 %collective-permute-start.12 = (bf16[256,1024]{1,0:T(8,128)(2,1)S(1)}, bf16[256,1024]{1,0:T(8,128)(2,1)S(1)}, u32[]{:S(2)}, u32[]{:S(2)}) collective-permute-start(bf16[256,1024]{1,0:T(8,128)(2,1)S(1)} %copy-done), channel_id=1, source_target_pairs={{0,2},{1,3},{2,0},{3,1},{4,6},{5,7},{6,4},{7,5},{8,10},{9,11},{10,... | collective-permute-start | bytes 1572872 | tf_op jit(solution)/shard_map/ppermute | solution.py:45
  17.5 16.5 %copy-start.24 = (bf16[64,768]{1,0:T(8,128)(2,1)}, bf16[64,768]{1,0:T(8,128)(2,1)S(1)}, u32[]{:S(2)}) copy-start(bf16[64,768]{1,0:T(8,128)(2,1)S(1)} %collective-permute-done.22.refs_2_) | copy-start | bytes 294916
  17.5 14.7 %collective-permute-start.3 = (bf16[64,768]{1,0:T(8,128)(2,1)S(1)}, bf16[64,768]{1,0:T(8,128)(2,1)S(1)}, u32[]{:S(2)}, u32[]{:S(2)}) collective-permute-start(bf16[64,768]{1,0:T(8,128)(2,1)S(1)} %get-tuple-element.22.refs_0_), channel_id=1, source_target_pairs={{0,2},{1,3},{2,0},{3,1},{4,6},{5,7},{6,4},{7,5},{8,10},{9,11},{10,... | collective-permute-start | bytes 294920 | tf_op jit(solution)/shard_map/ppermute | solution.py:45
  18.2 25.7 %copy-start.21 = (bf16[64,768]{1,0:T(8,128)(2,1)}, bf16[64,768]{1,0:T(8,128)(2,1)S(1)}, u32[]{:S(2)}) copy-start(bf16[64,768]{1,0:T(8,128)(2,1)S(1)} %collective-permute-done.15.refs_1_) | copy-start | bytes 294916
  18.2 14.5 %collective-permute-start.23 = (bf16[64,768]{1,0:T(8,128)(2,1)S(1)}, bf16[64,768]{1,0:T(8,128)(2,1)S(1)}, u32[]{:S(2)}, u32[]{:S(2)}) collective-permute-start(bf16[64,768]{1,0:T(8,128)(2,1)S(1)} %collective-permute-done.21.refs_1_), channel_id=1, source_target_pairs={{0,1},{1,0},{2,3},{3,2},{4,5},{5,4},{6,7},{7,6},{8,9},{9,8},{10,11... | collective-permute-start | bytes 294920 | tf_op jit(solution)/shard_map/ppermute | solution.py:45
  32.2 16.9 %copy-start.22 = (bf16[64,768]{1,0:T(8,128)(2,1)}, bf16[64,768]{1,0:T(8,128)(2,1)S(1)}, u32[]{:S(2)}) copy-start(bf16[64,768]{1,0:T(8,128)(2,1)S(1)} %collective-permute-done.3.refs_1_) | copy-start | bytes 294916
  32.2 7.0 %collective-permute-start.16 = (bf16[64,768]{1,0:T(8,128)(2,1)S(1)}, bf16[64,768]{1,0:T(8,128)(2,1)S(1)}, u32[]{:S(2)}, u32[]{:S(2)}) collective-permute-start(bf16[64,768]{1,0:T(8,128)(2,1)S(1)} %get-tuple-element.21.refs_0_), channel_id=1, source_target_pairs={{0,1},{1,0},{2,3},{3,2},{4,5},{5,4},{6,7},{7,6},{8,9},{9,8},{10,11... | collective-permute-start | bytes 294920 | tf_op jit(solution)/shard_map/ppermute | solution.py:45
  32.2 7.2 %collective-permute-start.4 = (bf16[64,768]{1,0:T(8,128)(2,1)S(1)}, bf16[64,768]{1,0:T(8,128)(2,1)S(1)}, u32[]{:S(2)}, u32[]{:S(2)}) collective-permute-start(bf16[64,768]{1,0:T(8,128)(2,1)S(1)} %get-tuple-element.22.refs_0_), channel_id=1, source_target_pairs={{0,1},{1,0},{2,3},{3,2},{4,5},{5,4},{6,7},{7,6},{8,9},{9,8},{10,11... | collective-permute-start | bytes 294920 | tf_op jit(solution)/shard_map/ppermute | solution.py:45
  32.7 9.3 %collective-permute-start.17 = (bf16[64,768]{1,0:T(8,128)(2,1)S(1)}, bf16[64,768]{1,0:T(8,128)(2,1)S(1)}, u32[]{:S(2)}, u32[]{:S(2)}) collective-permute-start(bf16[64,768]{1,0:T(8,128)(2,1)S(1)} %collective-permute-done.15.refs_1_), channel_id=1, source_target_pairs={{0,1},{1,0},{2,3},{3,2},{4,5},{5,4},{6,7},{7,6},{8,9},{9,8},{10,11... | collective-permute-start | bytes 294920 | tf_op jit(solution)/shard_map/ppermute | solution.py:45
  32.8 10.9 %collective-permute-start.5 = (bf16[64,768]{1,0:T(8,128)(2,1)S(1)}, bf16[64,768]{1,0:T(8,128)(2,1)S(1)}, u32[]{:S(2)}, u32[]{:S(2)}) collective-permute-start(bf16[64,768]{1,0:T(8,128)(2,1)S(1)} %collective-permute-done.3.refs_1_), channel_id=1, source_target_pairs={{0,1},{1,0},{2,3},{3,2},{4,5},{5,4},{6,7},{7,6},{8,9},{9,8},{10,11... | collective-permute-start | bytes 294920 | tf_op jit(solution)/shard_map/ppermute | solution.py:45
  39.2 24.4 %collective-permute-start.13 = (bf16[256,1024]{1,0:T(8,128)(2,1)S(1)}, bf16[256,1024]{1,0:T(8,128)(2,1)S(1)}, u32[]{:S(2)}, u32[]{:S(2)}) collective-permute-start(bf16[256,1024]{1,0:T(8,128)(2,1)S(1)} %copy-done), channel_id=1, source_target_pairs={{0,1},{1,0},{2,3},{3,2},{4,5},{5,4},{6,7},{7,6},{8,9},{9,8},{10,11... | collective-permute-start | bytes 1572872 | tf_op jit(solution)/shard_map/ppermute | solution.py:45
  39.3 9.7 %copy-start.25 = (bf16[64,768]{1,0:T(8,128)(2,1)}, bf16[64,768]{1,0:T(8,128)(2,1)S(1)}, u32[]{:S(2)}) copy-start(bf16[64,768]{1,0:T(8,128)(2,1)S(1)} %collective-permute-done.4.refs_2_) | copy-start | bytes 294916
  39.3 14.9 %collective-permute-start.2 = (bf16[4,3,1152]{2,1,0:T(4,128)(2,1)S(1)}, bf16[4,3,1152]{2,1,0:T(4,128)(2,1)S(1)}, u32[]{:S(2)}, u32[]{:S(2)}) collective-permute-start(bf16[4,3,1152]{2,1,0:T(4,128)(2,1)S(1)} %pad_maximum_fusion.3), channel_id=1, source_target_pairs={{0,16},{4,20},{8,24},{12,28},{16,0},{20,4},{24,8},{28,12},{1,17},{... | collective-permute-start | bytes 82952 | tf_op jit(solution)/shard_map/ppermute | solution.py:45
  41.9 12.8 %collective-permute-start.24 = (bf16[256,256]{1,0:T(8,128)(2,1)}, bf16[256,256]{1,0:T(8,128)(2,1)S(1)}, u32[]{:S(2)}, u32[]{:S(2)}) collective-permute-start(bf16[256,256]{1,0:T(8,128)(2,1)} %get-tuple-element.17.refs_0_), channel_id=1, source_target_pairs={{0,2},{1,3},{2,0},{3,1},{4,6},{5,7},{6,4},{7,5},{8,10},{9,11},{10,... | collective-permute-start | bytes 393224 | tf_op jit(solution)/shard_map/ppermute | solution.py:45
  43.7 12.7 %collective-permute-start.25 = (bf16[256,256]{1,0:T(8,128)(2,1)}, bf16[256,256]{1,0:T(8,128)(2,1)S(1)}, u32[]{:S(2)}, u32[]{:S(2)}) collective-permute-start(bf16[256,256]{1,0:T(8,128)(2,1)} %get-tuple-element.17.refs_0_), channel_id=1, source_target_pairs={{0,1},{1,0},{2,3},{3,2},{4,5},{5,4},{6,7},{7,6},{8,9},{9,8},{10,11... | collective-permute-start | bytes 393224 | tf_op jit(solution)/shard_map/ppermute | solution.py:45
  49.0 7.8 %copy-start.30 = (bf16[3,1152]{1,0:T(4,128)(2,1)S(1)}, bf16[3,1152]{1,0:T(4,128)(2,1)}, u32[]{:S(2)}) copy-start(bf16[3,1152]{1,0:T(4,128)(2,1)} %get-tuple-element.10) | copy-start | bytes 20740
  54.2 6.4 %collective-permute-start.18 = (bf16[256,256]{1,0:T(8,128)(2,1)S(1)}, bf16[256,256]{1,0:T(8,128)(2,1)S(1)}, u32[]{:S(2)}, u32[]{:S(2)}) collective-permute-start(bf16[256,256]{1,0:T(8,128)(2,1)S(1)} %copy-done.13), channel_id=1, source_target_pairs={{0,2},{1,3},{2,0},{3,1},{4,6},{5,7},{6,4},{7,5},{8,10},{9,11},{10,... | collective-permute-start | bytes 393224 | tf_op jit(solution)/shard_map/ppermute | solution.py:45
  54.7 8.9 %copy-start.11 = (bf16[256,256]{1,0:T(8,128)(2,1)}, bf16[256,256]{1,0:T(8,128)(2,1)S(1)}, u32[]{:S(2)}) copy-start(bf16[256,256]{1,0:T(8,128)(2,1)S(1)} %collective-permute-done.24.refs_1_) | copy-start | bytes 393220
  54.8 8.3 %collective-permute-start.9 = (bf16[256,256]{1,0:T(8,128)(2,1)}, bf16[256,256]{1,0:T(8,128)(2,1)S(1)}, u32[]{:S(2)}, u32[]{:S(2)}) collective-permute-start(bf16[256,256]{1,0:T(8,128)(2,1)} %get-tuple-element.13.refs_0_), channel_id=1, source_target_pairs={{0,2},{1,3},{2,0},{3,1},{4,6},{5,7},{6,4},{7,5},{8,10},{9,11},{10,... | collective-permute-start | bytes 393224 | tf_op jit(solution)/shard_map/ppermute | solution.py:45
  56.3 7.3 %copy-start.12 = (bf16[256,256]{1,0:T(8,128)(2,1)}, bf16[256,256]{1,0:T(8,128)(2,1)S(1)}, u32[]{:S(2)}) copy-start(bf16[256,256]{1,0:T(8,128)(2,1)S(1)} %collective-permute-done.25.refs_2_) | copy-start | bytes 393220
  56.3 6.7 %collective-permute-start.26 = (bf16[256,256]{1,0:T(8,128)(2,1)S(1)}, bf16[256,256]{1,0:T(8,128)(2,1)S(1)}, u32[]{:S(2)}, u32[]{:S(2)}) collective-permute-start(bf16[256,256]{1,0:T(8,128)(2,1)S(1)} %collective-permute-done.24.refs_1_), channel_id=1, source_target_pairs={{0,1},{1,0},{2,3},{3,2},{4,5},{5,4},{6,7},{7,6},{8,9},{9,8},{10,11... | collective-permute-start | bytes 393224 | tf_op jit(solution)/shard_map/ppermute | solution.py:45
  56.4 7.3 %collective-permute-start.14 = (bf16[256,1024]{1,0:T(8,128)(2,1)S(1)}, bf16[256,1024]{1,0:T(8,128)(2,1)S(1)}, u32[]{:S(2)}, u32[]{:S(2)}) collective-permute-start(bf16[256,1024]{1,0:T(8,128)(2,1)S(1)} %collective-permute-done.12.refs_5_), channel_id=1, source_target_pairs={{0,1},{1,0},{2,3},{3,2},{4,5},{5,4},{6,7},{7,6},{8,9},{9,8},{10,11... | collective-permute-start | bytes 1572872 | tf_op jit(solution)/shard_map/ppermute | solution.py:45
  60.7 9.1 %copy-start.15 = (bf16[256,256]{1,0:T(8,128)(2,1)}, bf16[256,256]{1,0:T(8,128)(2,1)S(1)}, u32[]{:S(2)}) copy-start(bf16[256,256]{1,0:T(8,128)(2,1)S(1)} %collective-permute-done.18.refs_1_) | copy-start | bytes 393220
  60.7 9.0 %collective-permute-start.19 = (bf16[256,256]{1,0:T(8,128)(2,1)S(1)}, bf16[256,256]{1,0:T(8,128)(2,1)S(1)}, u32[]{:S(2)}, u32[]{:S(2)}) collective-permute-start(bf16[256,256]{1,0:T(8,128)(2,1)S(1)} %copy-done.13), channel_id=1, source_target_pairs={{0,1},{1,0},{2,3},{3,2},{4,5},{5,4},{6,7},{7,6},{8,9},{9,8},{10,11... | collective-permute-start | bytes 393224 | tf_op jit(solution)/shard_map/ppermute | solution.py:45
  63.0 12.6 %copy-start.14 = (bf16[256,256]{1,0:T(8,128)(2,1)}, bf16[256,256]{1,0:T(8,128)(2,1)S(1)}, u32[]{:S(2)}) copy-start(bf16[256,256]{1,0:T(8,128)(2,1)S(1)} %collective-permute-done.9.refs_1_) | copy-start | bytes 393220
  63.0 12.6 %collective-permute-start.10 = (bf16[256,256]{1,0:T(8,128)(2,1)}, bf16[256,256]{1,0:T(8,128)(2,1)S(1)}, u32[]{:S(2)}, u32[]{:S(2)}) collective-permute-start(bf16[256,256]{1,0:T(8,128)(2,1)} %get-tuple-element.13.refs_0_), channel_id=1, source_target_pairs={{0,1},{1,0},{2,3},{3,2},{4,5},{5,4},{6,7},{7,6},{8,9},{9,8},{10,11... | collective-permute-start | bytes 393224 | tf_op jit(solution)/shard_map/ppermute | solution.py:45
  63.0 6.7 %collective-permute-start.20 = (bf16[256,256]{1,0:T(8,128)(2,1)S(1)}, bf16[256,256]{1,0:T(8,128)(2,1)S(1)}, u32[]{:S(2)}, u32[]{:S(2)}) collective-permute-start(bf16[256,256]{1,0:T(8,128)(2,1)S(1)} %collective-permute-done.18.refs_1_), channel_id=1, source_target_pairs={{0,1},{1,0},{2,3},{3,2},{4,5},{5,4},{6,7},{7,6},{8,9},{9,8},{10,11... | collective-permute-start | bytes 393224 | tf_op jit(solution)/shard_map/ppermute | solution.py:45
  63.5 12.1 %collective-permute-start.11 = (bf16[256,256]{1,0:T(8,128)(2,1)S(1)}, bf16[256,256]{1,0:T(8,128)(2,1)S(1)}, u32[]{:S(2)}, u32[]{:S(2)}) collective-permute-start(bf16[256,256]{1,0:T(8,128)(2,1)S(1)} %collective-permute-done.9.refs_1_), channel_id=1, source_target_pairs={{0,1},{1,0},{2,3},{3,2},{4,5},{5,4},{6,7},{7,6},{8,9},{9,8},{10,11... | collective-permute-start | bytes 393224 | tf_op jit(solution)/shard_map/ppermute | solution.py:45
  84.2 1.4 %collective-permute-start.27 = (f32[3,1024]{1,0:T(4,128)}, f32[3,1024]{1,0:T(4,128)S(1)}, u32[]{:S(2)}, u32[]{:S(2)}) collective-permute-start(f32[3,1024]{1,0:T(4,128)} %reduce.3), channel_id=1, source_target_pairs={{0,1},{1,0},{2,3},{3,2},{4,5},{5,4},{6,7},{7,6},{8,9},{9,8},{10,11... | collective-permute-start | bytes 36872 | tf_op jit(solution)/shard_map/ppermute | solution.py:45
  86.4 3.7 %collective-permute-start.28 = (f32[3,1024]{1,0:T(4,128)S(1)}, f32[3,1024]{1,0:T(4,128)S(1)}, u32[]{:S(2)}, u32[]{:S(2)}) collective-permute-start(f32[3,1024]{1,0:T(4,128)S(1)} %add.43), channel_id=1, source_target_pairs={{0,2},{1,3},{2,0},{3,1},{4,6},{5,7},{6,4},{7,5},{8,10},{9,11},{10,... | collective-permute-start | bytes 36872 | tf_op jit(solution)/shard_map/ppermute | solution.py:45
  90.1 3.7 %collective-permute-start.29 = (f32[1,3,1024]{2,1,0:T(4,128)S(1)}, f32[1,3,1024]{2,1,0:T(4,128)S(1)}, u32[]{:S(2)}, u32[]{:S(2)}) collective-permute-start(f32[1,3,1024]{2,1,0:T(4,128)S(1)} %add_bitcast_fusion), channel_id=1, source_target_pairs={{0,4},{4,0},{8,12},{12,8},{16,20},{20,16},{24,28},{28,24},{1,5},{5... | collective-permute-start | bytes 36872 | tf_op jit(solution)/shard_map/ppermute | solution.py:45
  93.8 4.0 %collective-permute-start.30 = (f32[2,3,1024]{2,1,0:T(4,128)S(1)}, f32[2,3,1024]{2,1,0:T(4,128)S(1)}, u32[]{:S(2)}, u32[]{:S(2)}) collective-permute-start(f32[2,3,1024]{2,1,0:T(4,128)S(1)} %pad_maximum_fusion.4), channel_id=1, source_target_pairs={{0,8},{4,12},{8,0},{12,4},{16,24},{20,28},{24,16},{28,20},{1,9},{5... | collective-permute-start | bytes 73736 | tf_op jit(solution)/shard_map/ppermute | solution.py:45
  97.9 5.2 %collective-permute-start.31 = (f32[4,3,1024]{2,1,0:T(4,128)S(1)}, f32[4,3,1024]{2,1,0:T(4,128)S(1)}, u32[]{:S(2)}, u32[]{:S(2)}) collective-permute-start(f32[4,3,1024]{2,1,0:T(4,128)S(1)} %pad_maximum_fusion.2), channel_id=1, source_target_pairs={{0,16},{4,20},{8,24},{12,28},{16,0},{20,4},{24,8},{28,12},{1,17},{... | collective-permute-start | bytes 147464 | tf_op jit(solution)/shard_map/ppermute | solution.py:45
  (15 other events, 34.0 us)

commit v2 on v1

--- a/solution.py
+++ b/solution.py
@@ -7,12 +7,15 @@
 from jax.experimental.pallas import tpu as pltpu
 from jax.sharding import PartitionSpec as P
 
+
 HEAD_DIM = 64
 SEL_DEV = 2
 SEND_MOST = 3
 RECV_MOST = 4
 META = 128
+PIECES = 2
 EPS = 1e-06
+
 
 VMEM = pltpu.MemorySpace.VMEM
 SMEM = pltpu.MemorySpace.SMEM
@@ -62,16 +65,63 @@
     return blocks, order
 
 
+def small(mib):
+    return pltpu.CompilerParams(vmem_limit_bytes=mib << 20)
+
+
+def join_kernel(own_ref, other_ref, out_ref):
+    count = own_ref.shape[0]
+    out_ref[:count] = own_ref[...]
+    out_ref[count:] = other_ref[...]
+
+
+def join(own, other):
+    return pl.pallas_call(
+        join_kernel,
+        out_shape=jax.ShapeDtypeStruct((2 * own.shape[0],) + own.shape[1:], own.dtype),
+        in_specs=[vmem()] * 2,
+        out_specs=vmem(),
+        compiler_params=small(2),
+    )(own, other)
+
+
+def add_kernel(own_ref, other_ref, out_ref):
+    out_ref[...] = own_ref[...] + other_ref[...]
+
+
+def add(own, other):
+    return pl.pallas_call(
+        add_kernel,
+        out_shape=jax.ShapeDtypeStruct(own.shape, own.dtype),
+        in_specs=[vmem()] * 2,
+        out_specs=vmem(),
+        name="add",
+        compiler_params=small(1),
+    )(own, other)
+
+
 def double_stack(values, axis):
-    stacked = values[None]
+    size = lax.axis_size(axis)
     bit = 1
-    while bit < lax.axis_size(axis):
-        stacked = jnp.concatenate([stacked, swap(stacked, axis, bit)], axis=0)
+    while 2 * bit < size:
+        values = join(values, swap(values, axis, bit))
         bit *= 2
-    return stacked
-
-
-def pick_kernel(sel_ref, dest_ref, pixels_ref, cap_ref, rows_ref, meta_ref, sems):
+    return values, swap(values, axis, bit)
+
+
+def pick_kernel(pieces, sel_hbm, dest_hbm, pixels_ref, cap_hbm, output_ref, *refs):
+    row_refs = refs[:SEND_MOST]
+    meta_ref, piece_ref, sel_ref, dest_ref, cap_ref, sems = refs[SEND_MOST:]
+    first = [
+        pltpu.make_async_copy(source, target, sems.at[SEND_MOST + 1 + i])
+        for i, (source, target) in enumerate(
+            ((sel_hbm, sel_ref), (dest_hbm, dest_ref), (cap_hbm, cap_ref))
+        )
+    ]
+    for copy in first:
+        copy.start()
+    first[0].wait()
+    first[1].wait()
     count = jnp.int32(0)
     index = [jnp.int32(0)] * SEND_MOST
     target = [jnp.int32(0)] * SEND_MOST
@@ -82,12 +132,18 @@
             index[r] = jnp.where(take, e, index[r])
             target[r] = jnp.where(take, dest_ref[e], target[r])
         count = count + here.astype(jnp.int32)
-    copies = []
-    for r in range(SEND_MOST):
-        copies.append(
-            pltpu.make_async_copy(pixels_ref.at[index[r]], rows_ref.at[r], sems.at[r])
-        )
-        copies[-1].start()
+    copies = [
+        pltpu.make_async_copy(pixels_ref.at[index[r]], row_refs[r], sems.at[r])
+        for r in range(SEND_MOST)
+    ]
+    height = piece_ref.shape[0]
+    start = pl.multiple_of((lax.axis_index("dp") & (pieces - 1)) * height, height)
+    copies.append(
+        pltpu.make_async_copy(output_ref.at[pl.ds(start, height)], piece_ref, sems.at[SEND_MOST])
+    )
+    for copy in copies:
+        copy.start()
+    first[2].wait()
     captions = cap_ref[...].astype(F32)
     width = captions.shape[1]
     example = lax.broadcasted_iota(jnp.int32, captions.shape, 0)
@@ -96,25 +152,101 @@
         row = jnp.sum(jnp.where(example == index[r], captions, 0.0), axis=0, keepdims=True)
         live = (count > r).astype(F32)
         extra = jnp.where(lane == 0, live, jnp.where(lane == 1, target[r].astype(F32), 0.0))
-        meta_ref[r : r + 1, :width] = row.astype(BF16)
-        meta_ref[r : r + 1, width:] = extra.astype(BF16)
+        meta_ref[0, r : r + 1, :width] = row.astype(BF16)
+        meta_ref[0, r : r + 1, width:] = extra.astype(BF16)
     for copy in copies:
         copy.wait()
 
 
-def pick(selection, destination, pixels, captions):
+def pick(selection, destination, pixels, captions, output_weight, pieces):
     _, length, depth = pixels.shape
-    return pl.pallas_call(
-        pick_kernel,
+    fan, width = output_weight.shape
+    hbm = pl.BlockSpec(memory_space=pltpu.MemorySpace.HBM)
+    *rows, caption_meta, piece = pl.pallas_call(
+        functools.partial(pick_kernel, pieces),
+        out_shape=(jax.ShapeDtypeStruct((length, depth), BF16),) * SEND_MOST
+        + (
+            jax.ShapeDtypeStruct((1, SEND_MOST, captions.shape[1] + META), BF16),
+            jax.ShapeDtypeStruct((fan // pieces, width), BF16),
+        ),
+        in_specs=[hbm] * 5,
+        out_specs=(vmem(),) * (SEND_MOST + 2),
+        scratch_shapes=[
+            SMEM(selection.shape, jnp.int32),
+            SMEM(destination.shape, jnp.int32),
+            VMEM(captions.shape, BF16),
+            pltpu.SemaphoreType.DMA((SEND_MOST + 4,)),
+        ],
+        name="pick",
+        compiler_params=small(2),
+    )(*(
+        pltpu.with_memory_space_constraint(array, pltpu.MemorySpace.HBM)
+        for array in (selection, destination, pixels, captions, output_weight)
+    ))
+    return rows, caption_meta, piece
+
+
+def assemble_kernel(*refs):
+    out_ref = refs[-1]
+    pieces = refs[:-1]
+    height = pieces[0].shape[0]
+    here = lax.axis_index("dp") & (len(pieces) - 1)
+    for j, ref in enumerate(pieces):
+        start = pl.multiple_of((here ^ j) * height, height)
+        out_ref[pl.ds(start, height), :] = ref[...]
+
+
+def assemble(pieces):
+    height, width = pieces[0].shape
+    return pl.pallas_call(
+        assemble_kernel,
+        out_shape=jax.ShapeDtypeStruct((height * len(pieces), width), BF16),
+        in_specs=[vmem()] * len(pieces),
+        out_specs=vmem(),
+        name="assemble",
+        compiler_params=small(2),
+    )(*pieces)
+
+
+def route_kernel(first_ref, second_ref, cap_ref, meta_ref):
+    half = first_ref.shape[0]
+    rows = jnp.concatenate(
+        [ref[j].astype(F32) for ref in (first_ref, second_ref) for j in range(half)], axis=0
+    )
+    width = cap_ref.shape[1]
+    cap_ref[...] = unit_rows(rows[:, :width])
+    extra = rows[:, width:]
+    live, target = extra[:, 0:1], extra[:, 1:2]
+    me = lax.axis_index("dp")
+    offset = lax.broadcasted_iota(jnp.int32, (SEND_MOST, 1), 0)
+    spot = jnp.concatenate([(me ^ j) * SEND_MOST + offset for j in range(2 * half)], axis=0)
+    mine = (live > 0.0) & (target == me.astype(F32))
+    mine = jnp.where(mine, 1.0, 0.0)
+    count = rows.shape[0]
+    square = (count, count)
+    same = lax.broadcasted_iota(jnp.int32, square, 0) == lax.broadcasted_iota(jnp.int32, square, 1)
+    mine_row = jnp.sum(jnp.where(same, mine, 0.0), axis=0, keepdims=True)
+    spot_col = spot.astype(F32)
+    spot_row = jnp.sum(jnp.where(same, spot_col, 0.0), axis=0, keepdims=True)
+    place = jnp.sum(jnp.where(spot_row < spot_col, mine_row, 0.0), axis=1, keepdims=True)
+    lane = lax.broadcasted_iota(jnp.int32, (count, META), 1)
+    slot = jnp.where(place == (lane - 1).astype(F32), mine, 0.0)
+    meta_ref[...] = jnp.where(lane == 0, live, slot)
+
+
+def route(first, second):
+    count = 2 * first.shape[0] * SEND_MOST
+    return pl.pallas_call(
+        route_kernel,
         out_shape=(
-            jax.ShapeDtypeStruct((SEND_MOST, length, depth), BF16),
-            jax.ShapeDtypeStruct((SEND_MOST, captions.shape[1] + META), BF16),
+            jax.ShapeDtypeStruct((count, first.shape[2] - META), F32),
+            jax.ShapeDtypeStruct((count, META), F32),
         ),
-        in_specs=[smem(), smem(), pl.BlockSpec(memory_space=pl.ANY), vmem()],
-        out_specs=(vmem(), vmem()),
-        scratch_shapes=[pltpu.SemaphoreType.DMA((SEND_MOST,))],
-        name="pick",
-    )(selection, destination, pixels, captions)
+        in_specs=[vmem()] * 2,
+        out_specs=(vmem(),) * 2,
+        name="route",
+        compiler_params=small(6),
+    )(first, second)
 
 
 def attend_kernel(shards, gains_ref, patch_ref, qkv_ref, *refs):
@@ -155,7 +287,7 @@
         ),
         in_specs=[vmem()] * (3 + 2 * shards),
         out_specs=(vmem(), vmem()),
-        name="attend",
+        compiler_params=small(14),
     )(gains, patch_weight, qkv, *pixels, *positions)
 
 
@@ -183,11 +315,11 @@
         out_shape=jax.ShapeDtypeStruct((2, width), F32),
         in_specs=[vmem()] * (3 + 2 * len(order)),
         out_specs=vmem(),
-        name="expand",
+        compiler_params=small(14),
     )(gains, up_weight, hidden, *contexts, *outputs)
 
 
-def reduce_kernel(scale, own_ref, down_ref, *refs):
+def reduce_kernel(scale, down_ref, *refs):
     out_ref = refs[-1]
     sums = refs[:-1]
     units = jnp.concatenate([ref[1:2, :] for ref in sums], axis=0) * scale
@@ -197,64 +329,64 @@
     both = jnp.concatenate([high, low], axis=0)
     product = jnp.dot(both, down_ref[...], preferred_element_type=F32)
     count = len(sums)
-    own = own_ref[0].astype(F32)
+    own = (lax.axis_index("mp") == 0).astype(F32)
     out_ref[...] = product[:count] + product[count:] + residual * own
 
 
-def reduce_units(sums, own, down_weight, patches):
+def reduce_units(sums, down_weight, patches):
     return pl.pallas_call(
         functools.partial(reduce_kernel, 1.0 / patches),
         out_shape=jax.ShapeDtypeStruct((len(sums), down_weight.shape[1]), F32),
-        in_specs=[smem()] + [vmem()] * (1 + len(sums)),
+        in_specs=[vmem()] * (1 + len(sums)),
         out_specs=vmem(),
         name="reduce",
-    )(own, down_weight, *sums)
-
-
-def finish_kernel(total, params_ref, gains_ref, weight_ref, cap_ref, meta_ref, pooled_ref, out_ref, loss_ref):
-    count = meta_ref.shape[0]
-    rows = [
-        pooled_ref[c // SEND_MOST, c % SEND_MOST : c % SEND_MOST + 1, :] for c in range(count)
-    ]
+        compiler_params=small(6),
+    )(down_weight, *sums)
+
+
+def finish_kernel(total, params_ref, gains_ref, weight_ref, cap_ref, meta_ref, first_ref, second_ref, out_ref, loss_ref):
+    half = first_ref.shape[0]
+    rows = jnp.concatenate(
+        [ref[j] for ref in (first_ref, second_ref) for j in range(half)], axis=0
+    )
     meta = meta_ref[...]
     live = meta[:, 0:1]
-    slots = []
-    for k in range(RECV_MOST):
-        acc = None
-        for c in range(count):
-            term = jnp.where(meta[c : c + 1, k + 1 : k + 2] > 0.0, rows[c], 0.0)
-            acc = term if acc is None else acc + term
-        slots.append(acc)
-    pooled = jnp.concatenate(slots, axis=0)
-    filled = jnp.max(meta[:, 1 : RECV_MOST + 1], axis=0, keepdims=True)
+    pooled = jnp.concatenate(
+        [
+            jnp.sum(jnp.where(meta[:, k + 1 : k + 2] > 0.0, rows, 0.0), axis=0, keepdims=True)
+            for k in range(RECV_MOST)
+        ],
+        axis=0,
+    )
+    filled = jnp.max(meta, axis=0, keepdims=True)
     normed = layer_norm(pooled, gains_ref[2:3, :]).astype(BF16)
     embedded = jnp.dot(normed, weight_ref[...], preferred_element_type=F32)
     captions = cap_ref[...]
     scale = 10.0 * jnp.exp(jnp.full((1, 1), params_ref[0], F32))
     shift = 2.0 * params_ref[1]
     for k in range(RECV_MOST):
-        used = filled[:, k : k + 1] > 0.0
-        row = jnp.where(used, embedded[k : k + 1, :], 0.0)
+        used = filled[:, k + 1 : k + 2]
+        row = jnp.where(used > 0.0, embedded[k : k + 1, :], 0.0)
         out_ref[k : k + 1, :] = row
         logits = scale * jnp.sum(captions * unit_rows(row), axis=1, keepdims=True) + shift
         signs = jnp.where(meta[:, k + 1 : k + 2] > 0.0, 1.0, -1.0)
         value = -signs * logits
         terms = jnp.maximum(value, 0.0) + jnp.log1p(jnp.exp(-jnp.abs(value)))
-        lost = jnp.sum(terms * live) / total
-        loss_ref[k] = jnp.where(jnp.max(jnp.where(used, 1.0, 0.0)) > 0.0, lost, 0.0)
-
-
-def finish(pooled, captions, meta, params, gains, weight, total):
+        loss_ref[k] = jnp.sum(terms * live * used) / total
+
+
+def finish(first, second, captions, meta, params, gains, weight, total):
     return pl.pallas_call(
         functools.partial(finish_kernel, total),
         out_shape=(
             jax.ShapeDtypeStruct((RECV_MOST, weight.shape[1]), F32),
             jax.ShapeDtypeStruct((RECV_MOST,), F32),
         ),
-        in_specs=[smem()] + [vmem()] * 5,
+        in_specs=[smem()] + [vmem()] * 6,
         out_specs=(vmem(), smem()),
         name="finish",
-    )(params, gains, weight, captions, meta, pooled)
+        compiler_params=small(8),
+    )(params, gains, weight, captions, meta, first, second)
 
 
 def per_device(
@@ -273,39 +405,46 @@
     loss_params,
 ):
     devices_dp = lax.axis_size("dp")
-    rows, caption_meta = pick(selection, destination, pixels, caption_vectors)
+    shards = lax.axis_size("mp")
+    pieces = count_pieces(devices_dp)
     positions, order = gather_blocks(position, "mp")
-    pixel_blocks = [gather_blocks(rows[r], "mp")[0] for r in range(SEND_MOST)]
-    outputs, _ = gather_blocks(output_weight, "mp")
-
-    me = lax.axis_index("dp")
-    width = caption_vectors.shape[1]
-    gathered = double_stack(caption_meta, "dp").reshape(devices_dp * SEND_MOST, width + META)
-    captions = unit_rows(gathered[:, :width].astype(F32))
-    live = gathered[:, width] > 0
-    target = gathered[:, width + 1].astype(jnp.int32)
-    spot = (me ^ jnp.arange(devices_dp, dtype=jnp.int32))[:, None] * SEND_MOST
-    spot = (spot + jnp.arange(SEND_MOST, dtype=jnp.int32)).reshape(-1)
-    mine = live & (target == me)
-    ahead = mine[None, :] & (spot[None, :] < spot[:, None])
-    place = jnp.sum(ahead.astype(jnp.int32), axis=1)
-    slot = mine[:, None] & (place[:, None] == jnp.arange(RECV_MOST, dtype=jnp.int32))
-    meta = jnp.concatenate([live[:, None], slot], axis=1).astype(F32)
+    rows, caption_meta, piece = pick(
+        selection, destination, pixels, caption_vectors, output_weight, pieces
+    )
+    pixel_blocks = [gather_blocks(row, "mp")[0] for row in rows]
+
+    parts = [swap(piece, "mp", shards // 2)]
+    bit = 1
+    while bit < pieces:
+        parts = parts + [swap(part, "dp", bit) for part in parts]
+        bit *= 2
+    outputs = [output_weight, assemble(parts)]
+    for bit in bits_down(shards)[1:]:
+        outputs = outputs + [swap(block, "mp", bit) for block in outputs]
+
+    captions, meta = route(*double_stack(caption_meta, "dp"))
 
     sums = []
     for r in range(SEND_MOST):
-        hidden, context = attend(pixel_blocks[r], positions, norm_gains, patch_weight, query_key_value)
+        hidden, context = attend(
+            pixel_blocks[r], positions, norm_gains, patch_weight, query_key_value
+        )
         contexts, _ = gather_blocks(context, "mp")
         sums.append(expand(contexts, order, outputs, hidden, norm_gains, up_weight))
-    own = (lax.axis_index("mp") == 0).astype(jnp.int32).reshape(1)
-    patches = position.shape[0] * len(order)
-    pooled = reduce_units(sums, own, down_weight, patches)
-    for bit in reversed(bits_down(lax.axis_size("mp"))):
-        pooled = pooled + swap(pooled, "mp", bit)
-    pooled = double_stack(pooled, "dp")
+    pooled = reduce_units(sums, down_weight, position.shape[0] * shards)
+    for bit in reversed(bits_down(shards)):
+        pooled = add(pooled, swap(pooled, "mp", bit))
+    first, second = double_stack(pooled[None], "dp")
     return finish(
-        pooled, captions, meta, loss_params, norm_gains, embedding_weight, float(devices_dp * SEL_DEV)
-    )
+        first, second, captions, meta, loss_params, norm_gains, embedding_weight, float(devices_dp * SEL_DEV)
+    )
+
+
+def count_pieces(devices_dp):
+    pieces = 1
+    while pieces < PIECES and 2 * pieces <= devices_dp:
+        pieces *= 2
+    return pieces
 
 
 def solution(mesh):
@@ -325,6 +464,7 @@
         P(),
     )
     out_specs = (P("dp", None), P("dp"))
+
     return jax.shard_map(
         per_device, mesh=mesh, in_specs=in_specs, out_specs=out_specs, check_vma=False
     )

time: 108 us -> 79.3 us (0.73)
  Pallas kernels: 39.8 us -> 18.1 us
  other arithmetic: 4.97 us -> 0 us
  local copies, waits for them, and re-layouts: 3.47 us -> 0.95 us
  starting transfers between devices: 22.7 us -> 24 us
    pallas_call x3, Pallas kernels: 15.6 us -> 5.89 us  [expand(): pl.pallas_call(functools.partial(expand_kernel, tuple(order)), out_shape=...]
    pallas_call x3, Pallas kernels: 15.5 us -> 7.22 us  [attend(): pl.pallas_call(functools.partial(attend_kernel, shards), out_shape=(jax.S...]
    pallas_call x1, Pallas kernels: 2.61 us -> 0.38 us  [reduce_units(): pl.pallas_call(functools.partial(reduce_kernel, 1.0 / patches), out_shape...]
    concatenate x6 -> x0, other arithmetic: 2.22 us -> none  [double_stack(): stacked = jnp.concatenate([stacked, swap(stacked, axis, bit)], axis=0)]
    unnamed x62 -> x20, local copies, waits for them, and re-layouts: 2.34 us -> 0.95 us
    ppermute x32 -> x33, starting transfers between devices: 22.7 us -> 24 us  [swap(): return lax.ppermute(values, axis, [(i, i ^ bit) for i in range(size)])]
    pallas_call x1, Pallas kernels: 3.44 us -> 2.15 us  [finish(): pl.pallas_call(functools.partial(finish_kernel, total), out_shape=(jax.Sh...]
    pallas_call x1 -> x9, Pallas kernels: 2.66 us -> 2.42 us  [the longest x1 2.1 us: pick(): pl.pallas_call(functools.partial(pick_kernel, pieces), out_shape=(jax.Sha...]
  transfers between devices with their start and end apart: 32 -> 33, of which waited for: 9 -> 14; matrix products, arithmetic and copies ran while one was open for 4% -> 0% of each run, Pallas kernels for 24% -> 14%
where the time goes in v2:
time: 79.3 us; the launch traced here: 79.2 us
  waiting for transfers between devices  35.4 us (45%)
  starting transfers between devices  24 us (30%)
  Pallas kernels  18.1 us (23%)
  local copies, waits for them, and re-layouts  0.95 us (1%)
  between operations  0.83 us (1%)
    ppermute x33, waiting for transfers between devices, swap(): return lax.ppermute(values, axis, [(i, i ^ bit) for i in range(size)])  35.4 us
    ppermute x33, starting transfers between devices, swap(): return lax.ppermute(values, axis, [(i, i ^ bit) for i in range(size)])  24 us
    pallas_call x3, Pallas kernels, attend(): pl.pallas_call(functools.partial(attend_kernel, shards), out_shape=(jax.S...  7.22 us
    pallas_call x3, Pallas kernels, expand(): pl.pallas_call(functools.partial(expand_kernel, tuple(order)), out_shape=...  5.89 us
    pallas_call x1, Pallas kernels, finish(): pl.pallas_call(functools.partial(finish_kernel, total), out_shape=(jax.Sh...  2.15 us
    pallas_call x1, Pallas kernels, pick(): pl.pallas_call(functools.partial(pick_kernel, pieces), out_shape=(jax.Sha...  2.1 us
  transfers between devices with their start and end apart: 33, of which 14 were waited for; matrix products, arithmetic and copies ran while one was open for 0% of the time, Pallas kernels for 14%

profile of v2, /device:TPU:0, one launch (start us, length us, event | category | flops | bytes accessed | tf_op | source)
XLA Modules:
  0.0 79.2 jit_solution(2255018134602524368)
XLA Ops:
  0.7 2.1 %pick.1 = (bf16[64,768]{1,0:T(8,128)(2,1)S(1)}, bf16[64,768]{1,0:T(8,128)(2,1)S(1)}, bf16[64,768]{1,0:T(8,128)(2,1)S(1)}, bf16[1,3,1152]{2,1,0:T(4,128)(2,1)S(1)}, bf16[128,1024]{1,0:T(8,128)(2,1)S(1)}) custom-call(s32[16]{0:T(128)} %sel_hbm.1, s32[16]{0:T(128)} %dest_hbm.1, bf16[16,64,768]{2,1,0:T(8,128)(2,1)} %pixels_ref.1, bf16[16,1024]{1,0:T(8,128)(2,1)} %cap_hbm.1, ...), custom_call_target="tpu_custom_call" | custom-call | tf_op jit(solution)/shard_map/pick/pallas_call | solution.py:165
  2.8 3.0 %collective-permute-start.12 = (bf16[128,1024]{1,0:T(8,128)(2,1)S(1)}, bf16[128,1024]{1,0:T(8,128)(2,1)S(1)}, u32[]{:S(2)}, u32[]{:S(2)}) collective-permute-start(bf16[128,1024]{1,0:T(8,128)(2,1)S(1)} %get-tuple-element.21), channel_id=1, source_target_pairs={{0,2},{1,3},{2,0},{3,1},{4,6},{5,7},{6,4},{7,5},{8,10},{9,11},{10,... | collective-permute-start | bytes 786440 | tf_op jit(solution)/shard_map/ppermute | solution.py:48
  5.8 6.3 %collective-permute-done.12.refs_0_ = bf16[128,1024]{1,0:T(8,128)(2,1)S(1)} collective-permute-done((bf16[128,1024]{1,0:T(8,128)(2,1)S(1)}, bf16[128,1024]{1,0:T(8,128)(2,1)S(1)}, u32[]{:S(2)}, u32[]{:S(2)}) %collective-permute-start.12) | collective-permute-done | bytes 262176 | tf_op jit(solution)/shard_map/ppermute | solution.py:48
  12.1 1.8 %collective-permute-start.13 = (bf16[128,1024]{1,0:T(8,128)(2,1)S(1)}, bf16[128,1024]{1,0:T(8,128)(2,1)S(1)}, u32[]{:S(2)}, u32[]{:S(2)}) collective-permute-start(bf16[128,1024]{1,0:T(8,128)(2,1)S(1)} %collective-permute-done.12.refs_0_), channel_id=1, source_target_pairs={{0,4},{4,0},{8,12},{12,8},{16,20},{20,16},{24,28},{28,24},{1,5},{5... | collective-permute-start | bytes 786440 | tf_op jit(solution)/shard_map/ppermute | solution.py:48
  13.9 1.5 %collective-permute-start.22 = (bf16[64,768]{1,0:T(8,128)(2,1)S(1)}, bf16[64,768]{1,0:T(8,128)(2,1)S(1)}, u32[]{:S(2)}, u32[]{:S(2)}) collective-permute-start(bf16[64,768]{1,0:T(8,128)(2,1)S(1)} %get-tuple-element.25.refs_0_), channel_id=1, source_target_pairs={{0,2},{1,3},{2,0},{3,1},{4,6},{5,7},{6,4},{7,5},{8,10},{9,11},{10,... | collective-permute-start | bytes 294920 | tf_op jit(solution)/shard_map/ppermute | solution.py:48
  15.4 0.5 collective-permute-start.6
  15.9 1.5 %collective-permute-start.16 = (bf16[64,768]{1,0:T(8,128)(2,1)S(1)}, bf16[64,768]{1,0:T(8,128)(2,1)S(1)}, u32[]{:S(2)}, u32[]{:S(2)}) collective-permute-start(bf16[64,768]{1,0:T(8,128)(2,1)S(1)} %get-tuple-element.22.refs_0_), channel_id=1, source_target_pairs={{0,2},{1,3},{2,0},{3,1},{4,6},{5,7},{6,4},{7,5},{8,10},{9,11},{10,... | collective-permute-start | bytes 294920 | tf_op jit(solution)/shard_map/ppermute | solution.py:48
  17.4 1.7 %collective-permute-done.22.refs_1_ = bf16[64,768]{1,0:T(8,128)(2,1)S(1)} collective-permute-done((bf16[64,768]{1,0:T(8,128)(2,1)S(1)}, bf16[64,768]{1,0:T(8,128)(2,1)S(1)}, u32[]{:S(2)}, u32[]{:S(2)}) %collective-permute-start.22) | collective-permute-done | bytes 98336 | tf_op jit(solution)/shard_map/ppermute | solution.py:48
  19.1 0.5 collective-permute-start.7
  19.6 3.0 %collective-permute-done.16.refs_1_ = bf16[64,768]{1,0:T(8,128)(2,1)S(1)} collective-permute-done((bf16[64,768]{1,0:T(8,128)(2,1)S(1)}, bf16[64,768]{1,0:T(8,128)(2,1)S(1)}, u32[]{:S(2)}, u32[]{:S(2)}) %collective-permute-start.16) | collective-permute-done | bytes 98336 | tf_op jit(solution)/shard_map/ppermute | solution.py:48
  22.6 0.5 collective-permute-start.8
  23.2 0.7 collective-permute-done.17.refs_2_
  23.9 0.2 collective-permute-start.15
  24.0 1.1 %collective-permute-start.3 = (bf16[64,768]{1,0:T(8,128)(2,1)S(1)}, bf16[64,768]{1,0:T(8,128)(2,1)S(1)}, u32[]{:S(2)}, u32[]{:S(2)}) collective-permute-start(bf16[64,768]{1,0:T(8,128)(2,1)S(1)} %get-tuple-element.18.refs_0_), channel_id=1, source_target_pairs={{0,2},{1,3},{2,0},{3,1},{4,6},{5,7},{6,4},{7,5},{8,10},{9,11},{10,... | collective-permute-start | bytes 294920 | tf_op jit(solution)/shard_map/ppermute | solution.py:48
  25.2 0.4 collective-permute-start.18
  25.7 0.9 %copy-done.6 = bf16[64,1024]{1,0:T(8,128)(2,1)S(1)} copy-done((bf16[64,1024]{1,0:T(8,128)(2,1)S(1)}, bf16[64,1024]{1,0:T(8,128)(2,1)}, u32[]{:S(2)}) %copy-start.6) | copy-done | bytes 131096
  26.6 2.4 %shard_map.146 = (f32[256,1024]{1,0:T(8,128)S(1)}, bf16[256,256]{1,0:T(8,128)(2,1)S(1)}) custom-call(f32[3,1024]{1,0:T(4,128)S(1)} %copy-done.8, bf16[768,1024]{1,0:T(8,128)(2,1)S(1)} %copy-done.1, bf16[3,1024,256]{2,1,0:T(8,128)(2,1)S(1)} %copy-done.2, bf16[64,768]{1,0:T(8,128)(2,1)S(1)} %get-tuple-element.25.refs_0_, ...), custom_call_target="tpu_custom_call" | custom-call | tf_op jit(solution)/shard_map/pallas_call | solution.py:282
  29.0 0.1 collective-permute-done.3.refs_1_
  29.1 1.1 %collective-permute-start.25 = (bf16[256,256]{1,0:T(8,128)(2,1)S(1)}, bf16[256,256]{1,0:T(8,128)(2,1)S(1)}, u32[]{:S(2)}, u32[]{:S(2)}) collective-permute-start(bf16[256,256]{1,0:T(8,128)(2,1)S(1)} %get-tuple-element.27.refs_0_), channel_id=1, source_target_pairs={{0,2},{1,3},{2,0},{3,1},{4,6},{5,7},{6,4},{7,5},{8,10},{9,11},{10,... | collective-permute-start | bytes 393224 | tf_op jit(solution)/shard_map/ppermute | solution.py:48
  30.2 0.5 collective-permute-start.5
  30.7 2.4 %shard_map.144 = (f32[256,1024]{1,0:T(8,128)S(1)}, bf16[256,256]{1,0:T(8,128)(2,1)S(1)}) custom-call(f32[3,1024]{1,0:T(4,128)S(1)} %copy-done.8, bf16[768,1024]{1,0:T(8,128)(2,1)S(1)} %copy-done.1, bf16[3,1024,256]{2,1,0:T(8,128)(2,1)S(1)} %copy-done.2, bf16[64,768]{1,0:T(8,128)(2,1)S(1)} %get-tuple-element.22.refs_0_, ...), custom_call_target="tpu_custom_call" | custom-call | tf_op jit(solution)/shard_map/pallas_call | solution.py:282
  33.1 1.0 %collective-permute-start.19 = (bf16[256,256]{1,0:T(8,128)(2,1)S(1)}, bf16[256,256]{1,0:T(8,128)(2,1)S(1)}, u32[]{:S(2)}, u32[]{:S(2)}) collective-permute-start(bf16[256,256]{1,0:T(8,128)(2,1)S(1)} %get-tuple-element.24.refs_0_), channel_id=1, source_target_pairs={{0,2},{1,3},{2,0},{3,1},{4,6},{5,7},{6,4},{7,5},{8,10},{9,11},{10,... | collective-permute-start | bytes 393224 | tf_op jit(solution)/shard_map/ppermute | solution.py:48
  34.1 2.4 %shard_map.142 = (f32[256,1024]{1,0:T(8,128)S(1)}, bf16[256,256]{1,0:T(8,128)(2,1)S(1)}) custom-call(f32[3,1024]{1,0:T(4,128)S(1)} %copy-done.8, bf16[768,1024]{1,0:T(8,128)(2,1)S(1)} %copy-done.1, bf16[3,1024,256]{2,1,0:T(8,128)(2,1)S(1)} %copy-done.2, bf16[64,768]{1,0:T(8,128)(2,1)S(1)} %get-tuple-element.18.refs_0_, ...), custom_call_target="tpu_custom_call" | custom-call | tf_op jit(solution)/shard_map/pallas_call | solution.py:282
  36.5 1.2 %collective-permute-start.9 = (bf16[256,256]{1,0:T(8,128)(2,1)S(1)}, bf16[256,256]{1,0:T(8,128)(2,1)S(1)}, u32[]{:S(2)}, u32[]{:S(2)}) collective-permute-start(bf16[256,256]{1,0:T(8,128)(2,1)S(1)} %get-tuple-element.20.refs_0_), channel_id=1, source_target_pairs={{0,2},{1,3},{2,0},{3,1},{4,6},{5,7},{6,4},{7,5},{8,10},{9,11},{10,... | collective-permute-start | bytes 393224 | tf_op jit(solution)/shard_map/ppermute | solution.py:48
  37.7 1.0 %collective-permute-done.19.refs_1_ = bf16[256,256]{1,0:T(8,128)(2,1)S(1)} collective-permute-done((bf16[256,256]{1,0:T(8,128)(2,1)S(1)}, bf16[256,256]{1,0:T(8,128)(2,1)S(1)}, u32[]{:S(2)}, u32[]{:S(2)}) %collective-permute-start.19) | collective-permute-done | bytes 131104 | tf_op jit(solution)/shard_map/ppermute | solution.py:48
  38.7 3.1 %collective-permute-done.9.refs_1_ = bf16[256,256]{1,0:T(8,128)(2,1)S(1)} collective-permute-done((bf16[256,256]{1,0:T(8,128)(2,1)S(1)}, bf16[256,256]{1,0:T(8,128)(2,1)S(1)}, u32[]{:S(2)}, u32[]{:S(2)}) %collective-permute-start.9) | collective-permute-done | bytes 131104 | tf_op jit(solution)/shard_map/ppermute | solution.py:48
  41.8 0.5 collective-permute-start.10
  42.4 2.0 %shard_map.147.refs_2_ = f32[2,1024]{1,0:T(2,128)S(1)} custom-call(f32[3,1024]{1,0:T(4,128)S(1)} %copy-done.8, bf16[1024,1024]{1,0:T(8,128)(2,1)S(1)} %copy-done, f32[256,1024]{1,0:T(8,128)S(1)} %get-tuple-element.26.hidden_ref, bf16[256,256]{1,0:T(8,128)(2,1)S(1)} %get-tuple-element.27.refs_0_, bf16[256,256]{1,0:T(8,128)(2,1)S(1)} %collective-permute-done.25.refs_1_, ...), custom_call_target="tpu_custom_call" | custom-call | tf_op jit(solution)/shard_map/pallas_call | solution.py:313
  44.3 2.0 %shard_map.145.refs_1_ = f32[2,1024]{1,0:T(2,128)S(1)} custom-call(f32[3,1024]{1,0:T(4,128)S(1)} %copy-done.8, bf16[1024,1024]{1,0:T(8,128)(2,1)S(1)} %copy-done, f32[256,1024]{1,0:T(8,128)S(1)} %get-tuple-element.23.hidden_ref, bf16[256,256]{1,0:T(8,128)(2,1)S(1)} %get-tuple-element.24.refs_0_, bf16[256,256]{1,0:T(8,128)(2,1)S(1)} %collective-permute-done.19.refs_1_, ...), custom_call_target="tpu_custom_call" | custom-call | tf_op jit(solution)/shard_map/pallas_call | solution.py:313
  46.3 2.0 %shard_map.143.refs_0_ = f32[2,1024]{1,0:T(2,128)S(1)} custom-call(f32[3,1024]{1,0:T(4,128)S(1)} %copy-done.8, bf16[1024,1024]{1,0:T(8,128)(2,1)S(1)} %copy-done, f32[256,1024]{1,0:T(8,128)S(1)} %get-tuple-element.19.hidden_ref, bf16[256,256]{1,0:T(8,128)(2,1)S(1)} %get-tuple-element.20.refs_0_, bf16[256,256]{1,0:T(8,128)(2,1)S(1)} %collective-permute-done.9.refs_1_, ...), custom_call_target="tpu_custom_call" | custom-call | tf_op jit(solution)/shard_map/pallas_call | solution.py:313
  48.4 0.4 reduce.1.own_ref
  48.7 0.5 collective-permute-start.28
  49.2 0.8 %collective-permute-done.28.other_ref = f32[3,1024]{1,0:T(4,128)S(1)} collective-permute-done((f32[3,1024]{1,0:T(4,128)S(1)}, f32[3,1024]{1,0:T(4,128)S(1)}, u32[]{:S(2)}, u32[]{:S(2)}) %collective-permute-start.28) | collective-permute-done | bytes 12320 | tf_op jit(solution)/shard_map/ppermute | solution.py:48
  50.1 1.1 %collective-permute-start.29 = (f32[3,1024]{1,0:T(4,128)S(1)}, f32[3,1024]{1,0:T(4,128)S(1)}, u32[]{:S(2)}, u32[]{:S(2)}) collective-permute-start(f32[3,1024]{1,0:T(4,128)S(1)} %add.2.own_ref), channel_id=1, source_target_pairs={{0,2},{1,3},{2,0},{3,1},{4,6},{5,7},{6,4},{7,5},{8,10},{9,11},{10,... | collective-permute-start | bytes 36872 | tf_op jit(solution)/shard_map/ppermute | solution.py:48
  51.2 2.6 %collective-permute-done.29.other_ref = f32[3,1024]{1,0:T(4,128)S(1)} collective-permute-done((f32[3,1024]{1,0:T(4,128)S(1)}, f32[3,1024]{1,0:T(4,128)S(1)}, u32[]{:S(2)}, u32[]{:S(2)}) %collective-permute-start.29) | collective-permute-done | bytes 12320 | tf_op jit(solution)/shard_map/ppermute | solution.py:48
  53.8 0.5 collective-permute-start.30
  54.3 3.2 %collective-permute-done.30.other_ref = f32[1,3,1024]{2,1,0:T(4,128)S(1)} collective-permute-done((f32[1,3,1024]{2,1,0:T(4,128)S(1)}, f32[1,3,1024]{2,1,0:T(4,128)S(1)}, u32[]{:S(2)}, u32[]{:S(2)}) %collective-permute-start.30) | collective-permute-done | bytes 12320 | tf_op jit(solution)/shard_map/ppermute | solution.py:48
  57.6 1.5 %collective-permute-start.31 = (f32[2,3,1024]{2,1,0:T(4,128)S(1)}, f32[2,3,1024]{2,1,0:T(4,128)S(1)}, u32[]{:S(2)}, u32[]{:S(2)}) collective-permute-start(f32[2,3,1024]{2,1,0:T(4,128)S(1)} %shard_map.148.own_ref), channel_id=1, source_target_pairs={{0,8},{4,12},{8,0},{12,4},{16,24},{20,28},{24,16},{28,20},{1,9},{5... | collective-permute-start | bytes 73736 | tf_op jit(solution)/shard_map/ppermute | solution.py:48
  59.1 2.4 %collective-permute-done.31.other_ref = f32[2,3,1024]{2,1,0:T(4,128)S(1)} collective-permute-done((f32[2,3,1024]{2,1,0:T(4,128)S(1)}, f32[2,3,1024]{2,1,0:T(4,128)S(1)}, u32[]{:S(2)}, u32[]{:S(2)}) %collective-permute-start.31) | collective-permute-done | bytes 24608 | tf_op jit(solution)/shard_map/ppermute | solution.py:48
  61.5 2.9 %collective-permute-start.32 = (f32[4,3,1024]{2,1,0:T(4,128)S(1)}, f32[4,3,1024]{2,1,0:T(4,128)S(1)}, u32[]{:S(2)}, u32[]{:S(2)}) collective-permute-start(f32[4,3,1024]{2,1,0:T(4,128)S(1)} %shard_map.149.first_ref), channel_id=1, source_target_pairs={{0,16},{4,20},{8,24},{12,28},{16,0},{20,4},{24,8},{28,12},{1,17},{... | collective-permute-start | bytes 147464 | tf_op jit(solution)/shard_map/ppermute | solution.py:48
  64.4 0.5 collective-permute-start
  64.9 3.2 %collective-permute-done.other_ref = bf16[1,3,1152]{2,1,0:T(4,128)(2,1)S(1)} collective-permute-done((bf16[1,3,1152]{2,1,0:T(4,128)(2,1)S(1)}, bf16[1,3,1152]{2,1,0:T(4,128)(2,1)S(1)}, u32[]{:S(2)}, u32[]{:S(2)}) %collective-permute-start) | collective-permute-done | bytes 6944 | tf_op jit(solution)/shard_map/ppermute | solution.py:48
  68.1 1.2 %collective-permute-start.1 = (bf16[2,3,1152]{2,1,0:T(4,128)(2,1)S(1)}, bf16[2,3,1152]{2,1,0:T(4,128)(2,1)S(1)}, u32[]{:S(2)}, u32[]{:S(2)}) collective-permute-start(bf16[2,3,1152]{2,1,0:T(4,128)(2,1)S(1)} %shard_map.140.own_ref), channel_id=1, source_target_pairs={{0,8},{4,12},{8,0},{12,4},{16,24},{20,28},{24,16},{28,20},{1,9},{5... | collective-permute-start | bytes 41480 | tf_op jit(solution)/shard_map/ppermute | solution.py:48
  69.3 2.5 %collective-permute-done.1.other_ref = bf16[2,3,1152]{2,1,0:T(4,128)(2,1)S(1)} collective-permute-done((bf16[2,3,1152]{2,1,0:T(4,128)(2,1)S(1)}, bf16[2,3,1152]{2,1,0:T(4,128)(2,1)S(1)}, u32[]{:S(2)}, u32[]{:S(2)}) %collective-permute-start.1) | collective-permute-done | bytes 13856 | tf_op jit(solution)/shard_map/ppermute | solution.py:48
  71.8 0.1 collective-permute-start.2
  72.0 4.8 %collective-permute-done.2.second_ref = bf16[4,3,1152]{2,1,0:T(4,128)(2,1)S(1)} collective-permute-done((bf16[4,3,1152]{2,1,0:T(4,128)(2,1)S(1)}, bf16[4,3,1152]{2,1,0:T(4,128)(2,1)S(1)}, u32[]{:S(2)}, u32[]{:S(2)}) %collective-permute-start.2) | collective-permute-done | bytes 27680 | tf_op jit(solution)/shard_map/ppermute | solution.py:48
  76.8 0.2 route.1
  77.0 2.2 %finish.1 = (f32[4,1024]{1,0:T(4,128)}, f32[4]{0:T(128)}) custom-call(f32[2]{0:T(128)S(1)} %copy-done.9, f32[3,1024]{1,0:T(4,128)S(1)} %copy-done.8, bf16[1024,1024]{1,0:T(8,128)(2,1)S(1)} %copy-done.4, f32[24,1024]{1,0:T(8,128)S(1)} %get-tuple-element.16.cap_ref, f32[24,128]{1,0:T(8,128)S(1)} %get-tuple-element.17.meta_ref, ...), custom_call_target="tpu_custom_call" | custom-call | tf_op jit(solution)/shard_map/finish/pallas_call | solution.py:379
  (55 shorter events, 0.4 us)
Async XLA Ops:
  0.6 25.0 %copy-start.1 = (bf16[768,1024]{1,0:T(8,128)(2,1)S(1)}, bf16[768,1024]{1,0:T(8,128)(2,1)}, u32[]{:S(2)}) copy-start(bf16[768,1024]{1,0:T(8,128)(2,1)} %patch_ref.5) | copy-start | bytes 4718596
  0.6 25.0 %copy-start.2 = (bf16[3,1024,256]{2,1,0:T(8,128)(2,1)S(1)}, bf16[3,1024,256]{2,1,0:T(8,128)(2,1)}, u32[]{:S(2)}) copy-start(bf16[3,1024,256]{2,1,0:T(8,128)(2,1)} %qkv_ref.5) | copy-start | bytes 4718596
  0.7 25.0 %copy-start.8 = (f32[3,1024]{1,0:T(4,128)S(1)}, f32[3,1024]{1,0:T(4,128)}, u32[]{:S(2)}) copy-start(f32[3,1024]{1,0:T(4,128)} %gains_ref.13) | copy-start | bytes 36868
  2.8 9.3 %collective-permute-start.12 = (bf16[128,1024]{1,0:T(8,128)(2,1)S(1)}, bf16[128,1024]{1,0:T(8,128)(2,1)S(1)}, u32[]{:S(2)}, u32[]{:S(2)}) collective-permute-start(bf16[128,1024]{1,0:T(8,128)(2,1)S(1)} %get-tuple-element.21), channel_id=1, source_target_pairs={{0,2},{1,3},{2,0},{3,1},{4,6},{5,7},{6,4},{7,5},{8,10},{9,11},{10,... | collective-permute-start | bytes 786440 | tf_op jit(solution)/shard_map/ppermute | solution.py:48
  12.1 11.0 %collective-permute-start.13 = (bf16[128,1024]{1,0:T(8,128)(2,1)S(1)}, bf16[128,1024]{1,0:T(8,128)(2,1)S(1)}, u32[]{:S(2)}, u32[]{:S(2)}) collective-permute-start(bf16[128,1024]{1,0:T(8,128)(2,1)S(1)} %collective-permute-done.12.refs_0_), channel_id=1, source_target_pairs={{0,4},{4,0},{8,12},{12,8},{16,20},{20,16},{24,28},{28,24},{1,5},{5... | collective-permute-start | bytes 786440 | tf_op jit(solution)/shard_map/ppermute | solution.py:48
  13.9 5.2 %collective-permute-start.22 = (bf16[64,768]{1,0:T(8,128)(2,1)S(1)}, bf16[64,768]{1,0:T(8,128)(2,1)S(1)}, u32[]{:S(2)}, u32[]{:S(2)}) collective-permute-start(bf16[64,768]{1,0:T(8,128)(2,1)S(1)} %get-tuple-element.25.refs_0_), channel_id=1, source_target_pairs={{0,2},{1,3},{2,0},{3,1},{4,6},{5,7},{6,4},{7,5},{8,10},{9,11},{10,... | collective-permute-start | bytes 294920 | tf_op jit(solution)/shard_map/ppermute | solution.py:48
  15.4 7.2 %collective-permute-start.6 = (bf16[64,1024]{1,0:T(8,128)(2,1)}, bf16[64,1024]{1,0:T(8,128)(2,1)S(1)}, u32[]{:S(2)}, u32[]{:S(2)}) collective-permute-start(bf16[64,1024]{1,0:T(8,128)(2,1)} %refs_4_.10), channel_id=1, source_target_pairs={{0,2},{1,3},{2,0},{3,1},{4,6},{5,7},{6,4},{7,5},{8,10},{9,11},{10,... | collective-permute-start | bytes 393224 | tf_op jit(solution)/shard_map/ppermute | solution.py:48
  15.9 3.2 %collective-permute-start.23 = (bf16[64,768]{1,0:T(8,128)(2,1)S(1)}, bf16[64,768]{1,0:T(8,128)(2,1)S(1)}, u32[]{:S(2)}, u32[]{:S(2)}) collective-permute-start(bf16[64,768]{1,0:T(8,128)(2,1)S(1)} %get-tuple-element.25.refs_0_), channel_id=1, source_target_pairs={{0,1},{1,0},{2,3},{3,2},{4,5},{5,4},{6,7},{7,6},{8,9},{9,8},{10,11... | collective-permute-start | bytes 294920 | tf_op jit(solution)/shard_map/ppermute | solution.py:48
  15.9 6.7 %collective-permute-start.16 = (bf16[64,768]{1,0:T(8,128)(2,1)S(1)}, bf16[64,768]{1,0:T(8,128)(2,1)S(1)}, u32[]{:S(2)}, u32[]{:S(2)}) collective-permute-start(bf16[64,768]{1,0:T(8,128)(2,1)S(1)} %get-tuple-element.22.refs_0_), channel_id=1, source_target_pairs={{0,2},{1,3},{2,0},{3,1},{4,6},{5,7},{6,4},{7,5},{8,10},{9,11},{10,... | collective-permute-start | bytes 294920 | tf_op jit(solution)/shard_map/ppermute | solution.py:48
  19.1 23.2 %collective-permute-start.14 = (bf16[256,1024]{1,0:T(8,128)(2,1)}, bf16[256,1024]{1,0:T(8,128)(2,1)S(1)}, u32[]{:S(2)}, u32[]{:S(2)}) collective-permute-start(bf16[256,1024]{1,0:T(8,128)(2,1)} %refs_4_.11), channel_id=1, source_target_pairs={{0,1},{1,0},{2,3},{3,2},{4,5},{5,4},{6,7},{7,6},{8,9},{9,8},{10,11... | collective-permute-start | bytes 1572872 | tf_op jit(solution)/shard_map/ppermute | solution.py:48
  19.1 4.9 %collective-permute-start.7 = (bf16[64,1024]{1,0:T(8,128)(2,1)}, bf16[64,1024]{1,0:T(8,128)(2,1)S(1)}, u32[]{:S(2)}, u32[]{:S(2)}) collective-permute-start(bf16[64,1024]{1,0:T(8,128)(2,1)} %refs_4_.10), channel_id=1, source_target_pairs={{0,1},{1,0},{2,3},{3,2},{4,5},{5,4},{6,7},{7,6},{8,9},{9,8},{10,11... | collective-permute-start | bytes 393224 | tf_op jit(solution)/shard_map/ppermute | solution.py:48
  22.6 1.3 %collective-permute-start.17 = (bf16[64,768]{1,0:T(8,128)(2,1)S(1)}, bf16[64,768]{1,0:T(8,128)(2,1)S(1)}, u32[]{:S(2)}, u32[]{:S(2)}) collective-permute-start(bf16[64,768]{1,0:T(8,128)(2,1)S(1)} %get-tuple-element.22.refs_0_), channel_id=1, source_target_pairs={{0,1},{1,0},{2,3},{3,2},{4,5},{5,4},{6,7},{7,6},{8,9},{9,8},{10,11... | collective-permute-start | bytes 294920 | tf_op jit(solution)/shard_map/ppermute | solution.py:48
  22.6 2.7 %collective-permute-start.8 = (bf16[64,1024]{1,0:T(8,128)(2,1)S(1)}, bf16[64,1024]{1,0:T(8,128)(2,1)S(1)}, u32[]{:S(2)}, u32[]{:S(2)}) collective-permute-start(bf16[64,1024]{1,0:T(8,128)(2,1)S(1)} %collective-permute-done.6.refs_5_), channel_id=1, source_target_pairs={{0,1},{1,0},{2,3},{3,2},{4,5},{5,4},{6,7},{7,6},{8,9},{9,8},{10,11... | collective-permute-start | bytes 393224 | tf_op jit(solution)/shard_map/ppermute | solution.py:48
  23.1 2.1 %collective-permute-start.24 = (bf16[64,768]{1,0:T(8,128)(2,1)S(1)}, bf16[64,768]{1,0:T(8,128)(2,1)S(1)}, u32[]{:S(2)}, u32[]{:S(2)}) collective-permute-start(bf16[64,768]{1,0:T(8,128)(2,1)S(1)} %collective-permute-done.22.refs_1_), channel_id=1, source_target_pairs={{0,1},{1,0},{2,3},{3,2},{4,5},{5,4},{6,7},{7,6},{8,9},{9,8},{10,11... | collective-permute-start | bytes 294920 | tf_op jit(solution)/shard_map/ppermute | solution.py:48
  23.9 18.5 %collective-permute-start.15 = (bf16[256,1024]{1,0:T(8,128)(2,1)S(1)}, bf16[256,1024]{1,0:T(8,128)(2,1)S(1)}, u32[]{:S(2)}, u32[]{:S(2)}) collective-permute-start(bf16[256,1024]{1,0:T(8,128)(2,1)S(1)} %assemble.1.refs_5_), channel_id=1, source_target_pairs={{0,1},{1,0},{2,3},{3,2},{4,5},{5,4},{6,7},{7,6},{8,9},{9,8},{10,11... | collective-permute-start | bytes 1572872 | tf_op jit(solution)/shard_map/ppermute | solution.py:48
  24.0 5.1 %collective-permute-start.3 = (bf16[64,768]{1,0:T(8,128)(2,1)S(1)}, bf16[64,768]{1,0:T(8,128)(2,1)S(1)}, u32[]{:S(2)}, u32[]{:S(2)}) collective-permute-start(bf16[64,768]{1,0:T(8,128)(2,1)S(1)} %get-tuple-element.18.refs_0_), channel_id=1, source_target_pairs={{0,2},{1,3},{2,0},{3,1},{4,6},{5,7},{6,4},{7,5},{8,10},{9,11},{10,... | collective-permute-start | bytes 294920 | tf_op jit(solution)/shard_map/ppermute | solution.py:48
  25.1 5.1 %collective-permute-start.4 = (bf16[64,768]{1,0:T(8,128)(2,1)S(1)}, bf16[64,768]{1,0:T(8,128)(2,1)S(1)}, u32[]{:S(2)}, u32[]{:S(2)}) collective-permute-start(bf16[64,768]{1,0:T(8,128)(2,1)S(1)} %get-tuple-element.18.refs_0_), channel_id=1, source_target_pairs={{0,1},{1,0},{2,3},{3,2},{4,5},{5,4},{6,7},{7,6},{8,9},{9,8},{10,11... | collective-permute-start | bytes 294920 | tf_op jit(solution)/shard_map/ppermute | solution.py:48
  25.2 5.0 %collective-permute-start.18 = (bf16[64,768]{1,0:T(8,128)(2,1)S(1)}, bf16[64,768]{1,0:T(8,128)(2,1)S(1)}, u32[]{:S(2)}, u32[]{:S(2)}) collective-permute-start(bf16[64,768]{1,0:T(8,128)(2,1)S(1)} %collective-permute-done.16.refs_1_), channel_id=1, source_target_pairs={{0,1},{1,0},{2,3},{3,2},{4,5},{5,4},{6,7},{7,6},{8,9},{9,8},{10,11... | collective-permute-start | bytes 294920 | tf_op jit(solution)/shard_map/ppermute | solution.py:48
  25.7 0.9 %copy-start.6 = (bf16[64,1024]{1,0:T(8,128)(2,1)S(1)}, bf16[64,1024]{1,0:T(8,128)(2,1)}, u32[]{:S(2)}) copy-start(bf16[64,1024]{1,0:T(8,128)(2,1)} %refs_4_.10) | copy-start | bytes 393220
  29.0 5.1 %copy-start.7 = (bf16[64,1024]{1,0:T(8,128)(2,1)S(1)}, bf16[64,1024]{1,0:T(8,128)(2,1)}, u32[]{:S(2)}) copy-start(bf16[64,1024]{1,0:T(8,128)(2,1)} %refs_4_.10) | copy-start | bytes 393220
  29.1 7.4 %collective-permute-start.25 = (bf16[256,256]{1,0:T(8,128)(2,1)S(1)}, bf16[256,256]{1,0:T(8,128)(2,1)S(1)}, u32[]{:S(2)}, u32[]{:S(2)}) collective-permute-start(bf16[256,256]{1,0:T(8,128)(2,1)S(1)} %get-tuple-element.27.refs_0_), channel_id=1, source_target_pairs={{0,2},{1,3},{2,0},{3,1},{4,6},{5,7},{6,4},{7,5},{8,10},{9,11},{10,... | collective-permute-start | bytes 393224 | tf_op jit(solution)/shard_map/ppermute | solution.py:48
  30.2 7.5 %collective-permute-start.26 = (bf16[256,256]{1,0:T(8,128)(2,1)S(1)}, bf16[256,256]{1,0:T(8,128)(2,1)S(1)}, u32[]{:S(2)}, u32[]{:S(2)}) collective-permute-start(bf16[256,256]{1,0:T(8,128)(2,1)S(1)} %get-tuple-element.27.refs_0_), channel_id=1, source_target_pairs={{0,1},{1,0},{2,3},{3,2},{4,5},{5,4},{6,7},{7,6},{8,9},{9,8},{10,11... | collective-permute-start | bytes 393224 | tf_op jit(solution)/shard_map/ppermute | solution.py:48
  30.2 2.9 %collective-permute-start.5 = (bf16[64,768]{1,0:T(8,128)(2,1)S(1)}, bf16[64,768]{1,0:T(8,128)(2,1)S(1)}, u32[]{:S(2)}, u32[]{:S(2)}) collective-permute-start(bf16[64,768]{1,0:T(8,128)(2,1)S(1)} %collective-permute-done.3.refs_1_), channel_id=1, source_target_pairs={{0,1},{1,0},{2,3},{3,2},{4,5},{5,4},{6,7},{7,6},{8,9},{9,8},{10,11... | collective-permute-start | bytes 294920 | tf_op jit(solution)/shard_map/ppermute | solution.py:48
  33.1 9.2 %copy-start = (bf16[1024,1024]{1,0:T(8,128)(2,1)S(1)}, bf16[1024,1024]{1,0:T(8,128)(2,1)}, u32[]{:S(2)}) copy-start(bf16[1024,1024]{1,0:T(8,128)(2,1)} %up_ref.5) | copy-start | bytes 6291460
  33.1 9.2 %copy-start.3 = (bf16[256,1024]{1,0:T(8,128)(2,1)S(1)}, bf16[256,1024]{1,0:T(8,128)(2,1)}, u32[]{:S(2)}) copy-start(bf16[256,1024]{1,0:T(8,128)(2,1)} %refs_4_.11) | copy-start | bytes 1572868
  33.1 5.5 %collective-permute-start.19 = (bf16[256,256]{1,0:T(8,128)(2,1)S(1)}, bf16[256,256]{1,0:T(8,128)(2,1)S(1)}, u32[]{:S(2)}, u32[]{:S(2)}) collective-permute-start(bf16[256,256]{1,0:T(8,128)(2,1)S(1)} %get-tuple-element.24.refs_0_), channel_id=1, source_target_pairs={{0,2},{1,3},{2,0},{3,1},{4,6},{5,7},{6,4},{7,5},{8,10},{9,11},{10,... | collective-permute-start | bytes 393224 | tf_op jit(solution)/shard_map/ppermute | solution.py:48
  36.5 5.2 %collective-permute-start.9 = (bf16[256,256]{1,0:T(8,128)(2,1)S(1)}, bf16[256,256]{1,0:T(8,128)(2,1)S(1)}, u32[]{:S(2)}, u32[]{:S(2)}) collective-permute-start(bf16[256,256]{1,0:T(8,128)(2,1)S(1)} %get-tuple-element.20.refs_0_), channel_id=1, source_target_pairs={{0,2},{1,3},{2,0},{3,1},{4,6},{5,7},{6,4},{7,5},{8,10},{9,11},{10,... | collective-permute-start | bytes 393224 | tf_op jit(solution)/shard_map/ppermute | solution.py:48
  37.7 4.1 %collective-permute-start.27 = (bf16[256,256]{1,0:T(8,128)(2,1)S(1)}, bf16[256,256]{1,0:T(8,128)(2,1)S(1)}, u32[]{:S(2)}, u32[]{:S(2)}) collective-permute-start(bf16[256,256]{1,0:T(8,128)(2,1)S(1)} %collective-permute-done.25.refs_1_), channel_id=1, source_target_pairs={{0,1},{1,0},{2,3},{3,2},{4,5},{5,4},{6,7},{7,6},{8,9},{9,8},{10,11... | collective-permute-start | bytes 393224 | tf_op jit(solution)/shard_map/ppermute | solution.py:48
  38.7 5.7 %collective-permute-start.20 = (bf16[256,256]{1,0:T(8,128)(2,1)S(1)}, bf16[256,256]{1,0:T(8,128)(2,1)S(1)}, u32[]{:S(2)}, u32[]{:S(2)}) collective-permute-start(bf16[256,256]{1,0:T(8,128)(2,1)S(1)} %get-tuple-element.24.refs_0_), channel_id=1, source_target_pairs={{0,1},{1,0},{2,3},{3,2},{4,5},{5,4},{6,7},{7,6},{8,9},{9,8},{10,11... | collective-permute-start | bytes 393224 | tf_op jit(solution)/shard_map/ppermute | solution.py:48
  41.8 2.6 %collective-permute-start.21 = (bf16[256,256]{1,0:T(8,128)(2,1)S(1)}, bf16[256,256]{1,0:T(8,128)(2,1)S(1)}, u32[]{:S(2)}, u32[]{:S(2)}) collective-permute-start(bf16[256,256]{1,0:T(8,128)(2,1)S(1)} %collective-permute-done.19.refs_1_), channel_id=1, source_target_pairs={{0,1},{1,0},{2,3},{3,2},{4,5},{5,4},{6,7},{7,6},{8,9},{9,8},{10,11... | collective-permute-start | bytes 393224 | tf_op jit(solution)/shard_map/ppermute | solution.py:48
  41.8 4.6 %collective-permute-start.10 = (bf16[256,256]{1,0:T(8,128)(2,1)S(1)}, bf16[256,256]{1,0:T(8,128)(2,1)S(1)}, u32[]{:S(2)}, u32[]{:S(2)}) collective-permute-start(bf16[256,256]{1,0:T(8,128)(2,1)S(1)} %get-tuple-element.20.refs_0_), channel_id=1, source_target_pairs={{0,1},{1,0},{2,3},{3,2},{4,5},{5,4},{6,7},{7,6},{8,9},{9,8},{10,11... | collective-permute-start | bytes 393224 | tf_op jit(solution)/shard_map/ppermute | solution.py:48
  42.3 4.1 %collective-permute-start.11 = (bf16[256,256]{1,0:T(8,128)(2,1)S(1)}, bf16[256,256]{1,0:T(8,128)(2,1)S(1)}, u32[]{:S(2)}, u32[]{:S(2)}) collective-permute-start(bf16[256,256]{1,0:T(8,128)(2,1)S(1)} %collective-permute-done.9.refs_1_), channel_id=1, source_target_pairs={{0,1},{1,0},{2,3},{3,2},{4,5},{5,4},{6,7},{7,6},{8,9},{9,8},{10,11... | collective-permute-start | bytes 393224 | tf_op jit(solution)/shard_map/ppermute | solution.py:48
  46.3 2.0 %copy-start.5 = (bf16[1024,1024]{1,0:T(8,128)(2,1)S(1)}, bf16[1024,1024]{1,0:T(8,128)(2,1)}, u32[]{:S(2)}) copy-start(bf16[1024,1024]{1,0:T(8,128)(2,1)} %down_ref.1) | copy-start | bytes 6291460
  48.3 28.7 %copy-start.4 = (bf16[1024,1024]{1,0:T(8,128)(2,1)S(1)}, bf16[1024,1024]{1,0:T(8,128)(2,1)}, u32[]{:S(2)}) copy-start(bf16[1024,1024]{1,0:T(8,128)(2,1)} %weight_ref.1) | copy-start | bytes 6291460
  48.3 28.7 %copy-start.9 = (f32[2]{0:T(128)S(1)}, f32[2]{0:T(128)}, u32[]{:S(2)}) copy-start(f32[2]{0:T(128)} %params_ref.1) | copy-start | bytes 28
  48.7 1.3 %collective-permute-start.28 = (f32[3,1024]{1,0:T(4,128)S(1)}, f32[3,1024]{1,0:T(4,128)S(1)}, u32[]{:S(2)}, u32[]{:S(2)}) collective-permute-start(f32[3,1024]{1,0:T(4,128)S(1)} %reduce.1.own_ref), channel_id=1, source_target_pairs={{0,1},{1,0},{2,3},{3,2},{4,5},{5,4},{6,7},{7,6},{8,9},{9,8},{10,11... | collective-permute-start | bytes 36872 | tf_op jit(solution)/shard_map/ppermute | solution.py:48
  50.1 3.7 %collective-permute-start.29 = (f32[3,1024]{1,0:T(4,128)S(1)}, f32[3,1024]{1,0:T(4,128)S(1)}, u32[]{:S(2)}, u32[]{:S(2)}) collective-permute-start(f32[3,1024]{1,0:T(4,128)S(1)} %add.2.own_ref), channel_id=1, source_target_pairs={{0,2},{1,3},{2,0},{3,1},{4,6},{5,7},{6,4},{7,5},{8,10},{9,11},{10,... | collective-permute-start | bytes 36872 | tf_op jit(solution)/shard_map/ppermute | solution.py:48
  53.8 3.7 %collective-permute-start.30 = (f32[1,3,1024]{2,1,0:T(4,128)S(1)}, f32[1,3,1024]{2,1,0:T(4,128)S(1)}, u32[]{:S(2)}, u32[]{:S(2)}) collective-permute-start(f32[1,3,1024]{2,1,0:T(4,128)S(1)} %bitcast.1), channel_id=1, source_target_pairs={{0,4},{4,0},{8,12},{12,8},{16,20},{20,16},{24,28},{28,24},{1,5},{5... | collective-permute-start | bytes 36872 | tf_op jit(solution)/shard_map/ppermute | solution.py:48
  57.6 3.9 %collective-permute-start.31 = (f32[2,3,1024]{2,1,0:T(4,128)S(1)}, f32[2,3,1024]{2,1,0:T(4,128)S(1)}, u32[]{:S(2)}, u32[]{:S(2)}) collective-permute-start(f32[2,3,1024]{2,1,0:T(4,128)S(1)} %shard_map.148.own_ref), channel_id=1, source_target_pairs={{0,8},{4,12},{8,0},{12,4},{16,24},{20,28},{24,16},{28,20},{1,9},{5... | collective-permute-start | bytes 73736 | tf_op jit(solution)/shard_map/ppermute | solution.py:48
  61.5 15.5 %collective-permute-start.32 = (f32[4,3,1024]{2,1,0:T(4,128)S(1)}, f32[4,3,1024]{2,1,0:T(4,128)S(1)}, u32[]{:S(2)}, u32[]{:S(2)}) collective-permute-start(f32[4,3,1024]{2,1,0:T(4,128)S(1)} %shard_map.149.first_ref), channel_id=1, source_target_pairs={{0,16},{4,20},{8,24},{12,28},{16,0},{20,4},{24,8},{28,12},{1,17},{... | collective-permute-start | bytes 147464 | tf_op jit(solution)/shard_map/ppermute | solution.py:48
  64.4 3.7 %collective-permute-start = (bf16[1,3,1152]{2,1,0:T(4,128)(2,1)S(1)}, bf16[1,3,1152]{2,1,0:T(4,128)(2,1)S(1)}, u32[]{:S(2)}, u32[]{:S(2)}) collective-permute-start(bf16[1,3,1152]{2,1,0:T(4,128)(2,1)S(1)} %get-tuple-element.15.own_ref), channel_id=1, source_target_pairs={{0,4},{4,0},{8,12},{12,8},{16,20},{20,16},{24,28},{28,24},{1,5},{5... | collective-permute-start | bytes 20744 | tf_op jit(solution)/shard_map/ppermute | solution.py:48
  68.1 3.8 %collective-permute-start.1 = (bf16[2,3,1152]{2,1,0:T(4,128)(2,1)S(1)}, bf16[2,3,1152]{2,1,0:T(4,128)(2,1)S(1)}, u32[]{:S(2)}, u32[]{:S(2)}) collective-permute-start(bf16[2,3,1152]{2,1,0:T(4,128)(2,1)S(1)} %shard_map.140.own_ref), channel_id=1, source_target_pairs={{0,8},{4,12},{8,0},{12,4},{16,24},{20,28},{24,16},{28,20},{1,9},{5... | collective-permute-start | bytes 41480 | tf_op jit(solution)/shard_map/ppermute | solution.py:48
  71.8 4.9 %collective-permute-start.2 = (bf16[4,3,1152]{2,1,0:T(4,128)(2,1)S(1)}, bf16[4,3,1152]{2,1,0:T(4,128)(2,1)S(1)}, u32[]{:S(2)}, u32[]{:S(2)}) collective-permute-start(bf16[4,3,1152]{2,1,0:T(4,128)(2,1)S(1)} %shard_map.141.first_ref), channel_id=1, source_target_pairs={{0,16},{4,20},{8,24},{12,28},{16,0},{20,4},{24,8},{28,12},{1,17},{... | collective-permute-start | bytes 82952 | tf_op jit(solution)/shard_map/ppermute | solution.py:48

commit v3 on v2

--- a/solution.py
+++ b/solution.py
@@ -109,13 +109,13 @@
     return values, swap(values, axis, bit)
 
 
-def pick_kernel(pieces, sel_hbm, dest_hbm, pixels_ref, cap_hbm, output_ref, *refs):
+def pick_kernel(pieces, sel_hbm, dest_hbm, pixels_ref, cap_hbm, output_ref, pos_hbm, *refs):
     row_refs = refs[:SEND_MOST]
-    meta_ref, piece_ref, sel_ref, dest_ref, cap_ref, sems = refs[SEND_MOST:]
+    meta_ref, piece_ref, pos_ref, sel_ref, dest_ref, cap_ref, sems = refs[SEND_MOST:]
     first = [
         pltpu.make_async_copy(source, target, sems.at[SEND_MOST + 1 + i])
         for i, (source, target) in enumerate(
-            ((sel_hbm, sel_ref), (dest_hbm, dest_ref), (cap_hbm, cap_ref))
+            ((sel_hbm, sel_ref), (dest_hbm, dest_ref), (cap_hbm, cap_ref), (pos_hbm, pos_ref))
         )
     ]
     for copy in first:
@@ -154,36 +154,55 @@
         extra = jnp.where(lane == 0, live, jnp.where(lane == 1, target[r].astype(F32), 0.0))
         meta_ref[0, r : r + 1, :width] = row.astype(BF16)
         meta_ref[0, r : r + 1, width:] = extra.astype(BF16)
-    for copy in copies:
+    for copy in copies + first[3:]:
         copy.wait()
 
 
-def pick(selection, destination, pixels, captions, output_weight, pieces):
+def pick(selection, destination, pixels, captions, output_weight, position, pieces):
     _, length, depth = pixels.shape
     fan, width = output_weight.shape
     hbm = pl.BlockSpec(memory_space=pltpu.MemorySpace.HBM)
-    *rows, caption_meta, piece = pl.pallas_call(
+    *rows, caption_meta, piece, own_position = pl.pallas_call(
         functools.partial(pick_kernel, pieces),
         out_shape=(jax.ShapeDtypeStruct((length, depth), BF16),) * SEND_MOST
         + (
             jax.ShapeDtypeStruct((1, SEND_MOST, captions.shape[1] + META), BF16),
             jax.ShapeDtypeStruct((fan // pieces, width), BF16),
+            jax.ShapeDtypeStruct(position.shape, BF16),
         ),
-        in_specs=[hbm] * 5,
-        out_specs=(vmem(),) * (SEND_MOST + 2),
+        in_specs=[hbm] * 6,
+        out_specs=(vmem(),) * (SEND_MOST + 3),
         scratch_shapes=[
             SMEM(selection.shape, jnp.int32),
             SMEM(destination.shape, jnp.int32),
             VMEM(captions.shape, BF16),
-            pltpu.SemaphoreType.DMA((SEND_MOST + 4,)),
+            pltpu.SemaphoreType.DMA((SEND_MOST + 5,)),
         ],
         name="pick",
         compiler_params=small(2),
     )(*(
         pltpu.with_memory_space_constraint(array, pltpu.MemorySpace.HBM)
-        for array in (selection, destination, pixels, captions, output_weight)
+        for array in (selection, destination, pixels, captions, output_weight, position)
     ))
-    return rows, caption_meta, piece
+    return rows, caption_meta, piece, own_position
+
+
+def load_kernel(source_ref, out_ref, sem):
+    copy = pltpu.make_async_copy(source_ref, out_ref, sem)
+    copy.start()
+    copy.wait()
+
+
+def load(array):
+    return pl.pallas_call(
+        load_kernel,
+        out_shape=jax.ShapeDtypeStruct(array.shape, array.dtype),
+        in_specs=[pl.BlockSpec(memory_space=pltpu.MemorySpace.HBM)],
+        out_specs=vmem(),
+        scratch_shapes=[pltpu.SemaphoreType.DMA],
+        name="load",
+        compiler_params=small(2),
+    )(pltpu.with_memory_space_constraint(array, pltpu.MemorySpace.HBM))
 
 
 def assemble_kernel(*refs):
@@ -408,9 +427,11 @@
     shards = lax.axis_size("mp")
     pieces = count_pieces(devices_dp)
     positions, order = gather_blocks(position, "mp")
-    rows, caption_meta, piece = pick(
-        selection, destination, pixels, caption_vectors, output_weight, pieces
-    )
+    rows, caption_meta, piece, own_position = pick(
+        selection, destination, pixels, caption_vectors, output_weight, position, pieces
+    )
+    positions = [own_position] + positions[1:]
+    query_key_value = load(query_key_value)
     pixel_blocks = [gather_blocks(row, "mp")[0] for row in rows]
 
     parts = [swap(piece, "mp", shards // 2)]

time: 79.3 us -> 79.6 us (level)
  Pallas kernels: 18.1 us -> 19.3 us
  local copies, waits for them, and re-layouts: 0.95 us -> 0.04 us
    pallas_call x0 -> x1, Pallas kernels: none -> 1.42 us  [load(): pl.pallas_call(load_kernel, out_shape=jax.ShapeDtypeStruct(array.shape, a...]
    unnamed x20 -> x16, local copies, waits for them, and re-layouts: 0.95 us -> 0.04 us
  transfers between devices with their start and end apart: 33 -> 33, of which waited for: 14 -> 13; matrix products, arithmetic and copies ran while one was open for 0% -> 0% of each run, Pallas kernels for 14% -> 16%
where the time goes in v3:
time: 79.6 us; the launch traced here: 79.4 us
  waiting for transfers between devices  35.8 us (45%)
  starting transfers between devices  23.5 us (30%)
  Pallas kernels  19.3 us (24%)
  between operations  0.83 us (1%)
    ppermute x33, waiting for transfers between devices, swap(): return lax.ppermute(values, axis, [(i, i ^ bit) for i in range(size)])  35.8 us
    ppermute x33, starting transfers between devices, swap(): return lax.ppermute(values, axis, [(i, i ^ bit) for i in range(size)])  23.5 us
    pallas_call x3, Pallas kernels, attend(): pl.pallas_call(functools.partial(attend_kernel, shards), out_shape=(jax.S...  7.13 us
    pallas_call x3, Pallas kernels, expand(): pl.pallas_call(functools.partial(expand_kernel, tuple(order)), out_shape=...  5.8 us
    pallas_call x1, Pallas kernels, finish(): pl.pallas_call(functools.partial(finish_kernel, total), out_shape=(jax.Sh...  2.15 us
    pallas_call x1, Pallas kernels, pick(): pl.pallas_call(functools.partial(pick_kernel, pieces), out_shape=(jax.Sha...  2.07 us
  transfers between devices with their start and end apart: 33, of which 13 were waited for; matrix products, arithmetic and copies ran while one was open for 0% of the time, Pallas kernels for 16%

profile of v3, /device:TPU:0, one launch (start us, length us, event | category | flops | bytes accessed | tf_op | source)
XLA Modules:
  0.0 79.4 jit_solution(7098511406014795351)
XLA Ops:
  0.7 2.1 %pick.1 = (bf16[64,768]{1,0:T(8,128)(2,1)S(1)}, bf16[64,768]{1,0:T(8,128)(2,1)S(1)}, bf16[64,768]{1,0:T(8,128)(2,1)S(1)}, bf16[1,3,1152]{2,1,0:T(4,128)(2,1)S(1)...) custom-call(s32[16]{0:T(128)} %sel_hbm.1, s32[16]{0:T(128)} %dest_hbm.1, bf16[16,64,768]{2,1,0:T(8,128)(2,1)} %pixels_ref.1, ...), custom_call_target="tpu_custom_call" | custom-call | tf_op jit(solution)/shard_map/pick/pallas_call | solution.py:165
  2.7 3.0 %collective-permute-start.12 = (bf16[128,1024]{1,0:T(8,128)(2,1)S(1)}, bf16[128,1024]{1,0:T(8,128)(2,1)S(1)}, u32[]{:S(2)}, u32[]{:S(2)}) collective-permute-start(bf16[128,1024]{1,0:T(8,128)(2,1)S(1)} %get-tuple-element.23), channel_id=1, source_target_pairs={{0,2},{1,3},{2,0},{3,1},{4,6},{5,7},{6,4},{7,5},{8,10},{9,11},{10,... | collective-permute-start | bytes 786440 | tf_op jit(solution)/shard_map/ppermute | solution.py:48
  5.8 6.3 %collective-permute-done.12.refs_0_ = bf16[128,1024]{1,0:T(8,128)(2,1)S(1)} collective-permute-done((bf16[128,1024]{1,0:T(8,128)(2,1)S(1)}, bf16[128,1024]{1,0:T(8,128)(2,1)S(1)}, u32[]{:S(2)}, u32[]{:S(2)}) %collective-permute-start.12) | collective-permute-done | bytes 262176 | tf_op jit(solution)/shard_map/ppermute | solution.py:48
  12.1 1.8 %collective-permute-start.13 = (bf16[128,1024]{1,0:T(8,128)(2,1)S(1)}, bf16[128,1024]{1,0:T(8,128)(2,1)S(1)}, u32[]{:S(2)}, u32[]{:S(2)}) collective-permute-start(bf16[128,1024]{1,0:T(8,128)(2,1)S(1)} %collective-permute-done.12.refs_0_), channel_id=1, source_target_pairs={{0,4},{4,0},{8,12},{12,8},{16,20},{20,16},{24,28},{28,24},{1,5},{5... | collective-permute-start | bytes 786440 | tf_op jit(solution)/shard_map/ppermute | solution.py:48
  13.8 1.5 %collective-permute-start.22 = (bf16[64,768]{1,0:T(8,128)(2,1)S(1)}, bf16[64,768]{1,0:T(8,128)(2,1)S(1)}, u32[]{:S(2)}, u32[]{:S(2)}) collective-permute-start(bf16[64,768]{1,0:T(8,128)(2,1)S(1)} %get-tuple-element.27.refs_0_), channel_id=1, source_target_pairs={{0,2},{1,3},{2,0},{3,1},{4,6},{5,7},{6,4},{7,5},{8,10},{9,11},{10,... | collective-permute-start | bytes 294920 | tf_op jit(solution)/shard_map/ppermute | solution.py:48
  15.3 0.5 collective-permute-start.6
  15.9 1.5 %collective-permute-start.16 = (bf16[64,768]{1,0:T(8,128)(2,1)S(1)}, bf16[64,768]{1,0:T(8,128)(2,1)S(1)}, u32[]{:S(2)}, u32[]{:S(2)}) collective-permute-start(bf16[64,768]{1,0:T(8,128)(2,1)S(1)} %get-tuple-element.24.refs_0_), channel_id=1, source_target_pairs={{0,2},{1,3},{2,0},{3,1},{4,6},{5,7},{6,4},{7,5},{8,10},{9,11},{10,... | collective-permute-start | bytes 294920 | tf_op jit(solution)/shard_map/ppermute | solution.py:48
  17.4 1.4 %collective-permute-done.22.refs_1_ = bf16[64,768]{1,0:T(8,128)(2,1)S(1)} collective-permute-done((bf16[64,768]{1,0:T(8,128)(2,1)S(1)}, bf16[64,768]{1,0:T(8,128)(2,1)S(1)}, u32[]{:S(2)}, u32[]{:S(2)}) %collective-permute-start.22) | collective-permute-done | bytes 98336 | tf_op jit(solution)/shard_map/ppermute | solution.py:48
  18.8 0.5 collective-permute-start.7
  19.3 3.1 %collective-permute-done.16.refs_1_ = bf16[64,768]{1,0:T(8,128)(2,1)S(1)} collective-permute-done((bf16[64,768]{1,0:T(8,128)(2,1)S(1)}, bf16[64,768]{1,0:T(8,128)(2,1)S(1)}, u32[]{:S(2)}, u32[]{:S(2)}) %collective-permute-start.16) | collective-permute-done | bytes 98336 | tf_op jit(solution)/shard_map/ppermute | solution.py:48
  22.4 0.5 collective-permute-start.8
  22.9 0.1 collective-permute-start.24
  23.0 0.7 collective-permute-done.17.refs_2_
  23.7 0.2 collective-permute-start.15
  23.9 1.3 %collective-permute-start.3 = (bf16[64,768]{1,0:T(8,128)(2,1)S(1)}, bf16[64,768]{1,0:T(8,128)(2,1)S(1)}, u32[]{:S(2)}, u32[]{:S(2)}) collective-permute-start(bf16[64,768]{1,0:T(8,128)(2,1)S(1)} %get-tuple-element.19.refs_0_), channel_id=1, source_target_pairs={{0,2},{1,3},{2,0},{3,1},{4,6},{5,7},{6,4},{7,5},{8,10},{9,11},{10,... | collective-permute-start | bytes 294920 | tf_op jit(solution)/shard_map/ppermute | solution.py:48
  25.2 0.5 collective-permute-start.18
  25.6 1.4 %load.1.qkv_ref = bf16[3,1024,256]{2,1,0:T(8,128)(2,1)S(1)} custom-call(bf16[3,1024,256]{2,1,0:T(8,128)(2,1)} %source_ref.1), custom_call_target="tpu_custom_call" | custom-call | tf_op jit(solution)/shard_map/load/pallas_call | solution.py:197
  27.1 2.4 %shard_map.146 = (f32[256,1024]{1,0:T(8,128)S(1)}, bf16[256,256]{1,0:T(8,128)(2,1)S(1)}) custom-call(f32[3,1024]{1,0:T(4,128)S(1)} %copy-done.5, bf16[768,1024]{1,0:T(8,128)(2,1)S(1)} %copy-done.1, bf16[3,1024,256]{2,1,0:T(8,128)(2,1)S(1)} %load.1.qkv_ref, bf16[64,768]{1,0:T(8,128)(2,1)S(1)} %get-tuple-element.27.refs_0_, ...), custom_call_target="tpu_custom_call" | custom-call | tf_op jit(solution)/shard_map/pallas_call | solution.py:301
  29.5 0.8 %collective-permute-start.25 = (bf16[256,256]{1,0:T(8,128)(2,1)S(1)}, bf16[256,256]{1,0:T(8,128)(2,1)S(1)}, u32[]{:S(2)}, u32[]{:S(2)}) collective-permute-start(bf16[256,256]{1,0:T(8,128)(2,1)S(1)} %get-tuple-element.29.refs_0_), channel_id=1, source_target_pairs={{0,2},{1,3},{2,0},{3,1},{4,6},{5,7},{6,4},{7,5},{8,10},{9,11},{10,... | collective-permute-start | bytes 393224 | tf_op jit(solution)/shard_map/ppermute | solution.py:48
  30.3 0.5 collective-permute-start.5
  30.8 2.4 %shard_map.144 = (f32[256,1024]{1,0:T(8,128)S(1)}, bf16[256,256]{1,0:T(8,128)(2,1)S(1)}) custom-call(f32[3,1024]{1,0:T(4,128)S(1)} %copy-done.5, bf16[768,1024]{1,0:T(8,128)(2,1)S(1)} %copy-done.1, bf16[3,1024,256]{2,1,0:T(8,128)(2,1)S(1)} %load.1.qkv_ref, bf16[64,768]{1,0:T(8,128)(2,1)S(1)} %get-tuple-element.24.refs_0_, ...), custom_call_target="tpu_custom_call" | custom-call | tf_op jit(solution)/shard_map/pallas_call | solution.py:301
  33.2 1.3 %collective-permute-start.19 = (bf16[256,256]{1,0:T(8,128)(2,1)S(1)}, bf16[256,256]{1,0:T(8,128)(2,1)S(1)}, u32[]{:S(2)}, u32[]{:S(2)}) collective-permute-start(bf16[256,256]{1,0:T(8,128)(2,1)S(1)} %get-tuple-element.26.refs_0_), channel_id=1, source_target_pairs={{0,2},{1,3},{2,0},{3,1},{4,6},{5,7},{6,4},{7,5},{8,10},{9,11},{10,... | collective-permute-start | bytes 393224 | tf_op jit(solution)/shard_map/ppermute | solution.py:48
  34.5 2.4 %shard_map.142 = (f32[256,1024]{1,0:T(8,128)S(1)}, bf16[256,256]{1,0:T(8,128)(2,1)S(1)}) custom-call(f32[3,1024]{1,0:T(4,128)S(1)} %copy-done.5, bf16[768,1024]{1,0:T(8,128)(2,1)S(1)} %copy-done.1, bf16[3,1024,256]{2,1,0:T(8,128)(2,1)S(1)} %load.1.qkv_ref, bf16[64,768]{1,0:T(8,128)(2,1)S(1)} %get-tuple-element.19.refs_0_, ...), custom_call_target="tpu_custom_call" | custom-call | tf_op jit(solution)/shard_map/pallas_call | solution.py:301
  36.9 0.8 %collective-permute-start.9 = (bf16[256,256]{1,0:T(8,128)(2,1)S(1)}, bf16[256,256]{1,0:T(8,128)(2,1)S(1)}, u32[]{:S(2)}, u32[]{:S(2)}) collective-permute-start(bf16[256,256]{1,0:T(8,128)(2,1)S(1)} %get-tuple-element.22.refs_0_), channel_id=1, source_target_pairs={{0,2},{1,3},{2,0},{3,1},{4,6},{5,7},{6,4},{7,5},{8,10},{9,11},{10,... | collective-permute-start | bytes 393224 | tf_op jit(solution)/shard_map/ppermute | solution.py:48
  37.7 1.0 %collective-permute-done.19.refs_1_ = bf16[256,256]{1,0:T(8,128)(2,1)S(1)} collective-permute-done((bf16[256,256]{1,0:T(8,128)(2,1)S(1)}, bf16[256,256]{1,0:T(8,128)(2,1)S(1)}, u32[]{:S(2)}, u32[]{:S(2)}) %collective-permute-start.19) | collective-permute-done | bytes 131104 | tf_op jit(solution)/shard_map/ppermute | solution.py:48
  38.7 3.4 %collective-permute-done.9.refs_1_ = bf16[256,256]{1,0:T(8,128)(2,1)S(1)} collective-permute-done((bf16[256,256]{1,0:T(8,128)(2,1)S(1)}, bf16[256,256]{1,0:T(8,128)(2,1)S(1)}, u32[]{:S(2)}, u32[]{:S(2)}) %collective-permute-start.9) | collective-permute-done | bytes 131104 | tf_op jit(solution)/shard_map/ppermute | solution.py:48
  42.1 0.5 collective-permute-start.10
  42.7 1.9 %shard_map.147.refs_2_ = f32[2,1024]{1,0:T(2,128)S(1)} custom-call(f32[3,1024]{1,0:T(4,128)S(1)} %copy-done.5, bf16[1024,1024]{1,0:T(8,128)(2,1)S(1)} %copy-done, f32[256,1024]{1,0:T(8,128)S(1)} %get-tuple-element.28.hidden_ref, bf16[256,256]{1,0:T(8,128)(2,1)S(1)} %get-tuple-element.29.refs_0_, bf16[256,256]{1,0:T(8,128)(2,1)S(1)} %collective-permute-done.25.refs_1_, ...), custom_call_target="tpu_custom_call" | custom-call | tf_op jit(solution)/shard_map/pallas_call | solution.py:332
  44.7 1.9 %shard_map.145.refs_1_ = f32[2,1024]{1,0:T(2,128)S(1)} custom-call(f32[3,1024]{1,0:T(4,128)S(1)} %copy-done.5, bf16[1024,1024]{1,0:T(8,128)(2,1)S(1)} %copy-done, f32[256,1024]{1,0:T(8,128)S(1)} %get-tuple-element.25.hidden_ref, bf16[256,256]{1,0:T(8,128)(2,1)S(1)} %get-tuple-element.26.refs_0_, bf16[256,256]{1,0:T(8,128)(2,1)S(1)} %collective-permute-done.19.refs_1_, ...), custom_call_target="tpu_custom_call" | custom-call | tf_op jit(solution)/shard_map/pallas_call | solution.py:332
  46.7 1.9 %shard_map.143.refs_0_ = f32[2,1024]{1,0:T(2,128)S(1)} custom-call(f32[3,1024]{1,0:T(4,128)S(1)} %copy-done.5, bf16[1024,1024]{1,0:T(8,128)(2,1)S(1)} %copy-done, f32[256,1024]{1,0:T(8,128)S(1)} %get-tuple-element.21.hidden_ref, bf16[256,256]{1,0:T(8,128)(2,1)S(1)} %get-tuple-element.22.refs_0_, bf16[256,256]{1,0:T(8,128)(2,1)S(1)} %collective-permute-done.9.refs_1_, ...), custom_call_target="tpu_custom_call" | custom-call | tf_op jit(solution)/shard_map/pallas_call | solution.py:332
  48.6 0.4 reduce.1.own_ref
  49.0 0.4 collective-permute-start.28
  49.5 0.8 %collective-permute-done.28.other_ref = f32[3,1024]{1,0:T(4,128)S(1)} collective-permute-done((f32[3,1024]{1,0:T(4,128)S(1)}, f32[3,1024]{1,0:T(4,128)S(1)}, u32[]{:S(2)}, u32[]{:S(2)}) %collective-permute-start.28) | collective-permute-done | bytes 12320 | tf_op jit(solution)/shard_map/ppermute | solution.py:48
  50.3 0.8 collective-permute-start.29
  51.1 3.0 %collective-permute-done.29.other_ref = f32[3,1024]{1,0:T(4,128)S(1)} collective-permute-done((f32[3,1024]{1,0:T(4,128)S(1)}, f32[3,1024]{1,0:T(4,128)S(1)}, u32[]{:S(2)}, u32[]{:S(2)}) %collective-permute-start.29) | collective-permute-done | bytes 12320 | tf_op jit(solution)/shard_map/ppermute | solution.py:48
  54.1 0.5 collective-permute-start.30
  54.6 3.2 %collective-permute-done.30.other_ref = f32[1,3,1024]{2,1,0:T(4,128)S(1)} collective-permute-done((f32[1,3,1024]{2,1,0:T(4,128)S(1)}, f32[1,3,1024]{2,1,0:T(4,128)S(1)}, u32[]{:S(2)}, u32[]{:S(2)}) %collective-permute-start.30) | collective-permute-done | bytes 12320 | tf_op jit(solution)/shard_map/ppermute | solution.py:48
  57.8 1.6 %collective-permute-start.31 = (f32[2,3,1024]{2,1,0:T(4,128)S(1)}, f32[2,3,1024]{2,1,0:T(4,128)S(1)}, u32[]{:S(2)}, u32[]{:S(2)}) collective-permute-start(f32[2,3,1024]{2,1,0:T(4,128)S(1)} %shard_map.148.own_ref), channel_id=1, source_target_pairs={{0,8},{4,12},{8,0},{12,4},{16,24},{20,28},{24,16},{28,20},{1,9},{5... | collective-permute-start | bytes 73736 | tf_op jit(solution)/shard_map/ppermute | solution.py:48
  59.4 2.3 %collective-permute-done.31.other_ref = f32[2,3,1024]{2,1,0:T(4,128)S(1)} collective-permute-done((f32[2,3,1024]{2,1,0:T(4,128)S(1)}, f32[2,3,1024]{2,1,0:T(4,128)S(1)}, u32[]{:S(2)}, u32[]{:S(2)}) %collective-permute-start.31) | collective-permute-done | bytes 24608 | tf_op jit(solution)/shard_map/ppermute | solution.py:48
  61.7 2.9 %collective-permute-start.32 = (f32[4,3,1024]{2,1,0:T(4,128)S(1)}, f32[4,3,1024]{2,1,0:T(4,128)S(1)}, u32[]{:S(2)}, u32[]{:S(2)}) collective-permute-start(f32[4,3,1024]{2,1,0:T(4,128)S(1)} %shard_map.149.first_ref), channel_id=1, source_target_pairs={{0,16},{4,20},{8,24},{12,28},{16,0},{20,4},{24,8},{28,12},{1,17},{... | collective-permute-start | bytes 147464 | tf_op jit(solution)/shard_map/ppermute | solution.py:48
  64.7 0.5 collective-permute-start
  65.2 3.2 %collective-permute-done.other_ref = bf16[1,3,1152]{2,1,0:T(4,128)(2,1)S(1)} collective-permute-done((bf16[1,3,1152]{2,1,0:T(4,128)(2,1)S(1)}, bf16[1,3,1152]{2,1,0:T(4,128)(2,1)S(1)}, u32[]{:S(2)}, u32[]{:S(2)}) %collective-permute-start) | collective-permute-done | bytes 6944 | tf_op jit(solution)/shard_map/ppermute | solution.py:48
  68.3 1.2 %collective-permute-start.1 = (bf16[2,3,1152]{2,1,0:T(4,128)(2,1)S(1)}, bf16[2,3,1152]{2,1,0:T(4,128)(2,1)S(1)}, u32[]{:S(2)}, u32[]{:S(2)}) collective-permute-start(bf16[2,3,1152]{2,1,0:T(4,128)(2,1)S(1)} %shard_map.140.own_ref), channel_id=1, source_target_pairs={{0,8},{4,12},{8,0},{12,4},{16,24},{20,28},{24,16},{28,20},{1,9},{5... | collective-permute-start | bytes 41480 | tf_op jit(solution)/shard_map/ppermute | solution.py:48
  69.5 2.5 %collective-permute-done.1.other_ref = bf16[2,3,1152]{2,1,0:T(4,128)(2,1)S(1)} collective-permute-done((bf16[2,3,1152]{2,1,0:T(4,128)(2,1)S(1)}, bf16[2,3,1152]{2,1,0:T(4,128)(2,1)S(1)}, u32[]{:S(2)}, u32[]{:S(2)}) %collective-permute-start.1) | collective-permute-done | bytes 13856 | tf_op jit(solution)/shard_map/ppermute | solution.py:48
  72.1 0.1 collective-permute-start.2
  72.2 4.8 %collective-permute-done.2.second_ref = bf16[4,3,1152]{2,1,0:T(4,128)(2,1)S(1)} collective-permute-done((bf16[4,3,1152]{2,1,0:T(4,128)(2,1)S(1)}, bf16[4,3,1152]{2,1,0:T(4,128)(2,1)S(1)}, u32[]{:S(2)}, u32[]{:S(2)}) %collective-permute-start.2) | collective-permute-done | bytes 27680 | tf_op jit(solution)/shard_map/ppermute | solution.py:48
  77.0 0.2 route.1
  77.3 2.2 %finish.1 = (f32[4,1024]{1,0:T(4,128)}, f32[4]{0:T(128)}) custom-call(f32[2]{0:T(128)S(1)} %copy-done.6, f32[3,1024]{1,0:T(4,128)S(1)} %copy-done.5, bf16[1024,1024]{1,0:T(8,128)(2,1)S(1)} %copy-done.3, f32[24,1024]{1,0:T(8,128)S(1)} %get-tuple-element.17.cap_ref, f32[24,128]{1,0:T(8,128)S(1)} %get-tuple-element.18.meta_ref, ...), custom_call_target="tpu_custom_call" | custom-call | tf_op jit(solution)/shard_map/finish/pallas_call | solution.py:398
  (52 shorter events, 0.3 us)
Async XLA Ops:
  0.6 14.7 %copy-start.7 = (bf16[64,1024]{1,0:T(8,128)(2,1)S(1)}, bf16[64,1024]{1,0:T(8,128)(2,1)}, u32[]{:S(2)}) copy-start(bf16[64,1024]{1,0:T(8,128)(2,1)} %pos_hbm.1) | copy-start | bytes 393220
  0.6 18.2 %copy-start.2 = (bf16[256,1024]{1,0:T(8,128)(2,1)S(1)}, bf16[256,1024]{1,0:T(8,128)(2,1)}, u32[]{:S(2)}) copy-start(bf16[256,1024]{1,0:T(8,128)(2,1)} %refs_4_.5) | copy-start | bytes 1572868
  2.7 9.3 %collective-permute-start.12 = (bf16[128,1024]{1,0:T(8,128)(2,1)S(1)}, bf16[128,1024]{1,0:T(8,128)(2,1)S(1)}, u32[]{:S(2)}, u32[]{:S(2)}) collective-permute-start(bf16[128,1024]{1,0:T(8,128)(2,1)S(1)} %get-tuple-element.23), channel_id=1, source_target_pairs={{0,2},{1,3},{2,0},{3,1},{4,6},{5,7},{6,4},{7,5},{8,10},{9,11},{10,... | collective-permute-start | bytes 786440 | tf_op jit(solution)/shard_map/ppermute | solution.py:48
  12.1 10.9 %collective-permute-start.13 = (bf16[128,1024]{1,0:T(8,128)(2,1)S(1)}, bf16[128,1024]{1,0:T(8,128)(2,1)S(1)}, u32[]{:S(2)}, u32[]{:S(2)}) collective-permute-start(bf16[128,1024]{1,0:T(8,128)(2,1)S(1)} %collective-permute-done.12.refs_0_), channel_id=1, source_target_pairs={{0,4},{4,0},{8,12},{12,8},{16,20},{20,16},{24,28},{28,24},{1,5},{5... | collective-permute-start | bytes 786440 | tf_op jit(solution)/shard_map/ppermute | solution.py:48
  13.8 5.0 %collective-permute-start.22 = (bf16[64,768]{1,0:T(8,128)(2,1)S(1)}, bf16[64,768]{1,0:T(8,128)(2,1)S(1)}, u32[]{:S(2)}, u32[]{:S(2)}) collective-permute-start(bf16[64,768]{1,0:T(8,128)(2,1)S(1)} %get-tuple-element.27.refs_0_), channel_id=1, source_target_pairs={{0,2},{1,3},{2,0},{3,1},{4,6},{5,7},{6,4},{7,5},{8,10},{9,11},{10,... | collective-permute-start | bytes 294920 | tf_op jit(solution)/shard_map/ppermute | solution.py:48
  15.3 7.1 %collective-permute-start.6 = (bf16[64,1024]{1,0:T(8,128)(2,1)S(1)}, bf16[64,1024]{1,0:T(8,128)(2,1)S(1)}, u32[]{:S(2)}, u32[]{:S(2)}) collective-permute-start(bf16[64,1024]{1,0:T(8,128)(2,1)S(1)} %copy-done.7), channel_id=1, source_target_pairs={{0,2},{1,3},{2,0},{3,1},{4,6},{5,7},{6,4},{7,5},{8,10},{9,11},{10,... | collective-permute-start | bytes 393224 | tf_op jit(solution)/shard_map/ppermute | solution.py:48
  15.9 2.9 %collective-permute-start.23 = (bf16[64,768]{1,0:T(8,128)(2,1)S(1)}, bf16[64,768]{1,0:T(8,128)(2,1)S(1)}, u32[]{:S(2)}, u32[]{:S(2)}) collective-permute-start(bf16[64,768]{1,0:T(8,128)(2,1)S(1)} %get-tuple-element.27.refs_0_), channel_id=1, source_target_pairs={{0,1},{1,0},{2,3},{3,2},{4,5},{5,4},{6,7},{7,6},{8,9},{9,8},{10,11... | collective-permute-start | bytes 294920 | tf_op jit(solution)/shard_map/ppermute | solution.py:48
  15.9 6.5 %collective-permute-start.16 = (bf16[64,768]{1,0:T(8,128)(2,1)S(1)}, bf16[64,768]{1,0:T(8,128)(2,1)S(1)}, u32[]{:S(2)}, u32[]{:S(2)}) collective-permute-start(bf16[64,768]{1,0:T(8,128)(2,1)S(1)} %get-tuple-element.24.refs_0_), channel_id=1, source_target_pairs={{0,2},{1,3},{2,0},{3,1},{4,6},{5,7},{6,4},{7,5},{8,10},{9,11},{10,... | collective-permute-start | bytes 294920 | tf_op jit(solution)/shard_map/ppermute | solution.py:48
  18.8 23.9 %collective-permute-start.14 = (bf16[256,1024]{1,0:T(8,128)(2,1)S(1)}, bf16[256,1024]{1,0:T(8,128)(2,1)S(1)}, u32[]{:S(2)}, u32[]{:S(2)}) collective-permute-start(bf16[256,1024]{1,0:T(8,128)(2,1)S(1)} %copy-done.2), channel_id=1, source_target_pairs={{0,1},{1,0},{2,3},{3,2},{4,5},{5,4},{6,7},{7,6},{8,9},{9,8},{10,11... | collective-permute-start | bytes 1572872 | tf_op jit(solution)/shard_map/ppermute | solution.py:48
  18.8 5.1 %collective-permute-start.7 = (bf16[64,1024]{1,0:T(8,128)(2,1)S(1)}, bf16[64,1024]{1,0:T(8,128)(2,1)S(1)}, u32[]{:S(2)}, u32[]{:S(2)}) collective-permute-start(bf16[64,1024]{1,0:T(8,128)(2,1)S(1)} %copy-done.7), channel_id=1, source_target_pairs={{0,1},{1,0},{2,3},{3,2},{4,5},{5,4},{6,7},{7,6},{8,9},{9,8},{10,11... | collective-permute-start | bytes 393224 | tf_op jit(solution)/shard_map/ppermute | solution.py:48
  22.4 1.3 %collective-permute-start.17 = (bf16[64,768]{1,0:T(8,128)(2,1)S(1)}, bf16[64,768]{1,0:T(8,128)(2,1)S(1)}, u32[]{:S(2)}, u32[]{:S(2)}) collective-permute-start(bf16[64,768]{1,0:T(8,128)(2,1)S(1)} %get-tuple-element.24.refs_0_), channel_id=1, source_target_pairs={{0,1},{1,0},{2,3},{3,2},{4,5},{5,4},{6,7},{7,6},{8,9},{9,8},{10,11... | collective-permute-start | bytes 294920 | tf_op jit(solution)/shard_map/ppermute | solution.py:48
  22.4 2.8 %collective-permute-start.8 = (bf16[64,1024]{1,0:T(8,128)(2,1)S(1)}, bf16[64,1024]{1,0:T(8,128)(2,1)S(1)}, u32[]{:S(2)}, u32[]{:S(2)}) collective-permute-start(bf16[64,1024]{1,0:T(8,128)(2,1)S(1)} %collective-permute-done.6.refs_5_), channel_id=1, source_target_pairs={{0,1},{1,0},{2,3},{3,2},{4,5},{5,4},{6,7},{7,6},{8,9},{9,8},{10,11... | collective-permute-start | bytes 393224 | tf_op jit(solution)/shard_map/ppermute | solution.py:48
  22.9 2.2 %collective-permute-start.24 = (bf16[64,768]{1,0:T(8,128)(2,1)S(1)}, bf16[64,768]{1,0:T(8,128)(2,1)S(1)}, u32[]{:S(2)}, u32[]{:S(2)}) collective-permute-start(bf16[64,768]{1,0:T(8,128)(2,1)S(1)} %collective-permute-done.22.refs_1_), channel_id=1, source_target_pairs={{0,1},{1,0},{2,3},{3,2},{4,5},{5,4},{6,7},{7,6},{8,9},{9,8},{10,11... | collective-permute-start | bytes 294920 | tf_op jit(solution)/shard_map/ppermute | solution.py:48
  23.7 19.0 %collective-permute-start.15 = (bf16[256,1024]{1,0:T(8,128)(2,1)S(1)}, bf16[256,1024]{1,0:T(8,128)(2,1)S(1)}, u32[]{:S(2)}, u32[]{:S(2)}) collective-permute-start(bf16[256,1024]{1,0:T(8,128)(2,1)S(1)} %assemble.1.refs_5_), channel_id=1, source_target_pairs={{0,1},{1,0},{2,3},{3,2},{4,5},{5,4},{6,7},{7,6},{8,9},{9,8},{10,11... | collective-permute-start | bytes 1572872 | tf_op jit(solution)/shard_map/ppermute | solution.py:48
  23.9 3.2 %copy-start.1 = (bf16[768,1024]{1,0:T(8,128)(2,1)S(1)}, bf16[768,1024]{1,0:T(8,128)(2,1)}, u32[]{:S(2)}) copy-start(bf16[768,1024]{1,0:T(8,128)(2,1)} %patch_ref.5) | copy-start | bytes 4718596
  23.9 3.2 %copy-start.5 = (f32[3,1024]{1,0:T(4,128)S(1)}, f32[3,1024]{1,0:T(4,128)}, u32[]{:S(2)}) copy-start(f32[3,1024]{1,0:T(4,128)} %gains_ref.13) | copy-start | bytes 36868
  23.9 5.6 %collective-permute-start.3 = (bf16[64,768]{1,0:T(8,128)(2,1)S(1)}, bf16[64,768]{1,0:T(8,128)(2,1)S(1)}, u32[]{:S(2)}, u32[]{:S(2)}) collective-permute-start(bf16[64,768]{1,0:T(8,128)(2,1)S(1)} %get-tuple-element.19.refs_0_), channel_id=1, source_target_pairs={{0,2},{1,3},{2,0},{3,1},{4,6},{5,7},{6,4},{7,5},{8,10},{9,11},{10,... | collective-permute-start | bytes 294920 | tf_op jit(solution)/shard_map/ppermute | solution.py:48
  25.1 5.2 %collective-permute-start.4 = (bf16[64,768]{1,0:T(8,128)(2,1)S(1)}, bf16[64,768]{1,0:T(8,128)(2,1)S(1)}, u32[]{:S(2)}, u32[]{:S(2)}) collective-permute-start(bf16[64,768]{1,0:T(8,128)(2,1)S(1)} %get-tuple-element.19.refs_0_), channel_id=1, source_target_pairs={{0,1},{1,0},{2,3},{3,2},{4,5},{5,4},{6,7},{7,6},{8,9},{9,8},{10,11... | collective-permute-start | bytes 294920 | tf_op jit(solution)/shard_map/ppermute | solution.py:48
  25.2 5.1 %collective-permute-start.18 = (bf16[64,768]{1,0:T(8,128)(2,1)S(1)}, bf16[64,768]{1,0:T(8,128)(2,1)S(1)}, u32[]{:S(2)}, u32[]{:S(2)}) collective-permute-start(bf16[64,768]{1,0:T(8,128)(2,1)S(1)} %collective-permute-done.16.refs_1_), channel_id=1, source_target_pairs={{0,1},{1,0},{2,3},{3,2},{4,5},{5,4},{6,7},{7,6},{8,9},{9,8},{10,11... | collective-permute-start | bytes 294920 | tf_op jit(solution)/shard_map/ppermute | solution.py:48
  29.5 7.4 %collective-permute-start.25 = (bf16[256,256]{1,0:T(8,128)(2,1)S(1)}, bf16[256,256]{1,0:T(8,128)(2,1)S(1)}, u32[]{:S(2)}, u32[]{:S(2)}) collective-permute-start(bf16[256,256]{1,0:T(8,128)(2,1)S(1)} %get-tuple-element.29.refs_0_), channel_id=1, source_target_pairs={{0,2},{1,3},{2,0},{3,1},{4,6},{5,7},{6,4},{7,5},{8,10},{9,11},{10,... | collective-permute-start | bytes 393224 | tf_op jit(solution)/shard_map/ppermute | solution.py:48
  30.3 7.4 %collective-permute-start.26 = (bf16[256,256]{1,0:T(8,128)(2,1)S(1)}, bf16[256,256]{1,0:T(8,128)(2,1)S(1)}, u32[]{:S(2)}, u32[]{:S(2)}) collective-permute-start(bf16[256,256]{1,0:T(8,128)(2,1)S(1)} %get-tuple-element.29.refs_0_), channel_id=1, source_target_pairs={{0,1},{1,0},{2,3},{3,2},{4,5},{5,4},{6,7},{7,6},{8,9},{9,8},{10,11... | collective-permute-start | bytes 393224 | tf_op jit(solution)/shard_map/ppermute | solution.py:48
  30.3 2.9 %collective-permute-start.5 = (bf16[64,768]{1,0:T(8,128)(2,1)S(1)}, bf16[64,768]{1,0:T(8,128)(2,1)S(1)}, u32[]{:S(2)}, u32[]{:S(2)}) collective-permute-start(bf16[64,768]{1,0:T(8,128)(2,1)S(1)} %collective-permute-done.3.refs_1_), channel_id=1, source_target_pairs={{0,1},{1,0},{2,3},{3,2},{4,5},{5,4},{6,7},{7,6},{8,9},{9,8},{10,11... | collective-permute-start | bytes 294920 | tf_op jit(solution)/shard_map/ppermute | solution.py:48
  33.2 9.5 %copy-start = (bf16[1024,1024]{1,0:T(8,128)(2,1)S(1)}, bf16[1024,1024]{1,0:T(8,128)(2,1)}, u32[]{:S(2)}) copy-start(bf16[1024,1024]{1,0:T(8,128)(2,1)} %up_ref.5) | copy-start | bytes 6291460
  33.2 5.5 %collective-permute-start.19 = (bf16[256,256]{1,0:T(8,128)(2,1)S(1)}, bf16[256,256]{1,0:T(8,128)(2,1)S(1)}, u32[]{:S(2)}, u32[]{:S(2)}) collective-permute-start(bf16[256,256]{1,0:T(8,128)(2,1)S(1)} %get-tuple-element.26.refs_0_), channel_id=1, source_target_pairs={{0,2},{1,3},{2,0},{3,1},{4,6},{5,7},{6,4},{7,5},{8,10},{9,11},{10,... | collective-permute-start | bytes 393224 | tf_op jit(solution)/shard_map/ppermute | solution.py:48
  36.9 5.2 %collective-permute-start.9 = (bf16[256,256]{1,0:T(8,128)(2,1)S(1)}, bf16[256,256]{1,0:T(8,128)(2,1)S(1)}, u32[]{:S(2)}, u32[]{:S(2)}) collective-permute-start(bf16[256,256]{1,0:T(8,128)(2,1)S(1)} %get-tuple-element.22.refs_0_), channel_id=1, source_target_pairs={{0,2},{1,3},{2,0},{3,1},{4,6},{5,7},{6,4},{7,5},{8,10},{9,11},{10,... | collective-permute-start | bytes 393224 | tf_op jit(solution)/shard_map/ppermute | solution.py:48
  37.7 4.4 %collective-permute-start.27 = (bf16[256,256]{1,0:T(8,128)(2,1)S(1)}, bf16[256,256]{1,0:T(8,128)(2,1)S(1)}, u32[]{:S(2)}, u32[]{:S(2)}) collective-permute-start(bf16[256,256]{1,0:T(8,128)(2,1)S(1)} %collective-permute-done.25.refs_1_), channel_id=1, source_target_pairs={{0,1},{1,0},{2,3},{3,2},{4,5},{5,4},{6,7},{7,6},{8,9},{9,8},{10,11... | collective-permute-start | bytes 393224 | tf_op jit(solution)/shard_map/ppermute | solution.py:48
  38.7 5.9 %collective-permute-start.20 = (bf16[256,256]{1,0:T(8,128)(2,1)S(1)}, bf16[256,256]{1,0:T(8,128)(2,1)S(1)}, u32[]{:S(2)}, u32[]{:S(2)}) collective-permute-start(bf16[256,256]{1,0:T(8,128)(2,1)S(1)} %get-tuple-element.26.refs_0_), channel_id=1, source_target_pairs={{0,1},{1,0},{2,3},{3,2},{4,5},{5,4},{6,7},{7,6},{8,9},{9,8},{10,11... | collective-permute-start | bytes 393224 | tf_op jit(solution)/shard_map/ppermute | solution.py:48
  42.1 2.5 %collective-permute-start.21 = (bf16[256,256]{1,0:T(8,128)(2,1)S(1)}, bf16[256,256]{1,0:T(8,128)(2,1)S(1)}, u32[]{:S(2)}, u32[]{:S(2)}) collective-permute-start(bf16[256,256]{1,0:T(8,128)(2,1)S(1)} %collective-permute-done.19.refs_1_), channel_id=1, source_target_pairs={{0,1},{1,0},{2,3},{3,2},{4,5},{5,4},{6,7},{7,6},{8,9},{9,8},{10,11... | collective-permute-start | bytes 393224 | tf_op jit(solution)/shard_map/ppermute | solution.py:48
  42.1 4.5 %collective-permute-start.10 = (bf16[256,256]{1,0:T(8,128)(2,1)S(1)}, bf16[256,256]{1,0:T(8,128)(2,1)S(1)}, u32[]{:S(2)}, u32[]{:S(2)}) collective-permute-start(bf16[256,256]{1,0:T(8,128)(2,1)S(1)} %get-tuple-element.22.refs_0_), channel_id=1, source_target_pairs={{0,1},{1,0},{2,3},{3,2},{4,5},{5,4},{6,7},{7,6},{8,9},{9,8},{10,11... | collective-permute-start | bytes 393224 | tf_op jit(solution)/shard_map/ppermute | solution.py:48
  42.7 4.0 %collective-permute-start.11 = (bf16[256,256]{1,0:T(8,128)(2,1)S(1)}, bf16[256,256]{1,0:T(8,128)(2,1)S(1)}, u32[]{:S(2)}, u32[]{:S(2)}) collective-permute-start(bf16[256,256]{1,0:T(8,128)(2,1)S(1)} %collective-permute-done.9.refs_1_), channel_id=1, source_target_pairs={{0,1},{1,0},{2,3},{3,2},{4,5},{5,4},{6,7},{7,6},{8,9},{9,8},{10,11... | collective-permute-start | bytes 393224 | tf_op jit(solution)/shard_map/ppermute | solution.py:48
  46.6 2.0 %copy-start.4 = (bf16[1024,1024]{1,0:T(8,128)(2,1)S(1)}, bf16[1024,1024]{1,0:T(8,128)(2,1)}, u32[]{:S(2)}) copy-start(bf16[1024,1024]{1,0:T(8,128)(2,1)} %down_ref.1) | copy-start | bytes 6291460
  48.6 28.7 %copy-start.3 = (bf16[1024,1024]{1,0:T(8,128)(2,1)S(1)}, bf16[1024,1024]{1,0:T(8,128)(2,1)}, u32[]{:S(2)}) copy-start(bf16[1024,1024]{1,0:T(8,128)(2,1)} %weight_ref.1) | copy-start | bytes 6291460
  48.6 28.7 %copy-start.6 = (f32[2]{0:T(128)S(1)}, f32[2]{0:T(128)}, u32[]{:S(2)}) copy-start(f32[2]{0:T(128)} %params_ref.1) | copy-start | bytes 28
  49.0 1.3 %collective-permute-start.28 = (f32[3,1024]{1,0:T(4,128)S(1)}, f32[3,1024]{1,0:T(4,128)S(1)}, u32[]{:S(2)}, u32[]{:S(2)}) collective-permute-start(f32[3,1024]{1,0:T(4,128)S(1)} %reduce.1.own_ref), channel_id=1, source_target_pairs={{0,1},{1,0},{2,3},{3,2},{4,5},{5,4},{6,7},{7,6},{8,9},{9,8},{10,11... | collective-permute-start | bytes 36872 | tf_op jit(solution)/shard_map/ppermute | solution.py:48
  50.3 3.7 %collective-permute-start.29 = (f32[3,1024]{1,0:T(4,128)S(1)}, f32[3,1024]{1,0:T(4,128)S(1)}, u32[]{:S(2)}, u32[]{:S(2)}) collective-permute-start(f32[3,1024]{1,0:T(4,128)S(1)} %add.2.own_ref), channel_id=1, source_target_pairs={{0,2},{1,3},{2,0},{3,1},{4,6},{5,7},{6,4},{7,5},{8,10},{9,11},{10,... | collective-permute-start | bytes 36872 | tf_op jit(solution)/shard_map/ppermute | solution.py:48
  54.1 3.7 %collective-permute-start.30 = (f32[1,3,1024]{2,1,0:T(4,128)S(1)}, f32[1,3,1024]{2,1,0:T(4,128)S(1)}, u32[]{:S(2)}, u32[]{:S(2)}) collective-permute-start(f32[1,3,1024]{2,1,0:T(4,128)S(1)} %bitcast.1), channel_id=1, source_target_pairs={{0,4},{4,0},{8,12},{12,8},{16,20},{20,16},{24,28},{28,24},{1,5},{5... | collective-permute-start | bytes 36872 | tf_op jit(solution)/shard_map/ppermute | solution.py:48
  57.8 3.9 %collective-permute-start.31 = (f32[2,3,1024]{2,1,0:T(4,128)S(1)}, f32[2,3,1024]{2,1,0:T(4,128)S(1)}, u32[]{:S(2)}, u32[]{:S(2)}) collective-permute-start(f32[2,3,1024]{2,1,0:T(4,128)S(1)} %shard_map.148.own_ref), channel_id=1, source_target_pairs={{0,8},{4,12},{8,0},{12,4},{16,24},{20,28},{24,16},{28,20},{1,9},{5... | collective-permute-start | bytes 73736 | tf_op jit(solution)/shard_map/ppermute | solution.py:48
  61.7 15.5 %collective-permute-start.32 = (f32[4,3,1024]{2,1,0:T(4,128)S(1)}, f32[4,3,1024]{2,1,0:T(4,128)S(1)}, u32[]{:S(2)}, u32[]{:S(2)}) collective-permute-start(f32[4,3,1024]{2,1,0:T(4,128)S(1)} %shard_map.149.first_ref), channel_id=1, source_target_pairs={{0,16},{4,20},{8,24},{12,28},{16,0},{20,4},{24,8},{28,12},{1,17},{... | collective-permute-start | bytes 147464 | tf_op jit(solution)/shard_map/ppermute | solution.py:48
  64.7 3.7 %collective-permute-start = (bf16[1,3,1152]{2,1,0:T(4,128)(2,1)S(1)}, bf16[1,3,1152]{2,1,0:T(4,128)(2,1)S(1)}, u32[]{:S(2)}, u32[]{:S(2)}) collective-permute-start(bf16[1,3,1152]{2,1,0:T(4,128)(2,1)S(1)} %get-tuple-element.16.own_ref), channel_id=1, source_target_pairs={{0,4},{4,0},{8,12},{12,8},{16,20},{20,16},{24,28},{28,24},{1,5},{5... | collective-permute-start | bytes 20744 | tf_op jit(solution)/shard_map/ppermute | solution.py:48
  68.3 3.8 %collective-permute-start.1 = (bf16[2,3,1152]{2,1,0:T(4,128)(2,1)S(1)}, bf16[2,3,1152]{2,1,0:T(4,128)(2,1)S(1)}, u32[]{:S(2)}, u32[]{:S(2)}) collective-permute-start(bf16[2,3,1152]{2,1,0:T(4,128)(2,1)S(1)} %shard_map.140.own_ref), channel_id=1, source_target_pairs={{0,8},{4,12},{8,0},{12,4},{16,24},{20,28},{24,16},{28,20},{1,9},{5... | collective-permute-start | bytes 41480 | tf_op jit(solution)/shard_map/ppermute | solution.py:48
  72.1 4.9 %collective-permute-start.2 = (bf16[4,3,1152]{2,1,0:T(4,128)(2,1)S(1)}, bf16[4,3,1152]{2,1,0:T(4,128)(2,1)S(1)}, u32[]{:S(2)}, u32[]{:S(2)}) collective-permute-start(bf16[4,3,1152]{2,1,0:T(4,128)(2,1)S(1)} %shard_map.141.first_ref), channel_id=1, source_target_pairs={{0,16},{4,20},{8,24},{12,28},{16,0},{20,4},{24,8},{28,12},{1,17},{... | collective-permute-start | bytes 82952 | tf_op jit(solution)/shard_map/ppermute | solution.py:48

commit v4 on v3

--- a/solution.py
+++ b/solution.py
@@ -14,6 +14,8 @@
 RECV_MOST = 4
 META = 128
 PIECES = 2
+CHUNKS = (1, 1, 1)
+GRANT = 20
 EPS = 1e-06
 
 
@@ -110,8 +112,8 @@
 
 
 def pick_kernel(pieces, sel_hbm, dest_hbm, pixels_ref, cap_hbm, output_ref, pos_hbm, *refs):
-    row_refs = refs[:SEND_MOST]
-    meta_ref, piece_ref, pos_ref, sel_ref, dest_ref, cap_ref, sems = refs[SEND_MOST:]
+    row_refs = refs[: len(CHUNKS)]
+    meta_ref, piece_ref, pos_ref, sel_ref, dest_ref, cap_ref, sems = refs[len(CHUNKS) :]
     first = [
         pltpu.make_async_copy(source, target, sems.at[SEND_MOST + 1 + i])
         for i, (source, target) in enumerate(
@@ -132,10 +134,13 @@
             index[r] = jnp.where(take, e, index[r])
             target[r] = jnp.where(take, dest_ref[e], target[r])
         count = count + here.astype(jnp.int32)
-    copies = [
-        pltpu.make_async_copy(pixels_ref.at[index[r]], row_refs[r], sems.at[r])
-        for r in range(SEND_MOST)
-    ]
+    length = pos_ref.shape[0]
+    copies = []
+    for c, chunk in enumerate(CHUNKS):
+        for i in range(chunk):
+            r = sum(CHUNKS[:c]) + i
+            place = row_refs[c].at[pl.ds(i * length, length)]
+            copies.append(pltpu.make_async_copy(pixels_ref.at[index[r]], place, sems.at[r]))
     height = piece_ref.shape[0]
     start = pl.multiple_of((lax.axis_index("dp") & (pieces - 1)) * height, height)
     copies.append(
@@ -164,14 +169,16 @@
     hbm = pl.BlockSpec(memory_space=pltpu.MemorySpace.HBM)
     *rows, caption_meta, piece, own_position = pl.pallas_call(
         functools.partial(pick_kernel, pieces),
-        out_shape=(jax.ShapeDtypeStruct((length, depth), BF16),) * SEND_MOST
+        out_shape=tuple(
+            jax.ShapeDtypeStruct((chunk * length, depth), BF16) for chunk in CHUNKS
+        )
         + (
             jax.ShapeDtypeStruct((1, SEND_MOST, captions.shape[1] + META), BF16),
             jax.ShapeDtypeStruct((fan // pieces, width), BF16),
             jax.ShapeDtypeStruct(position.shape, BF16),
         ),
         in_specs=[hbm] * 6,
-        out_specs=(vmem(),) * (SEND_MOST + 3),
+        out_specs=(vmem(),) * (len(CHUNKS) + 3),
         scratch_shapes=[
             SMEM(selection.shape, jnp.int32),
             SMEM(destination.shape, jnp.int32),
@@ -272,26 +279,38 @@
     pixel_refs = refs[:shards]
     position_refs = refs[shards : 2 * shards]
     hidden_ref, context_ref = refs[2 * shards :]
-    pixels = jnp.concatenate([ref[...] for ref in pixel_refs], axis=0)
-    position = jnp.concatenate([ref[...] for ref in position_refs], axis=0)
+    block = position_refs[0].shape[0]
+    length = block * shards
+    images = range(pixel_refs[0].shape[0] // block)
+    pixels = jnp.concatenate(
+        [ref[i * block : (i + 1) * block, :] for i in images for ref in pixel_refs], axis=0
+    )
+    position = jnp.concatenate([ref[...] for ref in position_refs], axis=0).astype(F32)
     hidden = jnp.dot(pixels, patch_ref[...], preferred_element_type=F32)
-    hidden = hidden + position.astype(F32)
+    hidden = hidden + jnp.concatenate([position for _ in images], axis=0)
     hidden_ref[...] = hidden
     normed = layer_norm(hidden, gains_ref[0:1, :]).astype(BF16)
     query, key, value = [
         jnp.dot(normed, qkv_ref[t], preferred_element_type=F32).astype(BF16) for t in range(3)
     ]
     query = query * jnp.asarray(HEAD_DIM ** (-0.5), BF16)
-    parts = []
-    for h in range(query.shape[1] // HEAD_DIM):
-        cols = slice(h * HEAD_DIM, (h + 1) * HEAD_DIM)
-        scores = lax.dot_general(
-            query[:, cols], key[:, cols], (((1,), (1,)), ((), ())), preferred_element_type=F32
-        )
-        weights = jnp.exp(scores - jnp.max(scores, axis=-1, keepdims=True))
-        weights = weights * (1.0 / jnp.sum(weights, axis=-1, keepdims=True))
-        parts.append(jnp.dot(weights.astype(BF16), value[:, cols], preferred_element_type=F32))
-    context_ref[...] = jnp.concatenate(parts, axis=1).astype(BF16)
+    for i in images:
+        rows = slice(i * length, (i + 1) * length)
+        parts = []
+        for h in range(query.shape[1] // HEAD_DIM):
+            cols = slice(h * HEAD_DIM, (h + 1) * HEAD_DIM)
+            scores = lax.dot_general(
+                query[rows, cols],
+                key[rows, cols],
+                (((1,), (1,)), ((), ())),
+                preferred_element_type=F32,
+            )
+            weights = jnp.exp(scores - jnp.max(scores, axis=-1, keepdims=True))
+            weights = weights * (1.0 / jnp.sum(weights, axis=-1, keepdims=True))
+            parts.append(
+                jnp.dot(weights.astype(BF16), value[rows, cols], preferred_element_type=F32)
+            )
+        context_ref[rows, :] = jnp.concatenate(parts, axis=1).astype(BF16)
 
 
 def attend(pixels, positions, gains, patch_weight, qkv):
@@ -306,48 +325,54 @@
         ),
         in_specs=[vmem()] * (3 + 2 * shards),
         out_specs=(vmem(), vmem()),
-        compiler_params=small(14),
+        compiler_params=small(GRANT),
     )(gains, patch_weight, qkv, *pixels, *positions)
 
 
-def expand_kernel(order, gains_ref, up_ref, hidden_ref, *refs):
+def expand_kernel(order, images, gains_ref, up_ref, hidden_ref, *refs):
     shards = len(order)
     context_refs = refs[:shards]
     output_refs = refs[shards : 2 * shards]
     sums_ref = refs[2 * shards]
-    block = hidden_ref.shape[0] // shards
+    length = hidden_ref.shape[0] // images
+    block = length // shards
     hidden = hidden_ref[...]
     for j, ref in enumerate(context_refs):
         places = [order.index(order[p] ^ order[j]) for p in range(shards)]
-        context = jnp.concatenate([ref[q * block : (q + 1) * block, :] for q in places], axis=0)
+        starts = [i * length + q * block for i in range(images) for q in places]
+        context = jnp.concatenate([ref[at : at + block, :] for at in starts], axis=0)
         hidden = hidden + jnp.dot(context, output_refs[j][...], preferred_element_type=F32)
     normed = layer_norm(hidden, gains_ref[1:2, :]).astype(BF16)
     expanded = jax.nn.gelu(jnp.dot(normed, up_ref[...], preferred_element_type=F32)).astype(BF16)
-    sums_ref[0:1, :] = jnp.sum(hidden, axis=0, keepdims=True)
-    sums_ref[1:2, :] = jnp.sum(expanded.astype(F32), axis=0, keepdims=True)
-
-
-def expand(contexts, order, outputs, hidden, gains, up_weight):
+    expanded = expanded.astype(F32)
+    for i in range(images):
+        rows = slice(i * length, (i + 1) * length)
+        sums_ref[i : i + 1, :] = jnp.sum(hidden[rows], axis=0, keepdims=True)
+        sums_ref[images + i : images + i + 1, :] = jnp.sum(expanded[rows], axis=0, keepdims=True)
+
+
+def expand(contexts, order, images, outputs, hidden, gains, up_weight):
     width = hidden.shape[1]
     return pl.pallas_call(
-        functools.partial(expand_kernel, tuple(order)),
-        out_shape=jax.ShapeDtypeStruct((2, width), F32),
+        functools.partial(expand_kernel, tuple(order), images),
+        out_shape=jax.ShapeDtypeStruct((2 * images, width), F32),
         in_specs=[vmem()] * (3 + 2 * len(order)),
         out_specs=vmem(),
-        compiler_params=small(14),
+        compiler_params=small(GRANT),
     )(gains, up_weight, hidden, *contexts, *outputs)
 
 
 def reduce_kernel(scale, down_ref, *refs):
     out_ref = refs[-1]
     sums = refs[:-1]
-    units = jnp.concatenate([ref[1:2, :] for ref in sums], axis=0) * scale
-    residual = jnp.concatenate([ref[0:1, :] for ref in sums], axis=0) * scale
+    halves = [ref.shape[0] // 2 for ref in sums]
+    units = jnp.concatenate([ref[n:, :] for n, ref in zip(halves, sums)], axis=0) * scale
+    residual = jnp.concatenate([ref[:n, :] for n, ref in zip(halves, sums)], axis=0) * scale
     high = units.astype(BF16)
     low = (units - high.astype(F32)).astype(BF16)
     both = jnp.concatenate([high, low], axis=0)
     product = jnp.dot(both, down_ref[...], preferred_element_type=F32)
-    count = len(sums)
+    count = sum(halves)
     own = (lax.axis_index("mp") == 0).astype(F32)
     out_ref[...] = product[:count] + product[count:] + residual * own
 
@@ -355,7 +380,7 @@
 def reduce_units(sums, down_weight, patches):
     return pl.pallas_call(
         functools.partial(reduce_kernel, 1.0 / patches),
-        out_shape=jax.ShapeDtypeStruct((len(sums), down_weight.shape[1]), F32),
+        out_shape=jax.ShapeDtypeStruct((SEND_MOST, down_weight.shape[1]), F32),
         in_specs=[vmem()] * (1 + len(sums)),
         out_specs=vmem(),
         name="reduce",
@@ -446,12 +471,12 @@
     captions, meta = route(*double_stack(caption_meta, "dp"))
 
     sums = []
-    for r in range(SEND_MOST):
+    for r, images in enumerate(CHUNKS):
         hidden, context = attend(
             pixel_blocks[r], positions, norm_gains, patch_weight, query_key_value
         )
         contexts, _ = gather_blocks(context, "mp")
-        sums.append(expand(contexts, order, outputs, hidden, norm_gains, up_weight))
+        sums.append(expand(contexts, order, images, outputs, hidden, norm_gains, up_weight))
     pooled = reduce_units(sums, down_weight, position.shape[0] * shards)
     for bit in reversed(bits_down(shards)):
         pooled = add(pooled, swap(pooled, "mp", bit))

time: 79.6 us -> 79.6 us (level)
  no operation moved by 1% of the time
where the time goes in v4:
time: 79.6 us; the launch traced here: 79.4 us
  waiting for transfers between devices  35.8 us (45%)
  starting transfers between devices  23.5 us (30%)
  Pallas kernels  19.3 us (24%)
  between operations  0.83 us (1%)
    ppermute x33, waiting for transfers between devices, swap(): return lax.ppermute(values, axis, [(i, i ^ bit) for i in range(size)])  35.8 us
    ppermute x33, starting transfers between devices, swap(): return lax.ppermute(values, axis, [(i, i ^ bit) for i in range(size)])  23.5 us
    pallas_call x3, Pallas kernels, attend(): pl.pallas_call(functools.partial(attend_kernel, shards), out_shape=(jax.S...  7.13 us
    pallas_call x3, Pallas kernels, expand(): pl.pallas_call(functools.partial(expand_kernel, tuple(order), images), ou...  5.8 us
    pallas_call x1, Pallas kernels, finish(): pl.pallas_call(functools.partial(finish_kernel, total), out_shape=(jax.Sh...  2.15 us
    pallas_call x1, Pallas kernels, pick(): pl.pallas_call(functools.partial(pick_kernel, pieces), out_shape=tuple((j...  2.07 us
  transfers between devices with their start and end apart: 33, of which 13 were waited for; matrix products, arithmetic and copies ran while one was open for 0% of the time, Pallas kernels for 16%

profile of v4, /device:TPU:0, one launch (start us, length us, event | category | flops | bytes accessed | tf_op | source)
XLA Modules:
  0.0 79.4 jit_solution(17136593389653541086)
XLA Ops:
  0.7 2.1 %pick.1 = (bf16[64,768]{1,0:T(8,128)(2,1)S(1)}, bf16[64,768]{1,0:T(8,128)(2,1)S(1)}, bf16[64,768]{1,0:T(8,128)(2,1)S(1)}, bf16[1,3,1152]{2,1,0:T(4,128)(2,1)S(1)...) custom-call(s32[16]{0:T(128)} %sel_hbm.1, s32[16]{0:T(128)} %dest_hbm.1, bf16[16,64,768]{2,1,0:T(8,128)(2,1)} %pixels_ref.1, ...), custom_call_target="tpu_custom_call" | custom-call | tf_op jit(solution)/shard_map/pick/pallas_call | solution.py:170
  2.7 3.0 %collective-permute-start.12 = (bf16[128,1024]{1,0:T(8,128)(2,1)S(1)}, bf16[128,1024]{1,0:T(8,128)(2,1)S(1)}, u32[]{:S(2)}, u32[]{:S(2)}) collective-permute-start(bf16[128,1024]{1,0:T(8,128)(2,1)S(1)} %get-tuple-element.23), channel_id=1, source_target_pairs={{0,2},{1,3},{2,0},{3,1},{4,6},{5,7},{6,4},{7,5},{8,10},{9,11},{10,... | collective-permute-start | bytes 786440 | tf_op jit(solution)/shard_map/ppermute | solution.py:50
  5.8 6.3 %collective-permute-done.12.refs_0_ = bf16[128,1024]{1,0:T(8,128)(2,1)S(1)} collective-permute-done((bf16[128,1024]{1,0:T(8,128)(2,1)S(1)}, bf16[128,1024]{1,0:T(8,128)(2,1)S(1)}, u32[]{:S(2)}, u32[]{:S(2)}) %collective-permute-start.12) | collective-permute-done | bytes 262176 | tf_op jit(solution)/shard_map/ppermute | solution.py:50
  12.1 1.8 %collective-permute-start.13 = (bf16[128,1024]{1,0:T(8,128)(2,1)S(1)}, bf16[128,1024]{1,0:T(8,128)(2,1)S(1)}, u32[]{:S(2)}, u32[]{:S(2)}) collective-permute-start(bf16[128,1024]{1,0:T(8,128)(2,1)S(1)} %collective-permute-done.12.refs_0_), channel_id=1, source_target_pairs={{0,4},{4,0},{8,12},{12,8},{16,20},{20,16},{24,28},{28,24},{1,5},{5... | collective-permute-start | bytes 786440 | tf_op jit(solution)/shard_map/ppermute | solution.py:50
  13.8 1.5 %collective-permute-start.22 = (bf16[64,768]{1,0:T(8,128)(2,1)S(1)}, bf16[64,768]{1,0:T(8,128)(2,1)S(1)}, u32[]{:S(2)}, u32[]{:S(2)}) collective-permute-start(bf16[64,768]{1,0:T(8,128)(2,1)S(1)} %get-tuple-element.27.refs_0_), channel_id=1, source_target_pairs={{0,2},{1,3},{2,0},{3,1},{4,6},{5,7},{6,4},{7,5},{8,10},{9,11},{10,... | collective-permute-start | bytes 294920 | tf_op jit(solution)/shard_map/ppermute | solution.py:50
  15.3 0.5 collective-permute-start.6
  15.9 1.5 %collective-permute-start.16 = (bf16[64,768]{1,0:T(8,128)(2,1)S(1)}, bf16[64,768]{1,0:T(8,128)(2,1)S(1)}, u32[]{:S(2)}, u32[]{:S(2)}) collective-permute-start(bf16[64,768]{1,0:T(8,128)(2,1)S(1)} %get-tuple-element.24.refs_0_), channel_id=1, source_target_pairs={{0,2},{1,3},{2,0},{3,1},{4,6},{5,7},{6,4},{7,5},{8,10},{9,11},{10,... | collective-permute-start | bytes 294920 | tf_op jit(solution)/shard_map/ppermute | solution.py:50
  17.4 1.4 %collective-permute-done.22.refs_1_ = bf16[64,768]{1,0:T(8,128)(2,1)S(1)} collective-permute-done((bf16[64,768]{1,0:T(8,128)(2,1)S(1)}, bf16[64,768]{1,0:T(8,128)(2,1)S(1)}, u32[]{:S(2)}, u32[]{:S(2)}) %collective-permute-start.22) | collective-permute-done | bytes 98336 | tf_op jit(solution)/shard_map/ppermute | solution.py:50
  18.8 0.5 collective-permute-start.7
  19.3 3.1 %collective-permute-done.16.refs_1_ = bf16[64,768]{1,0:T(8,128)(2,1)S(1)} collective-permute-done((bf16[64,768]{1,0:T(8,128)(2,1)S(1)}, bf16[64,768]{1,0:T(8,128)(2,1)S(1)}, u32[]{:S(2)}, u32[]{:S(2)}) %collective-permute-start.16) | collective-permute-done | bytes 98336 | tf_op jit(solution)/shard_map/ppermute | solution.py:50
  22.4 0.5 collective-permute-start.8
  22.9 0.1 collective-permute-start.24
  23.0 0.7 collective-permute-done.17.refs_2_
  23.7 0.2 collective-permute-start.15
  23.9 1.3 %collective-permute-start.3 = (bf16[64,768]{1,0:T(8,128)(2,1)S(1)}, bf16[64,768]{1,0:T(8,128)(2,1)S(1)}, u32[]{:S(2)}, u32[]{:S(2)}) collective-permute-start(bf16[64,768]{1,0:T(8,128)(2,1)S(1)} %get-tuple-element.19.refs_0_), channel_id=1, source_target_pairs={{0,2},{1,3},{2,0},{3,1},{4,6},{5,7},{6,4},{7,5},{8,10},{9,11},{10,... | collective-permute-start | bytes 294920 | tf_op jit(solution)/shard_map/ppermute | solution.py:50
  25.2 0.5 collective-permute-start.18
  25.6 1.4 %load.1.qkv_ref = bf16[3,1024,256]{2,1,0:T(8,128)(2,1)S(1)} custom-call(bf16[3,1024,256]{2,1,0:T(8,128)(2,1)} %source_ref.1), custom_call_target="tpu_custom_call" | custom-call | tf_op jit(solution)/shard_map/load/pallas_call | solution.py:204
  27.1 2.4 %shard_map.146 = (f32[256,1024]{1,0:T(8,128)S(1)}, bf16[256,256]{1,0:T(8,128)(2,1)S(1)}) custom-call(f32[3,1024]{1,0:T(4,128)S(1)} %copy-done.5, bf16[768,1024]{1,0:T(8,128)(2,1)S(1)} %copy-done.1, bf16[3,1024,256]{2,1,0:T(8,128)(2,1)S(1)} %load.1.qkv_ref, bf16[64,768]{1,0:T(8,128)(2,1)S(1)} %get-tuple-element.27.refs_0_, ...), custom_call_target="tpu_custom_call" | custom-call | tf_op jit(solution)/shard_map/pallas_call | solution.py:320
  29.5 0.8 %collective-permute-start.25 = (bf16[256,256]{1,0:T(8,128)(2,1)S(1)}, bf16[256,256]{1,0:T(8,128)(2,1)S(1)}, u32[]{:S(2)}, u32[]{:S(2)}) collective-permute-start(bf16[256,256]{1,0:T(8,128)(2,1)S(1)} %get-tuple-element.29.refs_0_), channel_id=1, source_target_pairs={{0,2},{1,3},{2,0},{3,1},{4,6},{5,7},{6,4},{7,5},{8,10},{9,11},{10,... | collective-permute-start | bytes 393224 | tf_op jit(solution)/shard_map/ppermute | solution.py:50
  30.3 0.5 collective-permute-start.5
  30.8 2.4 %shard_map.144 = (f32[256,1024]{1,0:T(8,128)S(1)}, bf16[256,256]{1,0:T(8,128)(2,1)S(1)}) custom-call(f32[3,1024]{1,0:T(4,128)S(1)} %copy-done.5, bf16[768,1024]{1,0:T(8,128)(2,1)S(1)} %copy-done.1, bf16[3,1024,256]{2,1,0:T(8,128)(2,1)S(1)} %load.1.qkv_ref, bf16[64,768]{1,0:T(8,128)(2,1)S(1)} %get-tuple-element.24.refs_0_, ...), custom_call_target="tpu_custom_call" | custom-call | tf_op jit(solution)/shard_map/pallas_call | solution.py:320
  33.2 1.3 %collective-permute-start.19 = (bf16[256,256]{1,0:T(8,128)(2,1)S(1)}, bf16[256,256]{1,0:T(8,128)(2,1)S(1)}, u32[]{:S(2)}, u32[]{:S(2)}) collective-permute-start(bf16[256,256]{1,0:T(8,128)(2,1)S(1)} %get-tuple-element.26.refs_0_), channel_id=1, source_target_pairs={{0,2},{1,3},{2,0},{3,1},{4,6},{5,7},{6,4},{7,5},{8,10},{9,11},{10,... | collective-permute-start | bytes 393224 | tf_op jit(solution)/shard_map/ppermute | solution.py:50
  34.5 2.4 %shard_map.142 = (f32[256,1024]{1,0:T(8,128)S(1)}, bf16[256,256]{1,0:T(8,128)(2,1)S(1)}) custom-call(f32[3,1024]{1,0:T(4,128)S(1)} %copy-done.5, bf16[768,1024]{1,0:T(8,128)(2,1)S(1)} %copy-done.1, bf16[3,1024,256]{2,1,0:T(8,128)(2,1)S(1)} %load.1.qkv_ref, bf16[64,768]{1,0:T(8,128)(2,1)S(1)} %get-tuple-element.19.refs_0_, ...), custom_call_target="tpu_custom_call" | custom-call | tf_op jit(solution)/shard_map/pallas_call | solution.py:320
  36.9 0.8 %collective-permute-start.9 = (bf16[256,256]{1,0:T(8,128)(2,1)S(1)}, bf16[256,256]{1,0:T(8,128)(2,1)S(1)}, u32[]{:S(2)}, u32[]{:S(2)}) collective-permute-start(bf16[256,256]{1,0:T(8,128)(2,1)S(1)} %get-tuple-element.22.refs_0_), channel_id=1, source_target_pairs={{0,2},{1,3},{2,0},{3,1},{4,6},{5,7},{6,4},{7,5},{8,10},{9,11},{10,... | collective-permute-start | bytes 393224 | tf_op jit(solution)/shard_map/ppermute | solution.py:50
  37.7 1.0 %collective-permute-done.19.refs_1_ = bf16[256,256]{1,0:T(8,128)(2,1)S(1)} collective-permute-done((bf16[256,256]{1,0:T(8,128)(2,1)S(1)}, bf16[256,256]{1,0:T(8,128)(2,1)S(1)}, u32[]{:S(2)}, u32[]{:S(2)}) %collective-permute-start.19) | collective-permute-done | bytes 131104 | tf_op jit(solution)/shard_map/ppermute | solution.py:50
  38.7 3.4 %collective-permute-done.9.refs_1_ = bf16[256,256]{1,0:T(8,128)(2,1)S(1)} collective-permute-done((bf16[256,256]{1,0:T(8,128)(2,1)S(1)}, bf16[256,256]{1,0:T(8,128)(2,1)S(1)}, u32[]{:S(2)}, u32[]{:S(2)}) %collective-permute-start.9) | collective-permute-done | bytes 131104 | tf_op jit(solution)/shard_map/ppermute | solution.py:50
  42.1 0.5 collective-permute-start.10
  42.7 1.9 %shard_map.147.refs_2_ = f32[2,1024]{1,0:T(2,128)S(1)} custom-call(f32[3,1024]{1,0:T(4,128)S(1)} %copy-done.5, bf16[1024,1024]{1,0:T(8,128)(2,1)S(1)} %copy-done, f32[256,1024]{1,0:T(8,128)S(1)} %get-tuple-element.28.hidden_ref, bf16[256,256]{1,0:T(8,128)(2,1)S(1)} %get-tuple-element.29.refs_0_, bf16[256,256]{1,0:T(8,128)(2,1)S(1)} %collective-permute-done.25.refs_1_, ...), custom_call_target="tpu_custom_call" | custom-call | tf_op jit(solution)/shard_map/pallas_call | solution.py:356
  44.7 1.9 %shard_map.145.refs_1_ = f32[2,1024]{1,0:T(2,128)S(1)} custom-call(f32[3,1024]{1,0:T(4,128)S(1)} %copy-done.5, bf16[1024,1024]{1,0:T(8,128)(2,1)S(1)} %copy-done, f32[256,1024]{1,0:T(8,128)S(1)} %get-tuple-element.25.hidden_ref, bf16[256,256]{1,0:T(8,128)(2,1)S(1)} %get-tuple-element.26.refs_0_, bf16[256,256]{1,0:T(8,128)(2,1)S(1)} %collective-permute-done.19.refs_1_, ...), custom_call_target="tpu_custom_call" | custom-call | tf_op jit(solution)/shard_map/pallas_call | solution.py:356
  46.7 1.9 %shard_map.143.refs_0_ = f32[2,1024]{1,0:T(2,128)S(1)} custom-call(f32[3,1024]{1,0:T(4,128)S(1)} %copy-done.5, bf16[1024,1024]{1,0:T(8,128)(2,1)S(1)} %copy-done, f32[256,1024]{1,0:T(8,128)S(1)} %get-tuple-element.21.hidden_ref, bf16[256,256]{1,0:T(8,128)(2,1)S(1)} %get-tuple-element.22.refs_0_, bf16[256,256]{1,0:T(8,128)(2,1)S(1)} %collective-permute-done.9.refs_1_, ...), custom_call_target="tpu_custom_call" | custom-call | tf_op jit(solution)/shard_map/pallas_call | solution.py:356
  48.6 0.4 reduce.1.own_ref
  49.0 0.4 collective-permute-start.28
  49.5 0.8 %collective-permute-done.28.other_ref = f32[3,1024]{1,0:T(4,128)S(1)} collective-permute-done((f32[3,1024]{1,0:T(4,128)S(1)}, f32[3,1024]{1,0:T(4,128)S(1)}, u32[]{:S(2)}, u32[]{:S(2)}) %collective-permute-start.28) | collective-permute-done | bytes 12320 | tf_op jit(solution)/shard_map/ppermute | solution.py:50
  50.3 0.8 collective-permute-start.29
  51.1 3.0 %collective-permute-done.29.other_ref = f32[3,1024]{1,0:T(4,128)S(1)} collective-permute-done((f32[3,1024]{1,0:T(4,128)S(1)}, f32[3,1024]{1,0:T(4,128)S(1)}, u32[]{:S(2)}, u32[]{:S(2)}) %collective-permute-start.29) | collective-permute-done | bytes 12320 | tf_op jit(solution)/shard_map/ppermute | solution.py:50
  54.1 0.5 collective-permute-start.30
  54.6 3.2 %collective-permute-done.30.other_ref = f32[1,3,1024]{2,1,0:T(4,128)S(1)} collective-permute-done((f32[1,3,1024]{2,1,0:T(4,128)S(1)}, f32[1,3,1024]{2,1,0:T(4,128)S(1)}, u32[]{:S(2)}, u32[]{:S(2)}) %collective-permute-start.30) | collective-permute-done | bytes 12320 | tf_op jit(solution)/shard_map/ppermute | solution.py:50
  57.8 1.6 %collective-permute-start.31 = (f32[2,3,1024]{2,1,0:T(4,128)S(1)}, f32[2,3,1024]{2,1,0:T(4,128)S(1)}, u32[]{:S(2)}, u32[]{:S(2)}) collective-permute-start(f32[2,3,1024]{2,1,0:T(4,128)S(1)} %shard_map.148.own_ref), channel_id=1, source_target_pairs={{0,8},{4,12},{8,0},{12,4},{16,24},{20,28},{24,16},{28,20},{1,9},{5... | collective-permute-start | bytes 73736 | tf_op jit(solution)/shard_map/ppermute | solution.py:50
  59.4 2.3 %collective-permute-done.31.other_ref = f32[2,3,1024]{2,1,0:T(4,128)S(1)} collective-permute-done((f32[2,3,1024]{2,1,0:T(4,128)S(1)}, f32[2,3,1024]{2,1,0:T(4,128)S(1)}, u32[]{:S(2)}, u32[]{:S(2)}) %collective-permute-start.31) | collective-permute-done | bytes 24608 | tf_op jit(solution)/shard_map/ppermute | solution.py:50
  61.7 2.9 %collective-permute-start.32 = (f32[4,3,1024]{2,1,0:T(4,128)S(1)}, f32[4,3,1024]{2,1,0:T(4,128)S(1)}, u32[]{:S(2)}, u32[]{:S(2)}) collective-permute-start(f32[4,3,1024]{2,1,0:T(4,128)S(1)} %shard_map.149.first_ref), channel_id=1, source_target_pairs={{0,16},{4,20},{8,24},{12,28},{16,0},{20,4},{24,8},{28,12},{1,17},{... | collective-permute-start | bytes 147464 | tf_op jit(solution)/shard_map/ppermute | solution.py:50
  64.7 0.5 collective-permute-start
  65.2 3.2 %collective-permute-done.other_ref = bf16[1,3,1152]{2,1,0:T(4,128)(2,1)S(1)} collective-permute-done((bf16[1,3,1152]{2,1,0:T(4,128)(2,1)S(1)}, bf16[1,3,1152]{2,1,0:T(4,128)(2,1)S(1)}, u32[]{:S(2)}, u32[]{:S(2)}) %collective-permute-start) | collective-permute-done | bytes 6944 | tf_op jit(solution)/shard_map/ppermute | solution.py:50
  68.3 1.2 %collective-permute-start.1 = (bf16[2,3,1152]{2,1,0:T(4,128)(2,1)S(1)}, bf16[2,3,1152]{2,1,0:T(4,128)(2,1)S(1)}, u32[]{:S(2)}, u32[]{:S(2)}) collective-permute-start(bf16[2,3,1152]{2,1,0:T(4,128)(2,1)S(1)} %shard_map.140.own_ref), channel_id=1, source_target_pairs={{0,8},{4,12},{8,0},{12,4},{16,24},{20,28},{24,16},{28,20},{1,9},{5... | collective-permute-start | bytes 41480 | tf_op jit(solution)/shard_map/ppermute | solution.py:50
  69.5 2.5 %collective-permute-done.1.other_ref = bf16[2,3,1152]{2,1,0:T(4,128)(2,1)S(1)} collective-permute-done((bf16[2,3,1152]{2,1,0:T(4,128)(2,1)S(1)}, bf16[2,3,1152]{2,1,0:T(4,128)(2,1)S(1)}, u32[]{:S(2)}, u32[]{:S(2)}) %collective-permute-start.1) | collective-permute-done | bytes 13856 | tf_op jit(solution)/shard_map/ppermute | solution.py:50
  72.1 0.1 collective-permute-start.2
  72.2 4.8 %collective-permute-done.2.second_ref = bf16[4,3,1152]{2,1,0:T(4,128)(2,1)S(1)} collective-permute-done((bf16[4,3,1152]{2,1,0:T(4,128)(2,1)S(1)}, bf16[4,3,1152]{2,1,0:T(4,128)(2,1)S(1)}, u32[]{:S(2)}, u32[]{:S(2)}) %collective-permute-start.2) | collective-permute-done | bytes 27680 | tf_op jit(solution)/shard_map/ppermute | solution.py:50
  77.0 0.2 route.1
  77.3 2.2 %finish.1 = (f32[4,1024]{1,0:T(4,128)}, f32[4]{0:T(128)}) custom-call(f32[2]{0:T(128)S(1)} %copy-done.6, f32[3,1024]{1,0:T(4,128)S(1)} %copy-done.5, bf16[1024,1024]{1,0:T(8,128)(2,1)S(1)} %copy-done.3, f32[24,1024]{1,0:T(8,128)S(1)} %get-tuple-element.17.cap_ref, f32[24,128]{1,0:T(8,128)S(1)} %get-tuple-element.18.meta_ref, ...), custom_call_target="tpu_custom_call" | custom-call | tf_op jit(solution)/shard_map/finish/pallas_call | solution.py:423
  (52 shorter events, 0.3 us)
Async XLA Ops:
  0.6 14.7 %copy-start.7 = (bf16[64,1024]{1,0:T(8,128)(2,1)S(1)}, bf16[64,1024]{1,0:T(8,128)(2,1)}, u32[]{:S(2)}) copy-start(bf16[64,1024]{1,0:T(8,128)(2,1)} %pos_hbm.1) | copy-start | bytes 393220
  0.6 18.2 %copy-start.2 = (bf16[256,1024]{1,0:T(8,128)(2,1)S(1)}, bf16[256,1024]{1,0:T(8,128)(2,1)}, u32[]{:S(2)}) copy-start(bf16[256,1024]{1,0:T(8,128)(2,1)} %refs_4_.5) | copy-start | bytes 1572868
  2.7 9.3 %collective-permute-start.12 = (bf16[128,1024]{1,0:T(8,128)(2,1)S(1)}, bf16[128,1024]{1,0:T(8,128)(2,1)S(1)}, u32[]{:S(2)}, u32[]{:S(2)}) collective-permute-start(bf16[128,1024]{1,0:T(8,128)(2,1)S(1)} %get-tuple-element.23), channel_id=1, source_target_pairs={{0,2},{1,3},{2,0},{3,1},{4,6},{5,7},{6,4},{7,5},{8,10},{9,11},{10,... | collective-permute-start | bytes 786440 | tf_op jit(solution)/shard_map/ppermute | solution.py:50
  12.1 10.9 %collective-permute-start.13 = (bf16[128,1024]{1,0:T(8,128)(2,1)S(1)}, bf16[128,1024]{1,0:T(8,128)(2,1)S(1)}, u32[]{:S(2)}, u32[]{:S(2)}) collective-permute-start(bf16[128,1024]{1,0:T(8,128)(2,1)S(1)} %collective-permute-done.12.refs_0_), channel_id=1, source_target_pairs={{0,4},{4,0},{8,12},{12,8},{16,20},{20,16},{24,28},{28,24},{1,5},{5... | collective-permute-start | bytes 786440 | tf_op jit(solution)/shard_map/ppermute | solution.py:50
  13.8 5.0 %collective-permute-start.22 = (bf16[64,768]{1,0:T(8,128)(2,1)S(1)}, bf16[64,768]{1,0:T(8,128)(2,1)S(1)}, u32[]{:S(2)}, u32[]{:S(2)}) collective-permute-start(bf16[64,768]{1,0:T(8,128)(2,1)S(1)} %get-tuple-element.27.refs_0_), channel_id=1, source_target_pairs={{0,2},{1,3},{2,0},{3,1},{4,6},{5,7},{6,4},{7,5},{8,10},{9,11},{10,... | collective-permute-start | bytes 294920 | tf_op jit(solution)/shard_map/ppermute | solution.py:50
  15.3 7.1 %collective-permute-start.6 = (bf16[64,1024]{1,0:T(8,128)(2,1)S(1)}, bf16[64,1024]{1,0:T(8,128)(2,1)S(1)}, u32[]{:S(2)}, u32[]{:S(2)}) collective-permute-start(bf16[64,1024]{1,0:T(8,128)(2,1)S(1)} %copy-done.7), channel_id=1, source_target_pairs={{0,2},{1,3},{2,0},{3,1},{4,6},{5,7},{6,4},{7,5},{8,10},{9,11},{10,... | collective-permute-start | bytes 393224 | tf_op jit(solution)/shard_map/ppermute | solution.py:50
  15.9 2.9 %collective-permute-start.23 = (bf16[64,768]{1,0:T(8,128)(2,1)S(1)}, bf16[64,768]{1,0:T(8,128)(2,1)S(1)}, u32[]{:S(2)}, u32[]{:S(2)}) collective-permute-start(bf16[64,768]{1,0:T(8,128)(2,1)S(1)} %get-tuple-element.27.refs_0_), channel_id=1, source_target_pairs={{0,1},{1,0},{2,3},{3,2},{4,5},{5,4},{6,7},{7,6},{8,9},{9,8},{10,11... | collective-permute-start | bytes 294920 | tf_op jit(solution)/shard_map/ppermute | solution.py:50
  15.9 6.5 %collective-permute-start.16 = (bf16[64,768]{1,0:T(8,128)(2,1)S(1)}, bf16[64,768]{1,0:T(8,128)(2,1)S(1)}, u32[]{:S(2)}, u32[]{:S(2)}) collective-permute-start(bf16[64,768]{1,0:T(8,128)(2,1)S(1)} %get-tuple-element.24.refs_0_), channel_id=1, source_target_pairs={{0,2},{1,3},{2,0},{3,1},{4,6},{5,7},{6,4},{7,5},{8,10},{9,11},{10,... | collective-permute-start | bytes 294920 | tf_op jit(solution)/shard_map/ppermute | solution.py:50
  18.8 23.9 %collective-permute-start.14 = (bf16[256,1024]{1,0:T(8,128)(2,1)S(1)}, bf16[256,1024]{1,0:T(8,128)(2,1)S(1)}, u32[]{:S(2)}, u32[]{:S(2)}) collective-permute-start(bf16[256,1024]{1,0:T(8,128)(2,1)S(1)} %copy-done.2), channel_id=1, source_target_pairs={{0,1},{1,0},{2,3},{3,2},{4,5},{5,4},{6,7},{7,6},{8,9},{9,8},{10,11... | collective-permute-start | bytes 1572872 | tf_op jit(solution)/shard_map/ppermute | solution.py:50
  18.8 5.1 %collective-permute-start.7 = (bf16[64,1024]{1,0:T(8,128)(2,1)S(1)}, bf16[64,1024]{1,0:T(8,128)(2,1)S(1)}, u32[]{:S(2)}, u32[]{:S(2)}) collective-permute-start(bf16[64,1024]{1,0:T(8,128)(2,1)S(1)} %copy-done.7), channel_id=1, source_target_pairs={{0,1},{1,0},{2,3},{3,2},{4,5},{5,4},{6,7},{7,6},{8,9},{9,8},{10,11... | collective-permute-start | bytes 393224 | tf_op jit(solution)/shard_map/ppermute | solution.py:50
  22.4 1.3 %collective-permute-start.17 = (bf16[64,768]{1,0:T(8,128)(2,1)S(1)}, bf16[64,768]{1,0:T(8,128)(2,1)S(1)}, u32[]{:S(2)}, u32[]{:S(2)}) collective-permute-start(bf16[64,768]{1,0:T(8,128)(2,1)S(1)} %get-tuple-element.24.refs_0_), channel_id=1, source_target_pairs={{0,1},{1,0},{2,3},{3,2},{4,5},{5,4},{6,7},{7,6},{8,9},{9,8},{10,11... | collective-permute-start | bytes 294920 | tf_op jit(solution)/shard_map/ppermute | solution.py:50
  22.4 2.8 %collective-permute-start.8 = (bf16[64,1024]{1,0:T(8,128)(2,1)S(1)}, bf16[64,1024]{1,0:T(8,128)(2,1)S(1)}, u32[]{:S(2)}, u32[]{:S(2)}) collective-permute-start(bf16[64,1024]{1,0:T(8,128)(2,1)S(1)} %collective-permute-done.6.refs_5_), channel_id=1, source_target_pairs={{0,1},{1,0},{2,3},{3,2},{4,5},{5,4},{6,7},{7,6},{8,9},{9,8},{10,11... | collective-permute-start | bytes 393224 | tf_op jit(solution)/shard_map/ppermute | solution.py:50
  22.9 2.2 %collective-permute-start.24 = (bf16[64,768]{1,0:T(8,128)(2,1)S(1)}, bf16[64,768]{1,0:T(8,128)(2,1)S(1)}, u32[]{:S(2)}, u32[]{:S(2)}) collective-permute-start(bf16[64,768]{1,0:T(8,128)(2,1)S(1)} %collective-permute-done.22.refs_1_), channel_id=1, source_target_pairs={{0,1},{1,0},{2,3},{3,2},{4,5},{5,4},{6,7},{7,6},{8,9},{9,8},{10,11... | collective-permute-start | bytes 294920 | tf_op jit(solution)/shard_map/ppermute | solution.py:50
  23.7 19.0 %collective-permute-start.15 = (bf16[256,1024]{1,0:T(8,128)(2,1)S(1)}, bf16[256,1024]{1,0:T(8,128)(2,1)S(1)}, u32[]{:S(2)}, u32[]{:S(2)}) collective-permute-start(bf16[256,1024]{1,0:T(8,128)(2,1)S(1)} %assemble.1.refs_5_), channel_id=1, source_target_pairs={{0,1},{1,0},{2,3},{3,2},{4,5},{5,4},{6,7},{7,6},{8,9},{9,8},{10,11... | collective-permute-start | bytes 1572872 | tf_op jit(solution)/shard_map/ppermute | solution.py:50
  23.9 3.2 %copy-start.1 = (bf16[768,1024]{1,0:T(8,128)(2,1)S(1)}, bf16[768,1024]{1,0:T(8,128)(2,1)}, u32[]{:S(2)}) copy-start(bf16[768,1024]{1,0:T(8,128)(2,1)} %patch_ref.5) | copy-start | bytes 4718596
  23.9 3.2 %copy-start.5 = (f32[3,1024]{1,0:T(4,128)S(1)}, f32[3,1024]{1,0:T(4,128)}, u32[]{:S(2)}) copy-start(f32[3,1024]{1,0:T(4,128)} %gains_ref.13) | copy-start | bytes 36868
  23.9 5.6 %collective-permute-start.3 = (bf16[64,768]{1,0:T(8,128)(2,1)S(1)}, bf16[64,768]{1,0:T(8,128)(2,1)S(1)}, u32[]{:S(2)}, u32[]{:S(2)}) collective-permute-start(bf16[64,768]{1,0:T(8,128)(2,1)S(1)} %get-tuple-element.19.refs_0_), channel_id=1, source_target_pairs={{0,2},{1,3},{2,0},{3,1},{4,6},{5,7},{6,4},{7,5},{8,10},{9,11},{10,... | collective-permute-start | bytes 294920 | tf_op jit(solution)/shard_map/ppermute | solution.py:50
  25.1 5.2 %collective-permute-start.4 = (bf16[64,768]{1,0:T(8,128)(2,1)S(1)}, bf16[64,768]{1,0:T(8,128)(2,1)S(1)}, u32[]{:S(2)}, u32[]{:S(2)}) collective-permute-start(bf16[64,768]{1,0:T(8,128)(2,1)S(1)} %get-tuple-element.19.refs_0_), channel_id=1, source_target_pairs={{0,1},{1,0},{2,3},{3,2},{4,5},{5,4},{6,7},{7,6},{8,9},{9,8},{10,11... | collective-permute-start | bytes 294920 | tf_op jit(solution)/shard_map/ppermute | solution.py:50
  25.2 5.1 %collective-permute-start.18 = (bf16[64,768]{1,0:T(8,128)(2,1)S(1)}, bf16[64,768]{1,0:T(8,128)(2,1)S(1)}, u32[]{:S(2)}, u32[]{:S(2)}) collective-permute-start(bf16[64,768]{1,0:T(8,128)(2,1)S(1)} %collective-permute-done.16.refs_1_), channel_id=1, source_target_pairs={{0,1},{1,0},{2,3},{3,2},{4,5},{5,4},{6,7},{7,6},{8,9},{9,8},{10,11... | collective-permute-start | bytes 294920 | tf_op jit(solution)/shard_map/ppermute | solution.py:50
  29.5 7.4 %collective-permute-start.25 = (bf16[256,256]{1,0:T(8,128)(2,1)S(1)}, bf16[256,256]{1,0:T(8,128)(2,1)S(1)}, u32[]{:S(2)}, u32[]{:S(2)}) collective-permute-start(bf16[256,256]{1,0:T(8,128)(2,1)S(1)} %get-tuple-element.29.refs_0_), channel_id=1, source_target_pairs={{0,2},{1,3},{2,0},{3,1},{4,6},{5,7},{6,4},{7,5},{8,10},{9,11},{10,... | collective-permute-start | bytes 393224 | tf_op jit(solution)/shard_map/ppermute | solution.py:50
  30.3 7.4 %collective-permute-start.26 = (bf16[256,256]{1,0:T(8,128)(2,1)S(1)}, bf16[256,256]{1,0:T(8,128)(2,1)S(1)}, u32[]{:S(2)}, u32[]{:S(2)}) collective-permute-start(bf16[256,256]{1,0:T(8,128)(2,1)S(1)} %get-tuple-element.29.refs_0_), channel_id=1, source_target_pairs={{0,1},{1,0},{2,3},{3,2},{4,5},{5,4},{6,7},{7,6},{8,9},{9,8},{10,11... | collective-permute-start | bytes 393224 | tf_op jit(solution)/shard_map/ppermute | solution.py:50
  30.3 2.9 %collective-permute-start.5 = (bf16[64,768]{1,0:T(8,128)(2,1)S(1)}, bf16[64,768]{1,0:T(8,128)(2,1)S(1)}, u32[]{:S(2)}, u32[]{:S(2)}) collective-permute-start(bf16[64,768]{1,0:T(8,128)(2,1)S(1)} %collective-permute-done.3.refs_1_), channel_id=1, source_target_pairs={{0,1},{1,0},{2,3},{3,2},{4,5},{5,4},{6,7},{7,6},{8,9},{9,8},{10,11... | collective-permute-start | bytes 294920 | tf_op jit(solution)/shard_map/ppermute | solution.py:50
  33.2 9.5 %copy-start = (bf16[1024,1024]{1,0:T(8,128)(2,1)S(1)}, bf16[1024,1024]{1,0:T(8,128)(2,1)}, u32[]{:S(2)}) copy-start(bf16[1024,1024]{1,0:T(8,128)(2,1)} %up_ref.5) | copy-start | bytes 6291460
  33.2 5.5 %collective-permute-start.19 = (bf16[256,256]{1,0:T(8,128)(2,1)S(1)}, bf16[256,256]{1,0:T(8,128)(2,1)S(1)}, u32[]{:S(2)}, u32[]{:S(2)}) collective-permute-start(bf16[256,256]{1,0:T(8,128)(2,1)S(1)} %get-tuple-element.26.refs_0_), channel_id=1, source_target_pairs={{0,2},{1,3},{2,0},{3,1},{4,6},{5,7},{6,4},{7,5},{8,10},{9,11},{10,... | collective-permute-start | bytes 393224 | tf_op jit(solution)/shard_map/ppermute | solution.py:50
  36.9 5.2 %collective-permute-start.9 = (bf16[256,256]{1,0:T(8,128)(2,1)S(1)}, bf16[256,256]{1,0:T(8,128)(2,1)S(1)}, u32[]{:S(2)}, u32[]{:S(2)}) collective-permute-start(bf16[256,256]{1,0:T(8,128)(2,1)S(1)} %get-tuple-element.22.refs_0_), channel_id=1, source_target_pairs={{0,2},{1,3},{2,0},{3,1},{4,6},{5,7},{6,4},{7,5},{8,10},{9,11},{10,... | collective-permute-start | bytes 393224 | tf_op jit(solution)/shard_map/ppermute | solution.py:50
  37.7 4.4 %collective-permute-start.27 = (bf16[256,256]{1,0:T(8,128)(2,1)S(1)}, bf16[256,256]{1,0:T(8,128)(2,1)S(1)}, u32[]{:S(2)}, u32[]{:S(2)}) collective-permute-start(bf16[256,256]{1,0:T(8,128)(2,1)S(1)} %collective-permute-done.25.refs_1_), channel_id=1, source_target_pairs={{0,1},{1,0},{2,3},{3,2},{4,5},{5,4},{6,7},{7,6},{8,9},{9,8},{10,11... | collective-permute-start | bytes 393224 | tf_op jit(solution)/shard_map/ppermute | solution.py:50
  38.7 5.9 %collective-permute-start.20 = (bf16[256,256]{1,0:T(8,128)(2,1)S(1)}, bf16[256,256]{1,0:T(8,128)(2,1)S(1)}, u32[]{:S(2)}, u32[]{:S(2)}) collective-permute-start(bf16[256,256]{1,0:T(8,128)(2,1)S(1)} %get-tuple-element.26.refs_0_), channel_id=1, source_target_pairs={{0,1},{1,0},{2,3},{3,2},{4,5},{5,4},{6,7},{7,6},{8,9},{9,8},{10,11... | collective-permute-start | bytes 393224 | tf_op jit(solution)/shard_map/ppermute | solution.py:50
  42.1 2.5 %collective-permute-start.21 = (bf16[256,256]{1,0:T(8,128)(2,1)S(1)}, bf16[256,256]{1,0:T(8,128)(2,1)S(1)}, u32[]{:S(2)}, u32[]{:S(2)}) collective-permute-start(bf16[256,256]{1,0:T(8,128)(2,1)S(1)} %collective-permute-done.19.refs_1_), channel_id=1, source_target_pairs={{0,1},{1,0},{2,3},{3,2},{4,5},{5,4},{6,7},{7,6},{8,9},{9,8},{10,11... | collective-permute-start | bytes 393224 | tf_op jit(solution)/shard_map/ppermute | solution.py:50
  42.1 4.5 %collective-permute-start.10 = (bf16[256,256]{1,0:T(8,128)(2,1)S(1)}, bf16[256,256]{1,0:T(8,128)(2,1)S(1)}, u32[]{:S(2)}, u32[]{:S(2)}) collective-permute-start(bf16[256,256]{1,0:T(8,128)(2,1)S(1)} %get-tuple-element.22.refs_0_), channel_id=1, source_target_pairs={{0,1},{1,0},{2,3},{3,2},{4,5},{5,4},{6,7},{7,6},{8,9},{9,8},{10,11... | collective-permute-start | bytes 393224 | tf_op jit(solution)/shard_map/ppermute | solution.py:50
  42.7 4.0 %collective-permute-start.11 = (bf16[256,256]{1,0:T(8,128)(2,1)S(1)}, bf16[256,256]{1,0:T(8,128)(2,1)S(1)}, u32[]{:S(2)}, u32[]{:S(2)}) collective-permute-start(bf16[256,256]{1,0:T(8,128)(2,1)S(1)} %collective-permute-done.9.refs_1_), channel_id=1, source_target_pairs={{0,1},{1,0},{2,3},{3,2},{4,5},{5,4},{6,7},{7,6},{8,9},{9,8},{10,11... | collective-permute-start | bytes 393224 | tf_op jit(solution)/shard_map/ppermute | solution.py:50
  46.6 2.0 %copy-start.4 = (bf16[1024,1024]{1,0:T(8,128)(2,1)S(1)}, bf16[1024,1024]{1,0:T(8,128)(2,1)}, u32[]{:S(2)}) copy-start(bf16[1024,1024]{1,0:T(8,128)(2,1)} %down_ref.1) | copy-start | bytes 6291460
  48.6 28.7 %copy-start.3 = (bf16[1024,1024]{1,0:T(8,128)(2,1)S(1)}, bf16[1024,1024]{1,0:T(8,128)(2,1)}, u32[]{:S(2)}) copy-start(bf16[1024,1024]{1,0:T(8,128)(2,1)} %weight_ref.1) | copy-start | bytes 6291460
  48.6 28.7 %copy-start.6 = (f32[2]{0:T(128)S(1)}, f32[2]{0:T(128)}, u32[]{:S(2)}) copy-start(f32[2]{0:T(128)} %params_ref.1) | copy-start | bytes 28
  49.0 1.3 %collective-permute-start.28 = (f32[3,1024]{1,0:T(4,128)S(1)}, f32[3,1024]{1,0:T(4,128)S(1)}, u32[]{:S(2)}, u32[]{:S(2)}) collective-permute-start(f32[3,1024]{1,0:T(4,128)S(1)} %reduce.1.own_ref), channel_id=1, source_target_pairs={{0,1},{1,0},{2,3},{3,2},{4,5},{5,4},{6,7},{7,6},{8,9},{9,8},{10,11... | collective-permute-start | bytes 36872 | tf_op jit(solution)/shard_map/ppermute | solution.py:50
  50.3 3.7 %collective-permute-start.29 = (f32[3,1024]{1,0:T(4,128)S(1)}, f32[3,1024]{1,0:T(4,128)S(1)}, u32[]{:S(2)}, u32[]{:S(2)}) collective-permute-start(f32[3,1024]{1,0:T(4,128)S(1)} %add.2.own_ref), channel_id=1, source_target_pairs={{0,2},{1,3},{2,0},{3,1},{4,6},{5,7},{6,4},{7,5},{8,10},{9,11},{10,... | collective-permute-start | bytes 36872 | tf_op jit(solution)/shard_map/ppermute | solution.py:50
  54.1 3.7 %collective-permute-start.30 = (f32[1,3,1024]{2,1,0:T(4,128)S(1)}, f32[1,3,1024]{2,1,0:T(4,128)S(1)}, u32[]{:S(2)}, u32[]{:S(2)}) collective-permute-start(f32[1,3,1024]{2,1,0:T(4,128)S(1)} %bitcast.1), channel_id=1, source_target_pairs={{0,4},{4,0},{8,12},{12,8},{16,20},{20,16},{24,28},{28,24},{1,5},{5... | collective-permute-start | bytes 36872 | tf_op jit(solution)/shard_map/ppermute | solution.py:50
  57.8 3.9 %collective-permute-start.31 = (f32[2,3,1024]{2,1,0:T(4,128)S(1)}, f32[2,3,1024]{2,1,0:T(4,128)S(1)}, u32[]{:S(2)}, u32[]{:S(2)}) collective-permute-start(f32[2,3,1024]{2,1,0:T(4,128)S(1)} %shard_map.148.own_ref), channel_id=1, source_target_pairs={{0,8},{4,12},{8,0},{12,4},{16,24},{20,28},{24,16},{28,20},{1,9},{5... | collective-permute-start | bytes 73736 | tf_op jit(solution)/shard_map/ppermute | solution.py:50
  61.7 15.5 %collective-permute-start.32 = (f32[4,3,1024]{2,1,0:T(4,128)S(1)}, f32[4,3,1024]{2,1,0:T(4,128)S(1)}, u32[]{:S(2)}, u32[]{:S(2)}) collective-permute-start(f32[4,3,1024]{2,1,0:T(4,128)S(1)} %shard_map.149.first_ref), channel_id=1, source_target_pairs={{0,16},{4,20},{8,24},{12,28},{16,0},{20,4},{24,8},{28,12},{1,17},{... | collective-permute-start | bytes 147464 | tf_op jit(solution)/shard_map/ppermute | solution.py:50
  64.7 3.7 %collective-permute-start = (bf16[1,3,1152]{2,1,0:T(4,128)(2,1)S(1)}, bf16[1,3,1152]{2,1,0:T(4,128)(2,1)S(1)}, u32[]{:S(2)}, u32[]{:S(2)}) collective-permute-start(bf16[1,3,1152]{2,1,0:T(4,128)(2,1)S(1)} %get-tuple-element.16.own_ref), channel_id=1, source_target_pairs={{0,4},{4,0},{8,12},{12,8},{16,20},{20,16},{24,28},{28,24},{1,5},{5... | collective-permute-start | bytes 20744 | tf_op jit(solution)/shard_map/ppermute | solution.py:50
  68.3 3.8 %collective-permute-start.1 = (bf16[2,3,1152]{2,1,0:T(4,128)(2,1)S(1)}, bf16[2,3,1152]{2,1,0:T(4,128)(2,1)S(1)}, u32[]{:S(2)}, u32[]{:S(2)}) collective-permute-start(bf16[2,3,1152]{2,1,0:T(4,128)(2,1)S(1)} %shard_map.140.own_ref), channel_id=1, source_target_pairs={{0,8},{4,12},{8,0},{12,4},{16,24},{20,28},{24,16},{28,20},{1,9},{5... | collective-permute-start | bytes 41480 | tf_op jit(solution)/shard_map/ppermute | solution.py:50
  72.1 4.9 %collective-permute-start.2 = (bf16[4,3,1152]{2,1,0:T(4,128)(2,1)S(1)}, bf16[4,3,1152]{2,1,0:T(4,128)(2,1)S(1)}, u32[]{:S(2)}, u32[]{:S(2)}) collective-permute-start(bf16[4,3,1152]{2,1,0:T(4,128)(2,1)S(1)} %shard_map.141.first_ref), channel_id=1, source_target_pairs={{0,16},{4,20},{8,24},{12,28},{16,0},{20,4},{24,8},{28,12},{1,17},{... | collective-permute-start | bytes 82952 | tf_op jit(solution)/shard_map/ppermute | solution.py:50

commit v5 on v4

--- a/solution.py
+++ b/solution.py
@@ -234,7 +234,7 @@
     )(*pieces)
 
 
-def route_kernel(first_ref, second_ref, cap_ref, meta_ref):
+def route_kernel(params_ref, first_ref, second_ref, cap_ref, slot_ref, live_ref, line_ref):
     half = first_ref.shape[0]
     rows = jnp.concatenate(
         [ref[j].astype(F32) for ref in (first_ref, second_ref) for j in range(half)], axis=0
@@ -256,23 +256,28 @@
     spot_row = jnp.sum(jnp.where(same, spot_col, 0.0), axis=0, keepdims=True)
     place = jnp.sum(jnp.where(spot_row < spot_col, mine_row, 0.0), axis=1, keepdims=True)
     lane = lax.broadcasted_iota(jnp.int32, (count, META), 1)
-    slot = jnp.where(place == (lane - 1).astype(F32), mine, 0.0)
-    meta_ref[...] = jnp.where(lane == 0, live, slot)
-
-
-def route(first, second):
+    slot_ref[...] = jnp.where(place == lane.astype(F32), mine, 0.0)
+    live_ref[...] = jnp.broadcast_to(live, (count, META))
+    row = lax.broadcasted_iota(jnp.int32, line_ref.shape, 0)
+    scale = 10.0 * jnp.exp(jnp.full(line_ref.shape, params_ref[0], F32))
+    line_ref[...] = jnp.where(row == 0, scale, 2.0 * params_ref[1])
+
+
+def route(first, second, params):
     count = 2 * first.shape[0] * SEND_MOST
     return pl.pallas_call(
         route_kernel,
         out_shape=(
             jax.ShapeDtypeStruct((count, first.shape[2] - META), F32),
             jax.ShapeDtypeStruct((count, META), F32),
+            jax.ShapeDtypeStruct((count, META), F32),
+            jax.ShapeDtypeStruct((2, META), F32),
         ),
-        in_specs=[vmem()] * 2,
-        out_specs=(vmem(),) * 2,
+        in_specs=[smem()] + [vmem()] * 2,
+        out_specs=(vmem(),) * 4,
         name="route",
         compiler_params=small(6),
-    )(first, second)
+    )(params, first, second)
 
 
 def attend_kernel(shards, gains_ref, patch_ref, qkv_ref, *refs):
@@ -329,19 +334,39 @@
     )(gains, patch_weight, qkv, *pixels, *positions)
 
 
-def expand_kernel(order, images, gains_ref, up_ref, hidden_ref, *refs):
+def mix(hidden, order, which, images, context_refs, output_refs):
     shards = len(order)
-    context_refs = refs[:shards]
-    output_refs = refs[shards : 2 * shards]
-    sums_ref = refs[2 * shards]
-    length = hidden_ref.shape[0] // images
+    length = hidden.shape[0] // images
     block = length // shards
-    hidden = hidden_ref[...]
-    for j, ref in enumerate(context_refs):
+    for j, context_ref, output_ref in zip(which, context_refs, output_refs):
         places = [order.index(order[p] ^ order[j]) for p in range(shards)]
         starts = [i * length + q * block for i in range(images) for q in places]
-        context = jnp.concatenate([ref[at : at + block, :] for at in starts], axis=0)
-        hidden = hidden + jnp.dot(context, output_refs[j][...], preferred_element_type=F32)
+        context = jnp.concatenate([context_ref[at : at + block, :] for at in starts], axis=0)
+        hidden = hidden + jnp.dot(context, output_ref[...], preferred_element_type=F32)
+    return hidden
+
+
+def blend_kernel(order, which, images, hidden_ref, *refs):
+    count = len(which)
+    hidden = hidden_ref[...]
+    refs[-1][...] = mix(hidden, order, which, images, refs[:count], refs[count : 2 * count])
+
+
+def blend(contexts, order, which, images, outputs, hidden):
+    return pl.pallas_call(
+        functools.partial(blend_kernel, tuple(order), tuple(which), images),
+        out_shape=jax.ShapeDtypeStruct(hidden.shape, F32),
+        in_specs=[vmem()] * (1 + 2 * len(which)),
+        out_specs=vmem(),
+        compiler_params=small(GRANT),
+    )(hidden, *(contexts[j] for j in which), *(outputs[j] for j in which))
+
+
+def expand_kernel(order, which, images, gains_ref, up_ref, hidden_ref, *refs):
+    count = len(which)
+    sums_ref = refs[2 * count]
+    length = hidden_ref.shape[0] // images
+    hidden = mix(hidden_ref[...], order, which, images, refs[:count], refs[count : 2 * count])
     normed = layer_norm(hidden, gains_ref[1:2, :]).astype(BF16)
     expanded = jax.nn.gelu(jnp.dot(normed, up_ref[...], preferred_element_type=F32)).astype(BF16)
     expanded = expanded.astype(F32)
@@ -351,15 +376,15 @@
         sums_ref[images + i : images + i + 1, :] = jnp.sum(expanded[rows], axis=0, keepdims=True)
 
 
-def expand(contexts, order, images, outputs, hidden, gains, up_weight):
+def expand(contexts, order, which, images, outputs, hidden, gains, up_weight):
     width = hidden.shape[1]
     return pl.pallas_call(
-        functools.partial(expand_kernel, tuple(order), images),
+        functools.partial(expand_kernel, tuple(order), tuple(which), images),
         out_shape=jax.ShapeDtypeStruct((2 * images, width), F32),
-        in_specs=[vmem()] * (3 + 2 * len(order)),
+        in_specs=[vmem()] * (3 + 2 * len(which)),
         out_specs=vmem(),
         compiler_params=small(GRANT),
-    )(gains, up_weight, hidden, *contexts, *outputs)
+    )(gains, up_weight, hidden, *(contexts[j] for j in which), *(outputs[j] for j in which))
 
 
 def reduce_kernel(scale, down_ref, *refs):
@@ -388,49 +413,52 @@
     )(down_weight, *sums)
 
 
-def finish_kernel(total, params_ref, gains_ref, weight_ref, cap_ref, meta_ref, first_ref, second_ref, out_ref, loss_ref):
+def finish_kernel(total, gains_ref, weight_ref, cap_ref, slot_ref, live_ref, line_ref, *refs):
+    first_ref, second_ref, out_ref, loss_ref = refs
     half = first_ref.shape[0]
     rows = jnp.concatenate(
         [ref[j] for ref in (first_ref, second_ref) for j in range(half)], axis=0
     )
-    meta = meta_ref[...]
-    live = meta[:, 0:1]
+    slot = slot_ref[...]
     pooled = jnp.concatenate(
         [
-            jnp.sum(jnp.where(meta[:, k + 1 : k + 2] > 0.0, rows, 0.0), axis=0, keepdims=True)
+            jnp.sum(jnp.where(slot[:, k : k + 1] > 0.0, rows, 0.0), axis=0, keepdims=True)
             for k in range(RECV_MOST)
         ],
         axis=0,
     )
-    filled = jnp.max(meta, axis=0, keepdims=True)
+    filled = jnp.max(slot, axis=0, keepdims=True)
+    used = jnp.concatenate([filled[:, k : k + 1] for k in range(RECV_MOST)], axis=0)
     normed = layer_norm(pooled, gains_ref[2:3, :]).astype(BF16)
     embedded = jnp.dot(normed, weight_ref[...], preferred_element_type=F32)
+    embedded = jnp.where(used > 0.0, embedded, 0.0)
+    out_ref[...] = embedded
     captions = cap_ref[...]
-    scale = 10.0 * jnp.exp(jnp.full((1, 1), params_ref[0], F32))
-    shift = 2.0 * params_ref[1]
+    images = unit_rows(embedded)
+    lane = lax.broadcasted_iota(jnp.int32, slot.shape, 1)
+    products = jnp.zeros(slot.shape, F32)
     for k in range(RECV_MOST):
-        used = filled[:, k + 1 : k + 2]
-        row = jnp.where(used > 0.0, embedded[k : k + 1, :], 0.0)
-        out_ref[k : k + 1, :] = row
-        logits = scale * jnp.sum(captions * unit_rows(row), axis=1, keepdims=True) + shift
-        signs = jnp.where(meta[:, k + 1 : k + 2] > 0.0, 1.0, -1.0)
-        value = -signs * logits
-        terms = jnp.maximum(value, 0.0) + jnp.log1p(jnp.exp(-jnp.abs(value)))
-        loss_ref[k] = jnp.sum(terms * live * used) / total
-
-
-def finish(first, second, captions, meta, params, gains, weight, total):
+        product = jnp.sum(captions * images[k : k + 1, :], axis=1, keepdims=True)
+        products = jnp.where(lane == k, product, products)
+    logits = line_ref[0:1, :] * products + line_ref[1:2, :]
+    value = jnp.where(slot > 0.0, -logits, logits)
+    terms = jnp.maximum(value, 0.0) + jnp.log1p(jnp.exp(-jnp.abs(value)))
+    losses = jnp.sum(terms * live_ref[...], axis=0, keepdims=True) * (1.0 / total) * filled
+    loss_ref[...] = losses[0, :RECV_MOST]
+
+
+def finish(first, second, routed, gains, weight, total):
     return pl.pallas_call(
         functools.partial(finish_kernel, total),
         out_shape=(
             jax.ShapeDtypeStruct((RECV_MOST, weight.shape[1]), F32),
             jax.ShapeDtypeStruct((RECV_MOST,), F32),
         ),
-        in_specs=[smem()] + [vmem()] * 6,
-        out_specs=(vmem(), smem()),
+        in_specs=[vmem()] * 8,
+        out_specs=(vmem(), vmem()),
         name="finish",
         compiler_params=small(8),
-    )(params, gains, weight, captions, meta, first, second)
+    )(gains, weight, *routed, first, second)
 
 
 def per_device(
@@ -468,7 +496,7 @@
     for bit in bits_down(shards)[1:]:
         outputs = outputs + [swap(block, "mp", bit) for block in outputs]
 
-    captions, meta = route(*double_stack(caption_meta, "dp"))
+    routed = route(*double_stack(caption_meta, "dp"), loss_params)
 
     sums = []
     for r, images in enumerate(CHUNKS):
@@ -476,13 +504,17 @@
             pixel_blocks[r], positions, norm_gains, patch_weight, query_key_value
         )
         contexts, _ = gather_blocks(context, "mp")
-        sums.append(expand(contexts, order, images, outputs, hidden, norm_gains, up_weight))
+        which = list(range(shards))
+        if r == len(CHUNKS) - 1:
+            hidden = blend(contexts, order, which[:-1], images, outputs, hidden)
+            which = which[-1:]
+        sums.append(expand(contexts, order, which, images, outputs, hidden, norm_gains, up_weight))
     pooled = reduce_units(sums, down_weight, position.shape[0] * shards)
     for bit in reversed(bits_down(shards)):
         pooled = add(pooled, swap(pooled, "mp", bit))
     first, second = double_stack(pooled[None], "dp")
     return finish(
-        first, second, captions, meta, loss_params, norm_gains, embedding_weight, float(devices_dp * SEL_DEV)
+        first, second, routed, norm_gains, embedding_weight, float(devices_dp * SEL_DEV)
     )
 
 

time: 79.6 us -> 81.9 us (1.029)
  waiting for transfers between devices: 35.8 us -> 37.1 us
  local copies, waits for them, and re-layouts: 0.04 us -> 1.03 us
    ppermute x33, waiting for transfers between devices: 35.8 us -> 37.1 us  [swap(): return lax.ppermute(values, axis, [(i, i ^ bit) for i in range(size)])]
    unnamed x16, local copies, waits for them, and re-layouts: 0.04 us -> 1.03 us
    pallas_call x3 -> x4, Pallas kernels: 5.8 us -> 6.07 us  [the longest x3 5.49 us: expand(): pl.pallas_call(functools.partial(expand_kernel, tuple(order), tuple(which...]
  transfers between devices with their start and end apart: 33 -> 33, of which waited for: 13 -> 13; matrix products, arithmetic and copies ran while one was open for 0% -> 0% of each run, Pallas kernels for 16% -> 17%
where the time goes in v5:
time: 81.9 us; the launch traced here: 81.7 us
  waiting for transfers between devices  37.1 us (45%)
  starting transfers between devices  23.4 us (29%)
  Pallas kernels  19.4 us (24%)
  local copies, waits for them, and re-layouts  1.03 us (1%)
  between operations  0.84 us (1%)
    ppermute x33, waiting for transfers between devices, swap(): return lax.ppermute(values, axis, [(i, i ^ bit) for i in range(size)])  37.1 us
    ppermute x33, starting transfers between devices, swap(): return lax.ppermute(values, axis, [(i, i ^ bit) for i in range(size)])  23.4 us
    pallas_call x3, Pallas kernels, attend(): pl.pallas_call(functools.partial(attend_kernel, shards), out_shape=(jax.S...  7.16 us
    pallas_call x3, Pallas kernels, expand(): pl.pallas_call(functools.partial(expand_kernel, tuple(order), tuple(which...  5.49 us
    pallas_call x1, Pallas kernels, pick(): pl.pallas_call(functools.partial(pick_kernel, pieces), out_shape=tuple((j...  2.07 us
  transfers between devices with their start and end apart: 33, of which 13 were waited for; matrix products, arithmetic and copies ran while one was open for 0% of the time, Pallas kernels for 17%

profile of v5, /device:TPU:0, one launch (start us, length us, event | category | flops | bytes accessed | tf_op | source)
XLA Modules:
  0.0 81.7 jit_solution(2459568492870781122)
XLA Ops:
  0.7 2.1 %pick.1 = (bf16[64,768]{1,0:T(8,128)(2,1)S(1)}, bf16[64,768]{1,0:T(8,128)(2,1)S(1)}, bf16[64,768]{1,0:T(8,128)(2,1)S(1)}, bf16[1,3,1152]{2,1,0:T(4,128)(2,1)S(1)...) custom-call(s32[16]{0:T(128)} %sel_hbm.1, s32[16]{0:T(128)} %dest_hbm.1, bf16[16,64,768]{2,1,0:T(8,128)(2,1)} %pixels_ref.1, ...), custom_call_target="tpu_custom_call" | custom-call | tf_op jit(solution)/shard_map/pick/pallas_call | solution.py:170
  2.7 3.0 %collective-permute-start.12 = (bf16[128,1024]{1,0:T(8,128)(2,1)S(1)}, bf16[128,1024]{1,0:T(8,128)(2,1)S(1)}, u32[]{:S(2)}, u32[]{:S(2)}) collective-permute-start(bf16[128,1024]{1,0:T(8,128)(2,1)S(1)} %get-tuple-element.27), channel_id=1, source_target_pairs={{0,2},{1,3},{2,0},{3,1},{4,6},{5,7},{6,4},{7,5},{8,10},{9,11},{10,... | collective-permute-start | bytes 786440 | tf_op jit(solution)/shard_map/ppermute | solution.py:50
  5.8 6.3 %collective-permute-done.12.refs_0_ = bf16[128,1024]{1,0:T(8,128)(2,1)S(1)} collective-permute-done((bf16[128,1024]{1,0:T(8,128)(2,1)S(1)}, bf16[128,1024]{1,0:T(8,128)(2,1)S(1)}, u32[]{:S(2)}, u32[]{:S(2)}) %collective-permute-start.12) | collective-permute-done | bytes 262176 | tf_op jit(solution)/shard_map/ppermute | solution.py:50
  12.1 1.8 %collective-permute-start.13 = (bf16[128,1024]{1,0:T(8,128)(2,1)S(1)}, bf16[128,1024]{1,0:T(8,128)(2,1)S(1)}, u32[]{:S(2)}, u32[]{:S(2)}) collective-permute-start(bf16[128,1024]{1,0:T(8,128)(2,1)S(1)} %collective-permute-done.12.refs_0_), channel_id=1, source_target_pairs={{0,4},{4,0},{8,12},{12,8},{16,20},{20,16},{24,28},{28,24},{1,5},{5... | collective-permute-start | bytes 786440 | tf_op jit(solution)/shard_map/ppermute | solution.py:50
  13.8 1.5 %collective-permute-start.3 = (bf16[64,768]{1,0:T(8,128)(2,1)S(1)}, bf16[64,768]{1,0:T(8,128)(2,1)S(1)}, u32[]{:S(2)}, u32[]{:S(2)}) collective-permute-start(bf16[64,768]{1,0:T(8,128)(2,1)S(1)} %get-tuple-element.23.refs_0_), channel_id=1, source_target_pairs={{0,2},{1,3},{2,0},{3,1},{4,6},{5,7},{6,4},{7,5},{8,10},{9,11},{10,... | collective-permute-start | bytes 294920 | tf_op jit(solution)/shard_map/ppermute | solution.py:50
  15.3 0.5 collective-permute-start.6
  15.9 1.5 %collective-permute-start.22 = (bf16[64,768]{1,0:T(8,128)(2,1)S(1)}, bf16[64,768]{1,0:T(8,128)(2,1)S(1)}, u32[]{:S(2)}, u32[]{:S(2)}) collective-permute-start(bf16[64,768]{1,0:T(8,128)(2,1)S(1)} %get-tuple-element.31.refs_0_), channel_id=1, source_target_pairs={{0,2},{1,3},{2,0},{3,1},{4,6},{5,7},{6,4},{7,5},{8,10},{9,11},{10,... | collective-permute-start | bytes 294920 | tf_op jit(solution)/shard_map/ppermute | solution.py:50
  17.4 1.4 %collective-permute-done.3.refs_1_ = bf16[64,768]{1,0:T(8,128)(2,1)S(1)} collective-permute-done((bf16[64,768]{1,0:T(8,128)(2,1)S(1)}, bf16[64,768]{1,0:T(8,128)(2,1)S(1)}, u32[]{:S(2)}, u32[]{:S(2)}) %collective-permute-start.3) | collective-permute-done | bytes 98336 | tf_op jit(solution)/shard_map/ppermute | solution.py:50
  18.8 0.5 collective-permute-start.7
  19.3 3.1 %collective-permute-done.22.refs_1_ = bf16[64,768]{1,0:T(8,128)(2,1)S(1)} collective-permute-done((bf16[64,768]{1,0:T(8,128)(2,1)S(1)}, bf16[64,768]{1,0:T(8,128)(2,1)S(1)}, u32[]{:S(2)}, u32[]{:S(2)}) %collective-permute-start.22) | collective-permute-done | bytes 98336 | tf_op jit(solution)/shard_map/ppermute | solution.py:50
  22.4 0.5 collective-permute-start.8
  23.0 0.7 collective-permute-done.23.refs_2_
  23.7 0.2 collective-permute-start.15
  23.9 0.4 collective-permute-start.24
  24.2 1.2 %collective-permute-start.16 = (bf16[64,768]{1,0:T(8,128)(2,1)S(1)}, bf16[64,768]{1,0:T(8,128)(2,1)S(1)}, u32[]{:S(2)}, u32[]{:S(2)}) collective-permute-start(bf16[64,768]{1,0:T(8,128)(2,1)S(1)} %get-tuple-element.28.refs_0_), channel_id=1, source_target_pairs={{0,2},{1,3},{2,0},{3,1},{4,6},{5,7},{6,4},{7,5},{8,10},{9,11},{10,... | collective-permute-start | bytes 294920 | tf_op jit(solution)/shard_map/ppermute | solution.py:50
  25.5 1.4 %load.1.qkv_ref = bf16[3,1024,256]{2,1,0:T(8,128)(2,1)S(1)} custom-call(bf16[3,1024,256]{2,1,0:T(8,128)(2,1)} %source_ref.1), custom_call_target="tpu_custom_call" | custom-call | tf_op jit(solution)/shard_map/load/pallas_call | solution.py:204
  26.9 2.4 %shard_map.142 = (f32[256,1024]{1,0:T(8,128)S(1)}, bf16[256,256]{1,0:T(8,128)(2,1)S(1)}) custom-call(f32[3,1024]{1,0:T(4,128)S(1)} %copy-done.5, bf16[768,1024]{1,0:T(8,128)(2,1)S(1)} %copy-done.1, bf16[3,1024,256]{2,1,0:T(8,128)(2,1)S(1)} %load.1.qkv_ref, bf16[64,768]{1,0:T(8,128)(2,1)S(1)} %get-tuple-element.23.refs_0_, ...), custom_call_target="tpu_custom_call" | custom-call | tf_op jit(solution)/shard_map/pallas_call | solution.py:325
  29.3 0.8 %collective-permute-start.9 = (bf16[256,256]{1,0:T(8,128)(2,1)S(1)}, bf16[256,256]{1,0:T(8,128)(2,1)S(1)}, u32[]{:S(2)}, u32[]{:S(2)}) collective-permute-start(bf16[256,256]{1,0:T(8,128)(2,1)S(1)} %get-tuple-element.26.refs_0_), channel_id=1, source_target_pairs={{0,2},{1,3},{2,0},{3,1},{4,6},{5,7},{6,4},{7,5},{8,10},{9,11},{10,... | collective-permute-start | bytes 393224 | tf_op jit(solution)/shard_map/ppermute | solution.py:50
  30.2 2.4 %shard_map.146 = (f32[256,1024]{1,0:T(8,128)S(1)}, bf16[256,256]{1,0:T(8,128)(2,1)S(1)}) custom-call(f32[3,1024]{1,0:T(4,128)S(1)} %copy-done.5, bf16[768,1024]{1,0:T(8,128)(2,1)S(1)} %copy-done.1, bf16[3,1024,256]{2,1,0:T(8,128)(2,1)S(1)} %load.1.qkv_ref, bf16[64,768]{1,0:T(8,128)(2,1)S(1)} %get-tuple-element.31.refs_0_, ...), custom_call_target="tpu_custom_call" | custom-call | tf_op jit(solution)/shard_map/pallas_call | solution.py:325
  32.5 1.3 %collective-permute-start.25 = (bf16[256,256]{1,0:T(8,128)(2,1)S(1)}, bf16[256,256]{1,0:T(8,128)(2,1)S(1)}, u32[]{:S(2)}, u32[]{:S(2)}) collective-permute-start(bf16[256,256]{1,0:T(8,128)(2,1)S(1)} %get-tuple-element.33.refs_0_), channel_id=1, source_target_pairs={{0,2},{1,3},{2,0},{3,1},{4,6},{5,7},{6,4},{7,5},{8,10},{9,11},{10,... | collective-permute-start | bytes 393224 | tf_op jit(solution)/shard_map/ppermute | solution.py:50
  33.8 1.3 %collective-permute-done.18.refs_3_ = bf16[64,768]{1,0:T(8,128)(2,1)S(1)} collective-permute-done((bf16[64,768]{1,0:T(8,128)(2,1)S(1)}, bf16[64,768]{1,0:T(8,128)(2,1)S(1)}, u32[]{:S(2)}, u32[]{:S(2)}) %collective-permute-start.18) | collective-permute-done | bytes 98336 | tf_op jit(solution)/shard_map/ppermute | solution.py:50
  35.1 2.4 %shard_map.144 = (f32[256,1024]{1,0:T(8,128)S(1)}, bf16[256,256]{1,0:T(8,128)(2,1)S(1)}) custom-call(f32[3,1024]{1,0:T(4,128)S(1)} %copy-done.5, bf16[768,1024]{1,0:T(8,128)(2,1)S(1)} %copy-done.1, bf16[3,1024,256]{2,1,0:T(8,128)(2,1)S(1)} %load.1.qkv_ref, bf16[64,768]{1,0:T(8,128)(2,1)S(1)} %get-tuple-element.28.refs_0_, ...), custom_call_target="tpu_custom_call" | custom-call | tf_op jit(solution)/shard_map/pallas_call | solution.py:325
  37.5 0.8 %collective-permute-start.19 = (bf16[256,256]{1,0:T(8,128)(2,1)S(1)}, bf16[256,256]{1,0:T(8,128)(2,1)S(1)}, u32[]{:S(2)}, u32[]{:S(2)}) collective-permute-start(bf16[256,256]{1,0:T(8,128)(2,1)S(1)} %get-tuple-element.30.refs_0_), channel_id=1, source_target_pairs={{0,2},{1,3},{2,0},{3,1},{4,6},{5,7},{6,4},{7,5},{8,10},{9,11},{10,... | collective-permute-start | bytes 393224 | tf_op jit(solution)/shard_map/ppermute | solution.py:50
  38.4 0.5 collective-permute-start.27
  38.9 4.2 %collective-permute-done.19.refs_1_ = bf16[256,256]{1,0:T(8,128)(2,1)S(1)} collective-permute-done((bf16[256,256]{1,0:T(8,128)(2,1)S(1)}, bf16[256,256]{1,0:T(8,128)(2,1)S(1)}, u32[]{:S(2)}, u32[]{:S(2)}) %collective-permute-start.19) | collective-permute-done | bytes 131104 | tf_op jit(solution)/shard_map/ppermute | solution.py:50
  43.1 0.5 collective-permute-start.11
  43.7 0.4 collective-permute-start.21
  44.1 0.6 shard_map.147.hidden_ref
  44.7 1.0 %copy-done = bf16[1024,1024]{1,0:T(8,128)(2,1)S(1)} copy-done((bf16[1024,1024]{1,0:T(8,128)(2,1)S(1)}, bf16[1024,1024]{1,0:T(8,128)(2,1)}, u32[]{:S(2)}) %copy-start) | copy-done | bytes 2097176
  45.7 1.6 %shard_map.148.refs_2_ = f32[2,1024]{1,0:T(2,128)S(1)} custom-call(f32[3,1024]{1,0:T(4,128)S(1)} %copy-done.5, bf16[1024,1024]{1,0:T(8,128)(2,1)S(1)} %copy-done, f32[256,1024]{1,0:T(8,128)S(1)} %shard_map.147.hidden_ref, bf16[256,256]{1,0:T(8,128)(2,1)S(1)} %collective-permute-done.27.refs_0_, bf16[256,1024]{1,0:T(8,128)(2,1)S(1)} %collective-permute-done.15.refs_7_.refs_1_), custom_call_target="tpu_custom_call" | custom-call | tf_op jit(solution)/shard_map/pallas_call | solution.py:381
  47.3 2.0 %shard_map.143.refs_0_ = f32[2,1024]{1,0:T(2,128)S(1)} custom-call(f32[3,1024]{1,0:T(4,128)S(1)} %copy-done.5, bf16[1024,1024]{1,0:T(8,128)(2,1)S(1)} %copy-done, f32[256,1024]{1,0:T(8,128)S(1)} %get-tuple-element.25.hidden_ref, bf16[256,256]{1,0:T(8,128)(2,1)S(1)} %get-tuple-element.26.refs_0_, bf16[256,256]{1,0:T(8,128)(2,1)S(1)} %collective-permute-done.9.refs_1_, ...), custom_call_target="tpu_custom_call" | custom-call | tf_op jit(solution)/shard_map/pallas_call | solution.py:381
  49.3 2.0 %shard_map.145.refs_1_ = f32[2,1024]{1,0:T(2,128)S(1)} custom-call(f32[3,1024]{1,0:T(4,128)S(1)} %copy-done.5, bf16[1024,1024]{1,0:T(8,128)(2,1)S(1)} %copy-done, f32[256,1024]{1,0:T(8,128)S(1)} %get-tuple-element.29.hidden_ref, bf16[256,256]{1,0:T(8,128)(2,1)S(1)} %get-tuple-element.30.refs_0_, bf16[256,256]{1,0:T(8,128)(2,1)S(1)} %collective-permute-done.19.refs_1_, ...), custom_call_target="tpu_custom_call" | custom-call | tf_op jit(solution)/shard_map/pallas_call | solution.py:381
  51.3 0.4 reduce.1.own_ref
  51.8 1.1 %collective-permute-done.28.other_ref = f32[3,1024]{1,0:T(4,128)S(1)} collective-permute-done((f32[3,1024]{1,0:T(4,128)S(1)}, f32[3,1024]{1,0:T(4,128)S(1)}, u32[]{:S(2)}, u32[]{:S(2)}) %collective-permute-start.28) | collective-permute-done | bytes 12320 | tf_op jit(solution)/shard_map/ppermute | solution.py:50
  52.9 0.8 collective-permute-start.29
  53.7 3.0 %collective-permute-done.29.other_ref = f32[3,1024]{1,0:T(4,128)S(1)} collective-permute-done((f32[3,1024]{1,0:T(4,128)S(1)}, f32[3,1024]{1,0:T(4,128)S(1)}, u32[]{:S(2)}, u32[]{:S(2)}) %collective-permute-start.29) | collective-permute-done | bytes 12320 | tf_op jit(solution)/shard_map/ppermute | solution.py:50
  56.7 0.5 collective-permute-start.30
  57.2 3.2 %collective-permute-done.30.other_ref = f32[1,3,1024]{2,1,0:T(4,128)S(1)} collective-permute-done((f32[1,3,1024]{2,1,0:T(4,128)S(1)}, f32[1,3,1024]{2,1,0:T(4,128)S(1)}, u32[]{:S(2)}, u32[]{:S(2)}) %collective-permute-start.30) | collective-permute-done | bytes 12320 | tf_op jit(solution)/shard_map/ppermute | solution.py:50
  60.4 1.6 %collective-permute-start.31 = (f32[2,3,1024]{2,1,0:T(4,128)S(1)}, f32[2,3,1024]{2,1,0:T(4,128)S(1)}, u32[]{:S(2)}, u32[]{:S(2)}) collective-permute-start(f32[2,3,1024]{2,1,0:T(4,128)S(1)} %shard_map.149.own_ref), channel_id=1, source_target_pairs={{0,8},{4,12},{8,0},{12,4},{16,24},{20,28},{24,16},{28,20},{1,9},{5... | collective-permute-start | bytes 73736 | tf_op jit(solution)/shard_map/ppermute | solution.py:50
  62.0 2.3 %collective-permute-done.31.other_ref = f32[2,3,1024]{2,1,0:T(4,128)S(1)} collective-permute-done((f32[2,3,1024]{2,1,0:T(4,128)S(1)}, f32[2,3,1024]{2,1,0:T(4,128)S(1)}, u32[]{:S(2)}, u32[]{:S(2)}) %collective-permute-start.31) | collective-permute-done | bytes 24608 | tf_op jit(solution)/shard_map/ppermute | solution.py:50
  64.3 2.8 %collective-permute-start.32 = (f32[4,3,1024]{2,1,0:T(4,128)S(1)}, f32[4,3,1024]{2,1,0:T(4,128)S(1)}, u32[]{:S(2)}, u32[]{:S(2)}) collective-permute-start(f32[4,3,1024]{2,1,0:T(4,128)S(1)} %shard_map.150.refs_0_), channel_id=1, source_target_pairs={{0,16},{4,20},{8,24},{12,28},{16,0},{20,4},{24,8},{28,12},{1,17},{... | collective-permute-start | bytes 147464 | tf_op jit(solution)/shard_map/ppermute | solution.py:50
  67.2 0.5 collective-permute-start
  67.7 3.2 %collective-permute-done.other_ref = bf16[1,3,1152]{2,1,0:T(4,128)(2,1)S(1)} collective-permute-done((bf16[1,3,1152]{2,1,0:T(4,128)(2,1)S(1)}, bf16[1,3,1152]{2,1,0:T(4,128)(2,1)S(1)}, u32[]{:S(2)}, u32[]{:S(2)}) %collective-permute-start) | collective-permute-done | bytes 6944 | tf_op jit(solution)/shard_map/ppermute | solution.py:50
  70.8 1.3 %collective-permute-start.1 = (bf16[2,3,1152]{2,1,0:T(4,128)(2,1)S(1)}, bf16[2,3,1152]{2,1,0:T(4,128)(2,1)S(1)}, u32[]{:S(2)}, u32[]{:S(2)}) collective-permute-start(bf16[2,3,1152]{2,1,0:T(4,128)(2,1)S(1)} %shard_map.140.own_ref), channel_id=1, source_target_pairs={{0,8},{4,12},{8,0},{12,4},{16,24},{20,28},{24,16},{28,20},{1,9},{5... | collective-permute-start | bytes 41480 | tf_op jit(solution)/shard_map/ppermute | solution.py:50
  72.2 2.4 %collective-permute-done.1.other_ref = bf16[2,3,1152]{2,1,0:T(4,128)(2,1)S(1)} collective-permute-done((bf16[2,3,1152]{2,1,0:T(4,128)(2,1)S(1)}, bf16[2,3,1152]{2,1,0:T(4,128)(2,1)S(1)}, u32[]{:S(2)}, u32[]{:S(2)}) %collective-permute-start.1) | collective-permute-done | bytes 13856 | tf_op jit(solution)/shard_map/ppermute | solution.py:50
  74.8 4.8 %collective-permute-done.2.second_ref = bf16[4,3,1152]{2,1,0:T(4,128)(2,1)S(1)} collective-permute-done((bf16[4,3,1152]{2,1,0:T(4,128)(2,1)S(1)}, bf16[4,3,1152]{2,1,0:T(4,128)(2,1)S(1)}, u32[]{:S(2)}, u32[]{:S(2)}) %collective-permute-start.2) | collective-permute-done | bytes 27680 | tf_op jit(solution)/shard_map/ppermute | solution.py:50
  79.5 0.8 route.1
  80.3 1.4 %finish.1 = (f32[4,1024]{1,0:T(4,128)}, f32[4]{0:T(128)}) custom-call(f32[3,1024]{1,0:T(4,128)S(1)} %copy-done.5, bf16[1024,1024]{1,0:T(8,128)(2,1)S(1)} %copy-done.4, f32[24,1024]{1,0:T(8,128)S(1)} %get-tuple-element.19.cap_ref, f32[24,128]{1,0:T(8,128)S(1)} %get-tuple-element.20.slot_ref, f32[24,128]{1,0:T(8,128)S(1)} %get-tuple-element.21.live_ref, ...), custom_call_target="tpu_custom_call" | custom-call | tf_op jit(solution)/shard_map/finish/pallas_call | solution.py:451
  (53 shorter events, 0.6 us)
Async XLA Ops:
  0.6 18.2 %copy-start.2 = (bf16[256,1024]{1,0:T(8,128)(2,1)S(1)}, bf16[256,1024]{1,0:T(8,128)(2,1)}, u32[]{:S(2)}) copy-start(bf16[256,1024]{1,0:T(8,128)(2,1)} %refs_3_.1) | copy-start | bytes 1572868
  0.6 14.7 %copy-start.7 = (bf16[64,1024]{1,0:T(8,128)(2,1)S(1)}, bf16[64,1024]{1,0:T(8,128)(2,1)}, u32[]{:S(2)}) copy-start(bf16[64,1024]{1,0:T(8,128)(2,1)} %pos_hbm.1) | copy-start | bytes 393220
  2.7 9.3 %collective-permute-start.12 = (bf16[128,1024]{1,0:T(8,128)(2,1)S(1)}, bf16[128,1024]{1,0:T(8,128)(2,1)S(1)}, u32[]{:S(2)}, u32[]{:S(2)}) collective-permute-start(bf16[128,1024]{1,0:T(8,128)(2,1)S(1)} %get-tuple-element.27), channel_id=1, source_target_pairs={{0,2},{1,3},{2,0},{3,1},{4,6},{5,7},{6,4},{7,5},{8,10},{9,11},{10,... | collective-permute-start | bytes 786440 | tf_op jit(solution)/shard_map/ppermute | solution.py:50
  12.1 10.9 %collective-permute-start.13 = (bf16[128,1024]{1,0:T(8,128)(2,1)S(1)}, bf16[128,1024]{1,0:T(8,128)(2,1)S(1)}, u32[]{:S(2)}, u32[]{:S(2)}) collective-permute-start(bf16[128,1024]{1,0:T(8,128)(2,1)S(1)} %collective-permute-done.12.refs_0_), channel_id=1, source_target_pairs={{0,4},{4,0},{8,12},{12,8},{16,20},{20,16},{24,28},{28,24},{1,5},{5... | collective-permute-start | bytes 786440 | tf_op jit(solution)/shard_map/ppermute | solution.py:50
  13.8 5.0 %collective-permute-start.3 = (bf16[64,768]{1,0:T(8,128)(2,1)S(1)}, bf16[64,768]{1,0:T(8,128)(2,1)S(1)}, u32[]{:S(2)}, u32[]{:S(2)}) collective-permute-start(bf16[64,768]{1,0:T(8,128)(2,1)S(1)} %get-tuple-element.23.refs_0_), channel_id=1, source_target_pairs={{0,2},{1,3},{2,0},{3,1},{4,6},{5,7},{6,4},{7,5},{8,10},{9,11},{10,... | collective-permute-start | bytes 294920 | tf_op jit(solution)/shard_map/ppermute | solution.py:50
  15.3 7.1 %collective-permute-start.6 = (bf16[64,1024]{1,0:T(8,128)(2,1)S(1)}, bf16[64,1024]{1,0:T(8,128)(2,1)S(1)}, u32[]{:S(2)}, u32[]{:S(2)}) collective-permute-start(bf16[64,1024]{1,0:T(8,128)(2,1)S(1)} %copy-done.7), channel_id=1, source_target_pairs={{0,2},{1,3},{2,0},{3,1},{4,6},{5,7},{6,4},{7,5},{8,10},{9,11},{10,... | collective-permute-start | bytes 393224 | tf_op jit(solution)/shard_map/ppermute | solution.py:50
  15.9 2.9 %collective-permute-start.4 = (bf16[64,768]{1,0:T(8,128)(2,1)S(1)}, bf16[64,768]{1,0:T(8,128)(2,1)S(1)}, u32[]{:S(2)}, u32[]{:S(2)}) collective-permute-start(bf16[64,768]{1,0:T(8,128)(2,1)S(1)} %get-tuple-element.23.refs_0_), channel_id=1, source_target_pairs={{0,1},{1,0},{2,3},{3,2},{4,5},{5,4},{6,7},{7,6},{8,9},{9,8},{10,11... | collective-permute-start | bytes 294920 | tf_op jit(solution)/shard_map/ppermute | solution.py:50
  15.9 6.5 %collective-permute-start.22 = (bf16[64,768]{1,0:T(8,128)(2,1)S(1)}, bf16[64,768]{1,0:T(8,128)(2,1)S(1)}, u32[]{:S(2)}, u32[]{:S(2)}) collective-permute-start(bf16[64,768]{1,0:T(8,128)(2,1)S(1)} %get-tuple-element.31.refs_0_), channel_id=1, source_target_pairs={{0,2},{1,3},{2,0},{3,1},{4,6},{5,7},{6,4},{7,5},{8,10},{9,11},{10,... | collective-permute-start | bytes 294920 | tf_op jit(solution)/shard_map/ppermute | solution.py:50
  18.8 24.8 %collective-permute-start.14 = (bf16[256,1024]{1,0:T(8,128)(2,1)S(1)}, bf16[256,1024]{1,0:T(8,128)(2,1)S(1)}, u32[]{:S(2)}, u32[]{:S(2)}) collective-permute-start(bf16[256,1024]{1,0:T(8,128)(2,1)S(1)} %copy-done.2), channel_id=1, source_target_pairs={{0,1},{1,0},{2,3},{3,2},{4,5},{5,4},{6,7},{7,6},{8,9},{9,8},{10,11... | collective-permute-start | bytes 1572872 | tf_op jit(solution)/shard_map/ppermute | solution.py:50
  18.8 5.1 %collective-permute-start.7 = (bf16[64,1024]{1,0:T(8,128)(2,1)S(1)}, bf16[64,1024]{1,0:T(8,128)(2,1)S(1)}, u32[]{:S(2)}, u32[]{:S(2)}) collective-permute-start(bf16[64,1024]{1,0:T(8,128)(2,1)S(1)} %copy-done.7), channel_id=1, source_target_pairs={{0,1},{1,0},{2,3},{3,2},{4,5},{5,4},{6,7},{7,6},{8,9},{9,8},{10,11... | collective-permute-start | bytes 393224 | tf_op jit(solution)/shard_map/ppermute | solution.py:50
  22.4 1.3 %collective-permute-start.23 = (bf16[64,768]{1,0:T(8,128)(2,1)S(1)}, bf16[64,768]{1,0:T(8,128)(2,1)S(1)}, u32[]{:S(2)}, u32[]{:S(2)}) collective-permute-start(bf16[64,768]{1,0:T(8,128)(2,1)S(1)} %get-tuple-element.31.refs_0_), channel_id=1, source_target_pairs={{0,1},{1,0},{2,3},{3,2},{4,5},{5,4},{6,7},{7,6},{8,9},{9,8},{10,11... | collective-permute-start | bytes 294920 | tf_op jit(solution)/shard_map/ppermute | solution.py:50
  22.4 3.1 %collective-permute-start.8 = (bf16[64,1024]{1,0:T(8,128)(2,1)S(1)}, bf16[64,1024]{1,0:T(8,128)(2,1)S(1)}, u32[]{:S(2)}, u32[]{:S(2)}) collective-permute-start(bf16[64,1024]{1,0:T(8,128)(2,1)S(1)} %collective-permute-done.6.refs_5_), channel_id=1, source_target_pairs={{0,1},{1,0},{2,3},{3,2},{4,5},{5,4},{6,7},{7,6},{8,9},{9,8},{10,11... | collective-permute-start | bytes 393224 | tf_op jit(solution)/shard_map/ppermute | solution.py:50
  22.9 1.3 %collective-permute-start.5 = (bf16[64,768]{1,0:T(8,128)(2,1)S(1)}, bf16[64,768]{1,0:T(8,128)(2,1)S(1)}, u32[]{:S(2)}, u32[]{:S(2)}) collective-permute-start(bf16[64,768]{1,0:T(8,128)(2,1)S(1)} %collective-permute-done.3.refs_1_), channel_id=1, source_target_pairs={{0,1},{1,0},{2,3},{3,2},{4,5},{5,4},{6,7},{7,6},{8,9},{9,8},{10,11... | collective-permute-start | bytes 294920 | tf_op jit(solution)/shard_map/ppermute | solution.py:50
  23.7 21.0 %collective-permute-start.15 = (bf16[256,1024]{1,0:T(8,128)(2,1)S(1)}, bf16[256,1024]{1,0:T(8,128)(2,1)S(1)}, u32[]{:S(2)}, u32[]{:S(2)}) collective-permute-start(bf16[256,1024]{1,0:T(8,128)(2,1)S(1)} %assemble.1.refs_5_.refs_4_), channel_id=1, source_target_pairs={{0,1},{1,0},{2,3},{3,2},{4,5},{5,4},{6,7},{7,6},{8,9},{9,8},{10,11... | collective-permute-start | bytes 1572872 | tf_op jit(solution)/shard_map/ppermute | solution.py:50
  23.9 5.5 %collective-permute-start.24 = (bf16[64,768]{1,0:T(8,128)(2,1)S(1)}, bf16[64,768]{1,0:T(8,128)(2,1)S(1)}, u32[]{:S(2)}, u32[]{:S(2)}) collective-permute-start(bf16[64,768]{1,0:T(8,128)(2,1)S(1)} %collective-permute-done.22.refs_1_), channel_id=1, source_target_pairs={{0,1},{1,0},{2,3},{3,2},{4,5},{5,4},{6,7},{7,6},{8,9},{9,8},{10,11... | collective-permute-start | bytes 294920 | tf_op jit(solution)/shard_map/ppermute | solution.py:50
  24.2 2.7 %copy-start.1 = (bf16[768,1024]{1,0:T(8,128)(2,1)S(1)}, bf16[768,1024]{1,0:T(8,128)(2,1)}, u32[]{:S(2)}) copy-start(bf16[768,1024]{1,0:T(8,128)(2,1)} %patch_ref.5) | copy-start | bytes 4718596
  24.2 2.7 %copy-start.5 = (f32[3,1024]{1,0:T(4,128)S(1)}, f32[3,1024]{1,0:T(4,128)}, u32[]{:S(2)}) copy-start(f32[3,1024]{1,0:T(4,128)} %gains_ref.13) | copy-start | bytes 36868
  24.2 8.3 %collective-permute-start.16 = (bf16[64,768]{1,0:T(8,128)(2,1)S(1)}, bf16[64,768]{1,0:T(8,128)(2,1)S(1)}, u32[]{:S(2)}, u32[]{:S(2)}) collective-permute-start(bf16[64,768]{1,0:T(8,128)(2,1)S(1)} %get-tuple-element.28.refs_0_), channel_id=1, source_target_pairs={{0,2},{1,3},{2,0},{3,1},{4,6},{5,7},{6,4},{7,5},{8,10},{9,11},{10,... | collective-permute-start | bytes 294920 | tf_op jit(solution)/shard_map/ppermute | solution.py:50
  25.5 8.4 %collective-permute-start.17 = (bf16[64,768]{1,0:T(8,128)(2,1)S(1)}, bf16[64,768]{1,0:T(8,128)(2,1)S(1)}, u32[]{:S(2)}, u32[]{:S(2)}) collective-permute-start(bf16[64,768]{1,0:T(8,128)(2,1)S(1)} %get-tuple-element.28.refs_0_), channel_id=1, source_target_pairs={{0,1},{1,0},{2,3},{3,2},{4,5},{5,4},{6,7},{7,6},{8,9},{9,8},{10,11... | collective-permute-start | bytes 294920 | tf_op jit(solution)/shard_map/ppermute | solution.py:50
  29.3 9.0 %collective-permute-start.9 = (bf16[256,256]{1,0:T(8,128)(2,1)S(1)}, bf16[256,256]{1,0:T(8,128)(2,1)S(1)}, u32[]{:S(2)}, u32[]{:S(2)}) collective-permute-start(bf16[256,256]{1,0:T(8,128)(2,1)S(1)} %get-tuple-element.26.refs_0_), channel_id=1, source_target_pairs={{0,2},{1,3},{2,0},{3,1},{4,6},{5,7},{6,4},{7,5},{8,10},{9,11},{10,... | collective-permute-start | bytes 393224 | tf_op jit(solution)/shard_map/ppermute | solution.py:50
  32.5 5.8 %collective-permute-start.25 = (bf16[256,256]{1,0:T(8,128)(2,1)S(1)}, bf16[256,256]{1,0:T(8,128)(2,1)S(1)}, u32[]{:S(2)}, u32[]{:S(2)}) collective-permute-start(bf16[256,256]{1,0:T(8,128)(2,1)S(1)} %get-tuple-element.33.refs_0_), channel_id=1, source_target_pairs={{0,2},{1,3},{2,0},{3,1},{4,6},{5,7},{6,4},{7,5},{8,10},{9,11},{10,... | collective-permute-start | bytes 393224 | tf_op jit(solution)/shard_map/ppermute | solution.py:50
  33.8 1.3 %collective-permute-start.18 = (bf16[64,768]{1,0:T(8,128)(2,1)S(1)}, bf16[64,768]{1,0:T(8,128)(2,1)S(1)}, u32[]{:S(2)}, u32[]{:S(2)}) collective-permute-start(bf16[64,768]{1,0:T(8,128)(2,1)S(1)} %collective-permute-done.16.refs_1_), channel_id=1, source_target_pairs={{0,1},{1,0},{2,3},{3,2},{4,5},{5,4},{6,7},{7,6},{8,9},{9,8},{10,11... | collective-permute-start | bytes 294920 | tf_op jit(solution)/shard_map/ppermute | solution.py:50
  37.5 5.6 %collective-permute-start.19 = (bf16[256,256]{1,0:T(8,128)(2,1)S(1)}, bf16[256,256]{1,0:T(8,128)(2,1)S(1)}, u32[]{:S(2)}, u32[]{:S(2)}) collective-permute-start(bf16[256,256]{1,0:T(8,128)(2,1)S(1)} %get-tuple-element.30.refs_0_), channel_id=1, source_target_pairs={{0,2},{1,3},{2,0},{3,1},{4,6},{5,7},{6,4},{7,5},{8,10},{9,11},{10,... | collective-permute-start | bytes 393224 | tf_op jit(solution)/shard_map/ppermute | solution.py:50
  38.3 4.8 %collective-permute-start.26 = (bf16[256,256]{1,0:T(8,128)(2,1)S(1)}, bf16[256,256]{1,0:T(8,128)(2,1)S(1)}, u32[]{:S(2)}, u32[]{:S(2)}) collective-permute-start(bf16[256,256]{1,0:T(8,128)(2,1)S(1)} %get-tuple-element.33.refs_0_), channel_id=1, source_target_pairs={{0,1},{1,0},{2,3},{3,2},{4,5},{5,4},{6,7},{7,6},{8,9},{9,8},{10,11... | collective-permute-start | bytes 393224 | tf_op jit(solution)/shard_map/ppermute | solution.py:50
  38.4 5.3 %collective-permute-start.27 = (bf16[256,256]{1,0:T(8,128)(2,1)S(1)}, bf16[256,256]{1,0:T(8,128)(2,1)S(1)}, u32[]{:S(2)}, u32[]{:S(2)}) collective-permute-start(bf16[256,256]{1,0:T(8,128)(2,1)S(1)} %collective-permute-done.25.refs_1_), channel_id=1, source_target_pairs={{0,1},{1,0},{2,3},{3,2},{4,5},{5,4},{6,7},{7,6},{8,9},{9,8},{10,11... | collective-permute-start | bytes 393224 | tf_op jit(solution)/shard_map/ppermute | solution.py:50
  43.1 4.2 %collective-permute-start.10 = (bf16[256,256]{1,0:T(8,128)(2,1)S(1)}, bf16[256,256]{1,0:T(8,128)(2,1)S(1)}, u32[]{:S(2)}, u32[]{:S(2)}) collective-permute-start(bf16[256,256]{1,0:T(8,128)(2,1)S(1)} %get-tuple-element.26.refs_0_), channel_id=1, source_target_pairs={{0,1},{1,0},{2,3},{3,2},{4,5},{5,4},{6,7},{7,6},{8,9},{9,8},{10,11... | collective-permute-start | bytes 393224 | tf_op jit(solution)/shard_map/ppermute | solution.py:50
  43.1 4.2 %collective-permute-start.11 = (bf16[256,256]{1,0:T(8,128)(2,1)S(1)}, bf16[256,256]{1,0:T(8,128)(2,1)S(1)}, u32[]{:S(2)}, u32[]{:S(2)}) collective-permute-start(bf16[256,256]{1,0:T(8,128)(2,1)S(1)} %collective-permute-done.9.refs_1_), channel_id=1, source_target_pairs={{0,1},{1,0},{2,3},{3,2},{4,5},{5,4},{6,7},{7,6},{8,9},{9,8},{10,11... | collective-permute-start | bytes 393224 | tf_op jit(solution)/shard_map/ppermute | solution.py:50
  43.6 5.7 %collective-permute-start.20 = (bf16[256,256]{1,0:T(8,128)(2,1)S(1)}, bf16[256,256]{1,0:T(8,128)(2,1)S(1)}, u32[]{:S(2)}, u32[]{:S(2)}) collective-permute-start(bf16[256,256]{1,0:T(8,128)(2,1)S(1)} %get-tuple-element.30.refs_0_), channel_id=1, source_target_pairs={{0,1},{1,0},{2,3},{3,2},{4,5},{5,4},{6,7},{7,6},{8,9},{9,8},{10,11... | collective-permute-start | bytes 393224 | tf_op jit(solution)/shard_map/ppermute | solution.py:50
  43.7 5.6 %collective-permute-start.21 = (bf16[256,256]{1,0:T(8,128)(2,1)S(1)}, bf16[256,256]{1,0:T(8,128)(2,1)S(1)}, u32[]{:S(2)}, u32[]{:S(2)}) collective-permute-start(bf16[256,256]{1,0:T(8,128)(2,1)S(1)} %collective-permute-done.19.refs_1_), channel_id=1, source_target_pairs={{0,1},{1,0},{2,3},{3,2},{4,5},{5,4},{6,7},{7,6},{8,9},{9,8},{10,11... | collective-permute-start | bytes 393224 | tf_op jit(solution)/shard_map/ppermute | solution.py:50
  44.1 1.6 %copy-start = (bf16[1024,1024]{1,0:T(8,128)(2,1)S(1)}, bf16[1024,1024]{1,0:T(8,128)(2,1)}, u32[]{:S(2)}) copy-start(bf16[1024,1024]{1,0:T(8,128)(2,1)} %up_ref.5) | copy-start | bytes 6291460
  49.3 2.0 %copy-start.3 = (bf16[1024,1024]{1,0:T(8,128)(2,1)S(1)}, bf16[1024,1024]{1,0:T(8,128)(2,1)}, u32[]{:S(2)}) copy-start(bf16[1024,1024]{1,0:T(8,128)(2,1)} %down_ref.1) | copy-start | bytes 6291460
  51.3 28.2 %copy-start.6 = (f32[2]{0:T(128)S(1)}, f32[2]{0:T(128)}, u32[]{:S(2)}) copy-start(f32[2]{0:T(128)} %params_ref.1) | copy-start | bytes 28
  51.3 29.0 %copy-start.4 = (bf16[1024,1024]{1,0:T(8,128)(2,1)S(1)}, bf16[1024,1024]{1,0:T(8,128)(2,1)}, u32[]{:S(2)}) copy-start(bf16[1024,1024]{1,0:T(8,128)(2,1)} %weight_ref.1) | copy-start | bytes 6291460
  51.7 1.2 %collective-permute-start.28 = (f32[3,1024]{1,0:T(4,128)S(1)}, f32[3,1024]{1,0:T(4,128)S(1)}, u32[]{:S(2)}, u32[]{:S(2)}) collective-permute-start(f32[3,1024]{1,0:T(4,128)S(1)} %reduce.1.own_ref), channel_id=1, source_target_pairs={{0,1},{1,0},{2,3},{3,2},{4,5},{5,4},{6,7},{7,6},{8,9},{9,8},{10,11... | collective-permute-start | bytes 36872 | tf_op jit(solution)/shard_map/ppermute | solution.py:50
  52.9 3.7 %collective-permute-start.29 = (f32[3,1024]{1,0:T(4,128)S(1)}, f32[3,1024]{1,0:T(4,128)S(1)}, u32[]{:S(2)}, u32[]{:S(2)}) collective-permute-start(f32[3,1024]{1,0:T(4,128)S(1)} %add.2.own_ref), channel_id=1, source_target_pairs={{0,2},{1,3},{2,0},{3,1},{4,6},{5,7},{6,4},{7,5},{8,10},{9,11},{10,... | collective-permute-start | bytes 36872 | tf_op jit(solution)/shard_map/ppermute | solution.py:50
  56.7 3.7 %collective-permute-start.30 = (f32[1,3,1024]{2,1,0:T(4,128)S(1)}, f32[1,3,1024]{2,1,0:T(4,128)S(1)}, u32[]{:S(2)}, u32[]{:S(2)}) collective-permute-start(f32[1,3,1024]{2,1,0:T(4,128)S(1)} %bitcast.1), channel_id=1, source_target_pairs={{0,4},{4,0},{8,12},{12,8},{16,20},{20,16},{24,28},{28,24},{1,5},{5... | collective-permute-start | bytes 36872 | tf_op jit(solution)/shard_map/ppermute | solution.py:50
  60.4 3.9 %collective-permute-start.31 = (f32[2,3,1024]{2,1,0:T(4,128)S(1)}, f32[2,3,1024]{2,1,0:T(4,128)S(1)}, u32[]{:S(2)}, u32[]{:S(2)}) collective-permute-start(f32[2,3,1024]{2,1,0:T(4,128)S(1)} %shard_map.149.own_ref), channel_id=1, source_target_pairs={{0,8},{4,12},{8,0},{12,4},{16,24},{20,28},{24,16},{28,20},{1,9},{5... | collective-permute-start | bytes 73736 | tf_op jit(solution)/shard_map/ppermute | solution.py:50
  64.3 16.0 %collective-permute-start.32 = (f32[4,3,1024]{2,1,0:T(4,128)S(1)}, f32[4,3,1024]{2,1,0:T(4,128)S(1)}, u32[]{:S(2)}, u32[]{:S(2)}) collective-permute-start(f32[4,3,1024]{2,1,0:T(4,128)S(1)} %shard_map.150.refs_0_), channel_id=1, source_target_pairs={{0,16},{4,20},{8,24},{12,28},{16,0},{20,4},{24,8},{28,12},{1,17},{... | collective-permute-start | bytes 147464 | tf_op jit(solution)/shard_map/ppermute | solution.py:50
  67.2 3.7 %collective-permute-start = (bf16[1,3,1152]{2,1,0:T(4,128)(2,1)S(1)}, bf16[1,3,1152]{2,1,0:T(4,128)(2,1)S(1)}, u32[]{:S(2)}, u32[]{:S(2)}) collective-permute-start(bf16[1,3,1152]{2,1,0:T(4,128)(2,1)S(1)} %get-tuple-element.18.own_ref), channel_id=1, source_target_pairs={{0,4},{4,0},{8,12},{12,8},{16,20},{20,16},{24,28},{28,24},{1,5},{5... | collective-permute-start | bytes 20744 | tf_op jit(solution)/shard_map/ppermute | solution.py:50
  70.8 3.8 %collective-permute-start.1 = (bf16[2,3,1152]{2,1,0:T(4,128)(2,1)S(1)}, bf16[2,3,1152]{2,1,0:T(4,128)(2,1)S(1)}, u32[]{:S(2)}, u32[]{:S(2)}) collective-permute-start(bf16[2,3,1152]{2,1,0:T(4,128)(2,1)S(1)} %shard_map.140.own_ref), channel_id=1, source_target_pairs={{0,8},{4,12},{8,0},{12,4},{16,24},{20,28},{24,16},{28,20},{1,9},{5... | collective-permute-start | bytes 41480 | tf_op jit(solution)/shard_map/ppermute | solution.py:50
  74.6 4.9 %collective-permute-start.2 = (bf16[4,3,1152]{2,1,0:T(4,128)(2,1)S(1)}, bf16[4,3,1152]{2,1,0:T(4,128)(2,1)S(1)}, u32[]{:S(2)}, u32[]{:S(2)}) collective-permute-start(bf16[4,3,1152]{2,1,0:T(4,128)(2,1)S(1)} %shard_map.141.first_ref), channel_id=1, source_target_pairs={{0,16},{4,20},{8,24},{12,28},{16,0},{20,4},{24,8},{28,12},{1,17},{... | collective-permute-start | bytes 82952 | tf_op jit(solution)/shard_map/ppermute | solution.py:50

commit v6 on v5

--- a/solution.py
+++ b/solution.py
@@ -102,13 +102,18 @@
     )(own, other)
 
 
+def trade_order(size):
+    order = [0]
+    for bit in bits_down(size):
+        order = order + [other ^ bit for other in order]
+    return order
+
+
 def double_stack(values, axis):
-    size = lax.axis_size(axis)
-    bit = 1
-    while 2 * bit < size:
+    *bits, last = bits_down(lax.axis_size(axis))
+    for bit in bits:
         values = join(values, swap(values, axis, bit))
-        bit *= 2
-    return values, swap(values, axis, bit)
+    return values, swap(values, axis, last)
 
 
 def pick_kernel(pieces, sel_hbm, dest_hbm, pixels_ref, cap_hbm, output_ref, pos_hbm, *refs):
@@ -245,7 +250,7 @@
     live, target = extra[:, 0:1], extra[:, 1:2]
     me = lax.axis_index("dp")
     offset = lax.broadcasted_iota(jnp.int32, (SEND_MOST, 1), 0)
-    spot = jnp.concatenate([(me ^ j) * SEND_MOST + offset for j in range(2 * half)], axis=0)
+    spot = jnp.concatenate([(me ^ j) * SEND_MOST + offset for j in trade_order(2 * half)], axis=0)
     mine = (live > 0.0) & (target == me.astype(F32))
     mine = jnp.where(mine, 1.0, 0.0)
     count = rows.shape[0]

time: 81.9 us -> 80.5 us (0.983)
  waiting for transfers between devices: 37.1 us -> 32.1 us
  starting transfers between devices: 23.4 us -> 26.9 us
    ppermute x33, waiting for transfers between devices: 37.1 us -> 32.1 us  [swap(): return lax.ppermute(values, axis, [(i, i ^ bit) for i in range(size)])]
    ppermute x33, starting transfers between devices: 23.4 us -> 26.9 us  [swap(): return lax.ppermute(values, axis, [(i, i ^ bit) for i in range(size)])]
where the time goes in v6:
time: 80.5 us; the launch traced here: 80.3 us
  waiting for transfers between devices  32.1 us (40%)
  starting transfers between devices  26.9 us (33%)
  Pallas kernels  19.4 us (24%)
  local copies, waits for them, and re-layouts  1.03 us (1%)
  between operations  0.84 us (1%)
    ppermute x33, waiting for transfers between devices, swap(): return lax.ppermute(values, axis, [(i, i ^ bit) for i in range(size)])  32.1 us
    ppermute x33, starting transfers between devices, swap(): return lax.ppermute(values, axis, [(i, i ^ bit) for i in range(size)])  26.9 us
    pallas_call x3, Pallas kernels, attend(): pl.pallas_call(functools.partial(attend_kernel, shards), out_shape=(jax.S...  7.16 us
    pallas_call x3, Pallas kernels, expand(): pl.pallas_call(functools.partial(expand_kernel, tuple(order), tuple(which...  5.49 us
    pallas_call x1, Pallas kernels, pick(): pl.pallas_call(functools.partial(pick_kernel, pieces), out_shape=tuple((j...  2.07 us
  transfers between devices with their start and end apart: 33, of which 13 were waited for; matrix products, arithmetic and copies ran while one was open for 0% of the time, Pallas kernels for 17%

profile of v6, /device:TPU:0, one launch (start us, length us, event | category | flops | bytes accessed | tf_op | source)
XLA Modules:
  0.0 80.3 jit_solution(11828628280664704196)
XLA Ops:
  0.7 2.1 %pick.1 = (bf16[64,768]{1,0:T(8,128)(2,1)S(1)}, bf16[64,768]{1,0:T(8,128)(2,1)S(1)}, bf16[64,768]{1,0:T(8,128)(2,1)S(1)}, bf16[1,3,1152]{2,1,0:T(4,128)(2,1)S(1)...) custom-call(s32[16]{0:T(128)} %sel_hbm.1, s32[16]{0:T(128)} %dest_hbm.1, bf16[16,64,768]{2,1,0:T(8,128)(2,1)} %pixels_ref.1, ...), custom_call_target="tpu_custom_call" | custom-call | tf_op jit(solution)/shard_map/pick/pallas_call | solution.py:175
  2.7 3.0 %collective-permute-start.12 = (bf16[128,1024]{1,0:T(8,128)(2,1)S(1)}, bf16[128,1024]{1,0:T(8,128)(2,1)S(1)}, u32[]{:S(2)}, u32[]{:S(2)}) collective-permute-start(bf16[128,1024]{1,0:T(8,128)(2,1)S(1)} %get-tuple-element.27), channel_id=1, source_target_pairs={{0,2},{1,3},{2,0},{3,1},{4,6},{5,7},{6,4},{7,5},{8,10},{9,11},{10,... | collective-permute-start | bytes 786440 | tf_op jit(solution)/shard_map/ppermute | solution.py:50
  5.8 6.3 %collective-permute-done.12.refs_0_ = bf16[128,1024]{1,0:T(8,128)(2,1)S(1)} collective-permute-done((bf16[128,1024]{1,0:T(8,128)(2,1)S(1)}, bf16[128,1024]{1,0:T(8,128)(2,1)S(1)}, u32[]{:S(2)}, u32[]{:S(2)}) %collective-permute-start.12) | collective-permute-done | bytes 262176 | tf_op jit(solution)/shard_map/ppermute | solution.py:50
  12.1 1.8 %collective-permute-start.13 = (bf16[128,1024]{1,0:T(8,128)(2,1)S(1)}, bf16[128,1024]{1,0:T(8,128)(2,1)S(1)}, u32[]{:S(2)}, u32[]{:S(2)}) collective-permute-start(bf16[128,1024]{1,0:T(8,128)(2,1)S(1)} %collective-permute-done.12.refs_0_), channel_id=1, source_target_pairs={{0,4},{4,0},{8,12},{12,8},{16,20},{20,16},{24,28},{28,24},{1,5},{5... | collective-permute-start | bytes 786440 | tf_op jit(solution)/shard_map/ppermute | solution.py:50
  13.8 1.5 %collective-permute-start.3 = (bf16[64,768]{1,0:T(8,128)(2,1)S(1)}, bf16[64,768]{1,0:T(8,128)(2,1)S(1)}, u32[]{:S(2)}, u32[]{:S(2)}) collective-permute-start(bf16[64,768]{1,0:T(8,128)(2,1)S(1)} %get-tuple-element.23.refs_0_), channel_id=1, source_target_pairs={{0,2},{1,3},{2,0},{3,1},{4,6},{5,7},{6,4},{7,5},{8,10},{9,11},{10,... | collective-permute-start | bytes 294920 | tf_op jit(solution)/shard_map/ppermute | solution.py:50
  15.3 0.5 collective-permute-start.6
  15.9 1.5 %collective-permute-start.22 = (bf16[64,768]{1,0:T(8,128)(2,1)S(1)}, bf16[64,768]{1,0:T(8,128)(2,1)S(1)}, u32[]{:S(2)}, u32[]{:S(2)}) collective-permute-start(bf16[64,768]{1,0:T(8,128)(2,1)S(1)} %get-tuple-element.31.refs_0_), channel_id=1, source_target_pairs={{0,2},{1,3},{2,0},{3,1},{4,6},{5,7},{6,4},{7,5},{8,10},{9,11},{10,... | collective-permute-start | bytes 294920 | tf_op jit(solution)/shard_map/ppermute | solution.py:50
  17.4 1.4 %collective-permute-done.3.refs_1_ = bf16[64,768]{1,0:T(8,128)(2,1)S(1)} collective-permute-done((bf16[64,768]{1,0:T(8,128)(2,1)S(1)}, bf16[64,768]{1,0:T(8,128)(2,1)S(1)}, u32[]{:S(2)}, u32[]{:S(2)}) %collective-permute-start.3) | collective-permute-done | bytes 98336 | tf_op jit(solution)/shard_map/ppermute | solution.py:50
  18.8 0.5 collective-permute-start.7
  19.3 3.1 %collective-permute-done.22.refs_1_ = bf16[64,768]{1,0:T(8,128)(2,1)S(1)} collective-permute-done((bf16[64,768]{1,0:T(8,128)(2,1)S(1)}, bf16[64,768]{1,0:T(8,128)(2,1)S(1)}, u32[]{:S(2)}, u32[]{:S(2)}) %collective-permute-start.22) | collective-permute-done | bytes 98336 | tf_op jit(solution)/shard_map/ppermute | solution.py:50
  22.4 0.5 collective-permute-start.8
  23.0 0.7 collective-permute-done.23.refs_2_
  23.9 0.4 collective-permute-start.24
  24.2 1.2 %collective-permute-start.16 = (bf16[64,768]{1,0:T(8,128)(2,1)S(1)}, bf16[64,768]{1,0:T(8,128)(2,1)S(1)}, u32[]{:S(2)}, u32[]{:S(2)}) collective-permute-start(bf16[64,768]{1,0:T(8,128)(2,1)S(1)} %get-tuple-element.28.refs_0_), channel_id=1, source_target_pairs={{0,2},{1,3},{2,0},{3,1},{4,6},{5,7},{6,4},{7,5},{8,10},{9,11},{10,... | collective-permute-start | bytes 294920 | tf_op jit(solution)/shard_map/ppermute | solution.py:50
  25.5 1.4 %load.1.qkv_ref = bf16[3,1024,256]{2,1,0:T(8,128)(2,1)S(1)} custom-call(bf16[3,1024,256]{2,1,0:T(8,128)(2,1)} %source_ref.1), custom_call_target="tpu_custom_call" | custom-call | tf_op jit(solution)/shard_map/load/pallas_call | solution.py:209
  26.9 2.4 %shard_map.142 = (f32[256,1024]{1,0:T(8,128)S(1)}, bf16[256,256]{1,0:T(8,128)(2,1)S(1)}) custom-call(f32[3,1024]{1,0:T(4,128)S(1)} %copy-done.5, bf16[768,1024]{1,0:T(8,128)(2,1)S(1)} %copy-done.1, bf16[3,1024,256]{2,1,0:T(8,128)(2,1)S(1)} %load.1.qkv_ref, bf16[64,768]{1,0:T(8,128)(2,1)S(1)} %get-tuple-element.23.refs_0_, ...), custom_call_target="tpu_custom_call" | custom-call | tf_op jit(solution)/shard_map/pallas_call | solution.py:330
  29.3 0.8 %collective-permute-start.9 = (bf16[256,256]{1,0:T(8,128)(2,1)S(1)}, bf16[256,256]{1,0:T(8,128)(2,1)S(1)}, u32[]{:S(2)}, u32[]{:S(2)}) collective-permute-start(bf16[256,256]{1,0:T(8,128)(2,1)S(1)} %get-tuple-element.26.refs_0_), channel_id=1, source_target_pairs={{0,2},{1,3},{2,0},{3,1},{4,6},{5,7},{6,4},{7,5},{8,10},{9,11},{10,... | collective-permute-start | bytes 393224 | tf_op jit(solution)/shard_map/ppermute | solution.py:50
  30.2 2.4 %shard_map.146 = (f32[256,1024]{1,0:T(8,128)S(1)}, bf16[256,256]{1,0:T(8,128)(2,1)S(1)}) custom-call(f32[3,1024]{1,0:T(4,128)S(1)} %copy-done.5, bf16[768,1024]{1,0:T(8,128)(2,1)S(1)} %copy-done.1, bf16[3,1024,256]{2,1,0:T(8,128)(2,1)S(1)} %load.1.qkv_ref, bf16[64,768]{1,0:T(8,128)(2,1)S(1)} %get-tuple-element.31.refs_0_, ...), custom_call_target="tpu_custom_call" | custom-call | tf_op jit(solution)/shard_map/pallas_call | solution.py:330
  32.5 1.3 %collective-permute-start.25 = (bf16[256,256]{1,0:T(8,128)(2,1)S(1)}, bf16[256,256]{1,0:T(8,128)(2,1)S(1)}, u32[]{:S(2)}, u32[]{:S(2)}) collective-permute-start(bf16[256,256]{1,0:T(8,128)(2,1)S(1)} %get-tuple-element.33.refs_0_), channel_id=1, source_target_pairs={{0,2},{1,3},{2,0},{3,1},{4,6},{5,7},{6,4},{7,5},{8,10},{9,11},{10,... | collective-permute-start | bytes 393224 | tf_op jit(solution)/shard_map/ppermute | solution.py:50
  33.8 1.3 %collective-permute-done.18.refs_3_ = bf16[64,768]{1,0:T(8,128)(2,1)S(1)} collective-permute-done((bf16[64,768]{1,0:T(8,128)(2,1)S(1)}, bf16[64,768]{1,0:T(8,128)(2,1)S(1)}, u32[]{:S(2)}, u32[]{:S(2)}) %collective-permute-start.18) | collective-permute-done | bytes 98336 | tf_op jit(solution)/shard_map/ppermute | solution.py:50
  35.1 2.4 %shard_map.144 = (f32[256,1024]{1,0:T(8,128)S(1)}, bf16[256,256]{1,0:T(8,128)(2,1)S(1)}) custom-call(f32[3,1024]{1,0:T(4,128)S(1)} %copy-done.5, bf16[768,1024]{1,0:T(8,128)(2,1)S(1)} %copy-done.1, bf16[3,1024,256]{2,1,0:T(8,128)(2,1)S(1)} %load.1.qkv_ref, bf16[64,768]{1,0:T(8,128)(2,1)S(1)} %get-tuple-element.28.refs_0_, ...), custom_call_target="tpu_custom_call" | custom-call | tf_op jit(solution)/shard_map/pallas_call | solution.py:330
  37.5 0.8 %collective-permute-start.19 = (bf16[256,256]{1,0:T(8,128)(2,1)S(1)}, bf16[256,256]{1,0:T(8,128)(2,1)S(1)}, u32[]{:S(2)}, u32[]{:S(2)}) collective-permute-start(bf16[256,256]{1,0:T(8,128)(2,1)S(1)} %get-tuple-element.30.refs_0_), channel_id=1, source_target_pairs={{0,2},{1,3},{2,0},{3,1},{4,6},{5,7},{6,4},{7,5},{8,10},{9,11},{10,... | collective-permute-start | bytes 393224 | tf_op jit(solution)/shard_map/ppermute | solution.py:50
  38.4 0.5 collective-permute-start.27
  38.9 4.2 %collective-permute-done.19.refs_1_ = bf16[256,256]{1,0:T(8,128)(2,1)S(1)} collective-permute-done((bf16[256,256]{1,0:T(8,128)(2,1)S(1)}, bf16[256,256]{1,0:T(8,128)(2,1)S(1)}, u32[]{:S(2)}, u32[]{:S(2)}) %collective-permute-start.19) | collective-permute-done | bytes 131104 | tf_op jit(solution)/shard_map/ppermute | solution.py:50
  43.1 0.5 collective-permute-start.11
  43.7 0.4 collective-permute-start.21
  44.1 0.6 shard_map.147.hidden_ref
  44.7 1.0 %copy-done = bf16[1024,1024]{1,0:T(8,128)(2,1)S(1)} copy-done((bf16[1024,1024]{1,0:T(8,128)(2,1)S(1)}, bf16[1024,1024]{1,0:T(8,128)(2,1)}, u32[]{:S(2)}) %copy-start) | copy-done | bytes 2097176
  45.7 1.6 %shard_map.148.refs_2_ = f32[2,1024]{1,0:T(2,128)S(1)} custom-call(f32[3,1024]{1,0:T(4,128)S(1)} %copy-done.5, bf16[1024,1024]{1,0:T(8,128)(2,1)S(1)} %copy-done, f32[256,1024]{1,0:T(8,128)S(1)} %shard_map.147.hidden_ref, bf16[256,256]{1,0:T(8,128)(2,1)S(1)} %collective-permute-done.27.refs_0_, bf16[256,1024]{1,0:T(8,128)(2,1)S(1)} %collective-permute-done.15.refs_7_.refs_1_), custom_call_target="tpu_custom_call" | custom-call | tf_op jit(solution)/shard_map/pallas_call | solution.py:386
  47.3 2.0 %shard_map.143.refs_0_ = f32[2,1024]{1,0:T(2,128)S(1)} custom-call(f32[3,1024]{1,0:T(4,128)S(1)} %copy-done.5, bf16[1024,1024]{1,0:T(8,128)(2,1)S(1)} %copy-done, f32[256,1024]{1,0:T(8,128)S(1)} %get-tuple-element.25.hidden_ref, bf16[256,256]{1,0:T(8,128)(2,1)S(1)} %get-tuple-element.26.refs_0_, bf16[256,256]{1,0:T(8,128)(2,1)S(1)} %collective-permute-done.9.refs_1_, ...), custom_call_target="tpu_custom_call" | custom-call | tf_op jit(solution)/shard_map/pallas_call | solution.py:386
  49.3 2.0 %shard_map.145.refs_1_ = f32[2,1024]{1,0:T(2,128)S(1)} custom-call(f32[3,1024]{1,0:T(4,128)S(1)} %copy-done.5, bf16[1024,1024]{1,0:T(8,128)(2,1)S(1)} %copy-done, f32[256,1024]{1,0:T(8,128)S(1)} %get-tuple-element.29.hidden_ref, bf16[256,256]{1,0:T(8,128)(2,1)S(1)} %get-tuple-element.30.refs_0_, bf16[256,256]{1,0:T(8,128)(2,1)S(1)} %collective-permute-done.19.refs_1_, ...), custom_call_target="tpu_custom_call" | custom-call | tf_op jit(solution)/shard_map/pallas_call | solution.py:386
  51.3 0.4 reduce.1.own_ref
  51.8 1.1 %collective-permute-done.28.other_ref = f32[3,1024]{1,0:T(4,128)S(1)} collective-permute-done((f32[3,1024]{1,0:T(4,128)S(1)}, f32[3,1024]{1,0:T(4,128)S(1)}, u32[]{:S(2)}, u32[]{:S(2)}) %collective-permute-start.28) | collective-permute-done | bytes 12320 | tf_op jit(solution)/shard_map/ppermute | solution.py:50
  52.9 0.8 collective-permute-start.29
  53.7 3.0 %collective-permute-done.29.other_ref = f32[3,1024]{1,0:T(4,128)S(1)} collective-permute-done((f32[3,1024]{1,0:T(4,128)S(1)}, f32[3,1024]{1,0:T(4,128)S(1)}, u32[]{:S(2)}, u32[]{:S(2)}) %collective-permute-start.29) | collective-permute-done | bytes 12320 | tf_op jit(solution)/shard_map/ppermute | solution.py:50
  56.7 2.6 %collective-permute-start.30 = (f32[1,3,1024]{2,1,0:T(4,128)S(1)}, f32[1,3,1024]{2,1,0:T(4,128)S(1)}, u32[]{:S(2)}, u32[]{:S(2)}) collective-permute-start(f32[1,3,1024]{2,1,0:T(4,128)S(1)} %bitcast.1), channel_id=1, source_target_pairs={{0,16},{4,20},{8,24},{12,28},{16,0},{20,4},{24,8},{28,12},{1,17},{... | collective-permute-start | bytes 36872 | tf_op jit(solution)/shard_map/ppermute | solution.py:50
  59.2 2.1 %collective-permute-done.30.other_ref = f32[1,3,1024]{2,1,0:T(4,128)S(1)} collective-permute-done((f32[1,3,1024]{2,1,0:T(4,128)S(1)}, f32[1,3,1024]{2,1,0:T(4,128)S(1)}, u32[]{:S(2)}, u32[]{:S(2)}) %collective-permute-start.30) | collective-permute-done | bytes 12320 | tf_op jit(solution)/shard_map/ppermute | solution.py:50
  61.3 1.6 %collective-permute-start.31 = (f32[2,3,1024]{2,1,0:T(4,128)S(1)}, f32[2,3,1024]{2,1,0:T(4,128)S(1)}, u32[]{:S(2)}, u32[]{:S(2)}) collective-permute-start(f32[2,3,1024]{2,1,0:T(4,128)S(1)} %shard_map.149.own_ref), channel_id=1, source_target_pairs={{0,8},{4,12},{8,0},{12,4},{16,24},{20,28},{24,16},{28,20},{1,9},{5... | collective-permute-start | bytes 73736 | tf_op jit(solution)/shard_map/ppermute | solution.py:50
  62.9 2.3 %collective-permute-done.31.other_ref = f32[2,3,1024]{2,1,0:T(4,128)S(1)} collective-permute-done((f32[2,3,1024]{2,1,0:T(4,128)S(1)}, f32[2,3,1024]{2,1,0:T(4,128)S(1)}, u32[]{:S(2)}, u32[]{:S(2)}) %collective-permute-start.31) | collective-permute-done | bytes 24608 | tf_op jit(solution)/shard_map/ppermute | solution.py:50
  65.2 0.5 collective-permute-start.32
  65.7 2.6 %collective-permute-start = (bf16[1,3,1152]{2,1,0:T(4,128)(2,1)S(1)}, bf16[1,3,1152]{2,1,0:T(4,128)(2,1)S(1)}, u32[]{:S(2)}, u32[]{:S(2)}) collective-permute-start(bf16[1,3,1152]{2,1,0:T(4,128)(2,1)S(1)} %get-tuple-element.18.own_ref), channel_id=1, source_target_pairs={{0,16},{4,20},{8,24},{12,28},{16,0},{20,4},{24,8},{28,12},{1,17},{... | collective-permute-start | bytes 20744 | tf_op jit(solution)/shard_map/ppermute | solution.py:50
  68.3 2.0 %collective-permute-done.other_ref = bf16[1,3,1152]{2,1,0:T(4,128)(2,1)S(1)} collective-permute-done((bf16[1,3,1152]{2,1,0:T(4,128)(2,1)S(1)}, bf16[1,3,1152]{2,1,0:T(4,128)(2,1)S(1)}, u32[]{:S(2)}, u32[]{:S(2)}) %collective-permute-start) | collective-permute-done | bytes 6944 | tf_op jit(solution)/shard_map/ppermute | solution.py:50
  70.3 1.6 %collective-permute-start.1 = (bf16[2,3,1152]{2,1,0:T(4,128)(2,1)S(1)}, bf16[2,3,1152]{2,1,0:T(4,128)(2,1)S(1)}, u32[]{:S(2)}, u32[]{:S(2)}) collective-permute-start(bf16[2,3,1152]{2,1,0:T(4,128)(2,1)S(1)} %shard_map.140.own_ref), channel_id=1, source_target_pairs={{0,8},{4,12},{8,0},{12,4},{16,24},{20,28},{24,16},{28,20},{1,9},{5... | collective-permute-start | bytes 41480 | tf_op jit(solution)/shard_map/ppermute | solution.py:50
  71.9 2.2 %collective-permute-done.1.other_ref = bf16[2,3,1152]{2,1,0:T(4,128)(2,1)S(1)} collective-permute-done((bf16[2,3,1152]{2,1,0:T(4,128)(2,1)S(1)}, bf16[2,3,1152]{2,1,0:T(4,128)(2,1)S(1)}, u32[]{:S(2)}, u32[]{:S(2)}) %collective-permute-start.1) | collective-permute-done | bytes 13856 | tf_op jit(solution)/shard_map/ppermute | solution.py:50
  74.1 1.6 %collective-permute-start.2 = (bf16[4,3,1152]{2,1,0:T(4,128)(2,1)S(1)}, bf16[4,3,1152]{2,1,0:T(4,128)(2,1)S(1)}, u32[]{:S(2)}, u32[]{:S(2)}) collective-permute-start(bf16[4,3,1152]{2,1,0:T(4,128)(2,1)S(1)} %shard_map.141.first_ref), channel_id=1, source_target_pairs={{0,4},{4,0},{8,12},{12,8},{16,20},{20,16},{24,28},{28,24},{1,5},{5... | collective-permute-start | bytes 82952 | tf_op jit(solution)/shard_map/ppermute | solution.py:50
  75.7 2.4 %collective-permute-done.2.second_ref = bf16[4,3,1152]{2,1,0:T(4,128)(2,1)S(1)} collective-permute-done((bf16[4,3,1152]{2,1,0:T(4,128)(2,1)S(1)}, bf16[4,3,1152]{2,1,0:T(4,128)(2,1)S(1)}, u32[]{:S(2)}, u32[]{:S(2)}) %collective-permute-start.2) | collective-permute-done | bytes 27680 | tf_op jit(solution)/shard_map/ppermute | solution.py:50
  78.1 0.8 route.1
  78.9 1.4 %finish.1 = (f32[4,1024]{1,0:T(4,128)}, f32[4]{0:T(128)}) custom-call(f32[3,1024]{1,0:T(4,128)S(1)} %copy-done.5, bf16[1024,1024]{1,0:T(8,128)(2,1)S(1)} %copy-done.4, f32[24,1024]{1,0:T(8,128)S(1)} %get-tuple-element.19.cap_ref, f32[24,128]{1,0:T(8,128)S(1)} %get-tuple-element.20.slot_ref, f32[24,128]{1,0:T(8,128)S(1)} %get-tuple-element.21.live_ref, ...), custom_call_target="tpu_custom_call" | custom-call | tf_op jit(solution)/shard_map/finish/pallas_call | solution.py:456
  (53 shorter events, 0.6 us)
Async XLA Ops:
  0.6 18.2 %copy-start.2 = (bf16[256,1024]{1,0:T(8,128)(2,1)S(1)}, bf16[256,1024]{1,0:T(8,128)(2,1)}, u32[]{:S(2)}) copy-start(bf16[256,1024]{1,0:T(8,128)(2,1)} %refs_3_.1) | copy-start | bytes 1572868
  0.6 14.7 %copy-start.7 = (bf16[64,1024]{1,0:T(8,128)(2,1)S(1)}, bf16[64,1024]{1,0:T(8,128)(2,1)}, u32[]{:S(2)}) copy-start(bf16[64,1024]{1,0:T(8,128)(2,1)} %pos_hbm.1) | copy-start | bytes 393220
  2.7 9.3 %collective-permute-start.12 = (bf16[128,1024]{1,0:T(8,128)(2,1)S(1)}, bf16[128,1024]{1,0:T(8,128)(2,1)S(1)}, u32[]{:S(2)}, u32[]{:S(2)}) collective-permute-start(bf16[128,1024]{1,0:T(8,128)(2,1)S(1)} %get-tuple-element.27), channel_id=1, source_target_pairs={{0,2},{1,3},{2,0},{3,1},{4,6},{5,7},{6,4},{7,5},{8,10},{9,11},{10,... | collective-permute-start | bytes 786440 | tf_op jit(solution)/shard_map/ppermute | solution.py:50
  12.1 10.9 %collective-permute-start.13 = (bf16[128,1024]{1,0:T(8,128)(2,1)S(1)}, bf16[128,1024]{1,0:T(8,128)(2,1)S(1)}, u32[]{:S(2)}, u32[]{:S(2)}) collective-permute-start(bf16[128,1024]{1,0:T(8,128)(2,1)S(1)} %collective-permute-done.12.refs_0_), channel_id=1, source_target_pairs={{0,4},{4,0},{8,12},{12,8},{16,20},{20,16},{24,28},{28,24},{1,5},{5... | collective-permute-start | bytes 786440 | tf_op jit(solution)/shard_map/ppermute | solution.py:50
  13.8 5.0 %collective-permute-start.3 = (bf16[64,768]{1,0:T(8,128)(2,1)S(1)}, bf16[64,768]{1,0:T(8,128)(2,1)S(1)}, u32[]{:S(2)}, u32[]{:S(2)}) collective-permute-start(bf16[64,768]{1,0:T(8,128)(2,1)S(1)} %get-tuple-element.23.refs_0_), channel_id=1, source_target_pairs={{0,2},{1,3},{2,0},{3,1},{4,6},{5,7},{6,4},{7,5},{8,10},{9,11},{10,... | collective-permute-start | bytes 294920 | tf_op jit(solution)/shard_map/ppermute | solution.py:50
  15.3 7.1 %collective-permute-start.6 = (bf16[64,1024]{1,0:T(8,128)(2,1)S(1)}, bf16[64,1024]{1,0:T(8,128)(2,1)S(1)}, u32[]{:S(2)}, u32[]{:S(2)}) collective-permute-start(bf16[64,1024]{1,0:T(8,128)(2,1)S(1)} %copy-done.7), channel_id=1, source_target_pairs={{0,2},{1,3},{2,0},{3,1},{4,6},{5,7},{6,4},{7,5},{8,10},{9,11},{10,... | collective-permute-start | bytes 393224 | tf_op jit(solution)/shard_map/ppermute | solution.py:50
  15.9 2.9 %collective-permute-start.4 = (bf16[64,768]{1,0:T(8,128)(2,1)S(1)}, bf16[64,768]{1,0:T(8,128)(2,1)S(1)}, u32[]{:S(2)}, u32[]{:S(2)}) collective-permute-start(bf16[64,768]{1,0:T(8,128)(2,1)S(1)} %get-tuple-element.23.refs_0_), channel_id=1, source_target_pairs={{0,1},{1,0},{2,3},{3,2},{4,5},{5,4},{6,7},{7,6},{8,9},{9,8},{10,11... | collective-permute-start | bytes 294920 | tf_op jit(solution)/shard_map/ppermute | solution.py:50
  15.9 6.5 %collective-permute-start.22 = (bf16[64,768]{1,0:T(8,128)(2,1)S(1)}, bf16[64,768]{1,0:T(8,128)(2,1)S(1)}, u32[]{:S(2)}, u32[]{:S(2)}) collective-permute-start(bf16[64,768]{1,0:T(8,128)(2,1)S(1)} %get-tuple-element.31.refs_0_), channel_id=1, source_target_pairs={{0,2},{1,3},{2,0},{3,1},{4,6},{5,7},{6,4},{7,5},{8,10},{9,11},{10,... | collective-permute-start | bytes 294920 | tf_op jit(solution)/shard_map/ppermute | solution.py:50
  18.8 24.8 %collective-permute-start.14 = (bf16[256,1024]{1,0:T(8,128)(2,1)S(1)}, bf16[256,1024]{1,0:T(8,128)(2,1)S(1)}, u32[]{:S(2)}, u32[]{:S(2)}) collective-permute-start(bf16[256,1024]{1,0:T(8,128)(2,1)S(1)} %copy-done.2), channel_id=1, source_target_pairs={{0,1},{1,0},{2,3},{3,2},{4,5},{5,4},{6,7},{7,6},{8,9},{9,8},{10,11... | collective-permute-start | bytes 1572872 | tf_op jit(solution)/shard_map/ppermute | solution.py:50
  18.8 5.1 %collective-permute-start.7 = (bf16[64,1024]{1,0:T(8,128)(2,1)S(1)}, bf16[64,1024]{1,0:T(8,128)(2,1)S(1)}, u32[]{:S(2)}, u32[]{:S(2)}) collective-permute-start(bf16[64,1024]{1,0:T(8,128)(2,1)S(1)} %copy-done.7), channel_id=1, source_target_pairs={{0,1},{1,0},{2,3},{3,2},{4,5},{5,4},{6,7},{7,6},{8,9},{9,8},{10,11... | collective-permute-start | bytes 393224 | tf_op jit(solution)/shard_map/ppermute | solution.py:50
  22.4 1.3 %collective-permute-start.23 = (bf16[64,768]{1,0:T(8,128)(2,1)S(1)}, bf16[64,768]{1,0:T(8,128)(2,1)S(1)}, u32[]{:S(2)}, u32[]{:S(2)}) collective-permute-start(bf16[64,768]{1,0:T(8,128)(2,1)S(1)} %get-tuple-element.31.refs_0_), channel_id=1, source_target_pairs={{0,1},{1,0},{2,3},{3,2},{4,5},{5,4},{6,7},{7,6},{8,9},{9,8},{10,11... | collective-permute-start | bytes 294920 | tf_op jit(solution)/shard_map/ppermute | solution.py:50
  22.4 3.1 %collective-permute-start.8 = (bf16[64,1024]{1,0:T(8,128)(2,1)S(1)}, bf16[64,1024]{1,0:T(8,128)(2,1)S(1)}, u32[]{:S(2)}, u32[]{:S(2)}) collective-permute-start(bf16[64,1024]{1,0:T(8,128)(2,1)S(1)} %collective-permute-done.6.refs_5_), channel_id=1, source_target_pairs={{0,1},{1,0},{2,3},{3,2},{4,5},{5,4},{6,7},{7,6},{8,9},{9,8},{10,11... | collective-permute-start | bytes 393224 | tf_op jit(solution)/shard_map/ppermute | solution.py:50
  22.9 1.3 %collective-permute-start.5 = (bf16[64,768]{1,0:T(8,128)(2,1)S(1)}, bf16[64,768]{1,0:T(8,128)(2,1)S(1)}, u32[]{:S(2)}, u32[]{:S(2)}) collective-permute-start(bf16[64,768]{1,0:T(8,128)(2,1)S(1)} %collective-permute-done.3.refs_1_), channel_id=1, source_target_pairs={{0,1},{1,0},{2,3},{3,2},{4,5},{5,4},{6,7},{7,6},{8,9},{9,8},{10,11... | collective-permute-start | bytes 294920 | tf_op jit(solution)/shard_map/ppermute | solution.py:50
  23.7 21.0 %collective-permute-start.15 = (bf16[256,1024]{1,0:T(8,128)(2,1)S(1)}, bf16[256,1024]{1,0:T(8,128)(2,1)S(1)}, u32[]{:S(2)}, u32[]{:S(2)}) collective-permute-start(bf16[256,1024]{1,0:T(8,128)(2,1)S(1)} %assemble.1.refs_5_.refs_4_), channel_id=1, source_target_pairs={{0,1},{1,0},{2,3},{3,2},{4,5},{5,4},{6,7},{7,6},{8,9},{9,8},{10,11... | collective-permute-start | bytes 1572872 | tf_op jit(solution)/shard_map/ppermute | solution.py:50
  23.9 5.5 %collective-permute-start.24 = (bf16[64,768]{1,0:T(8,128)(2,1)S(1)}, bf16[64,768]{1,0:T(8,128)(2,1)S(1)}, u32[]{:S(2)}, u32[]{:S(2)}) collective-permute-start(bf16[64,768]{1,0:T(8,128)(2,1)S(1)} %collective-permute-done.22.refs_1_), channel_id=1, source_target_pairs={{0,1},{1,0},{2,3},{3,2},{4,5},{5,4},{6,7},{7,6},{8,9},{9,8},{10,11... | collective-permute-start | bytes 294920 | tf_op jit(solution)/shard_map/ppermute | solution.py:50
  24.2 2.7 %copy-start.1 = (bf16[768,1024]{1,0:T(8,128)(2,1)S(1)}, bf16[768,1024]{1,0:T(8,128)(2,1)}, u32[]{:S(2)}) copy-start(bf16[768,1024]{1,0:T(8,128)(2,1)} %patch_ref.5) | copy-start | bytes 4718596
  24.2 2.7 %copy-start.5 = (f32[3,1024]{1,0:T(4,128)S(1)}, f32[3,1024]{1,0:T(4,128)}, u32[]{:S(2)}) copy-start(f32[3,1024]{1,0:T(4,128)} %gains_ref.13) | copy-start | bytes 36868
  24.2 8.3 %collective-permute-start.16 = (bf16[64,768]{1,0:T(8,128)(2,1)S(1)}, bf16[64,768]{1,0:T(8,128)(2,1)S(1)}, u32[]{:S(2)}, u32[]{:S(2)}) collective-permute-start(bf16[64,768]{1,0:T(8,128)(2,1)S(1)} %get-tuple-element.28.refs_0_), channel_id=1, source_target_pairs={{0,2},{1,3},{2,0},{3,1},{4,6},{5,7},{6,4},{7,5},{8,10},{9,11},{10,... | collective-permute-start | bytes 294920 | tf_op jit(solution)/shard_map/ppermute | solution.py:50
  25.5 8.4 %collective-permute-start.17 = (bf16[64,768]{1,0:T(8,128)(2,1)S(1)}, bf16[64,768]{1,0:T(8,128)(2,1)S(1)}, u32[]{:S(2)}, u32[]{:S(2)}) collective-permute-start(bf16[64,768]{1,0:T(8,128)(2,1)S(1)} %get-tuple-element.28.refs_0_), channel_id=1, source_target_pairs={{0,1},{1,0},{2,3},{3,2},{4,5},{5,4},{6,7},{7,6},{8,9},{9,8},{10,11... | collective-permute-start | bytes 294920 | tf_op jit(solution)/shard_map/ppermute | solution.py:50
  29.3 9.0 %collective-permute-start.9 = (bf16[256,256]{1,0:T(8,128)(2,1)S(1)}, bf16[256,256]{1,0:T(8,128)(2,1)S(1)}, u32[]{:S(2)}, u32[]{:S(2)}) collective-permute-start(bf16[256,256]{1,0:T(8,128)(2,1)S(1)} %get-tuple-element.26.refs_0_), channel_id=1, source_target_pairs={{0,2},{1,3},{2,0},{3,1},{4,6},{5,7},{6,4},{7,5},{8,10},{9,11},{10,... | collective-permute-start | bytes 393224 | tf_op jit(solution)/shard_map/ppermute | solution.py:50
  32.5 5.8 %collective-permute-start.25 = (bf16[256,256]{1,0:T(8,128)(2,1)S(1)}, bf16[256,256]{1,0:T(8,128)(2,1)S(1)}, u32[]{:S(2)}, u32[]{:S(2)}) collective-permute-start(bf16[256,256]{1,0:T(8,128)(2,1)S(1)} %get-tuple-element.33.refs_0_), channel_id=1, source_target_pairs={{0,2},{1,3},{2,0},{3,1},{4,6},{5,7},{6,4},{7,5},{8,10},{9,11},{10,... | collective-permute-start | bytes 393224 | tf_op jit(solution)/shard_map/ppermute | solution.py:50
  33.8 1.3 %collective-permute-start.18 = (bf16[64,768]{1,0:T(8,128)(2,1)S(1)}, bf16[64,768]{1,0:T(8,128)(2,1)S(1)}, u32[]{:S(2)}, u32[]{:S(2)}) collective-permute-start(bf16[64,768]{1,0:T(8,128)(2,1)S(1)} %collective-permute-done.16.refs_1_), channel_id=1, source_target_pairs={{0,1},{1,0},{2,3},{3,2},{4,5},{5,4},{6,7},{7,6},{8,9},{9,8},{10,11... | collective-permute-start | bytes 294920 | tf_op jit(solution)/shard_map/ppermute | solution.py:50
  37.5 5.6 %collective-permute-start.19 = (bf16[256,256]{1,0:T(8,128)(2,1)S(1)}, bf16[256,256]{1,0:T(8,128)(2,1)S(1)}, u32[]{:S(2)}, u32[]{:S(2)}) collective-permute-start(bf16[256,256]{1,0:T(8,128)(2,1)S(1)} %get-tuple-element.30.refs_0_), channel_id=1, source_target_pairs={{0,2},{1,3},{2,0},{3,1},{4,6},{5,7},{6,4},{7,5},{8,10},{9,11},{10,... | collective-permute-start | bytes 393224 | tf_op jit(solution)/shard_map/ppermute | solution.py:50
  38.3 4.8 %collective-permute-start.26 = (bf16[256,256]{1,0:T(8,128)(2,1)S(1)}, bf16[256,256]{1,0:T(8,128)(2,1)S(1)}, u32[]{:S(2)}, u32[]{:S(2)}) collective-permute-start(bf16[256,256]{1,0:T(8,128)(2,1)S(1)} %get-tuple-element.33.refs_0_), channel_id=1, source_target_pairs={{0,1},{1,0},{2,3},{3,2},{4,5},{5,4},{6,7},{7,6},{8,9},{9,8},{10,11... | collective-permute-start | bytes 393224 | tf_op jit(solution)/shard_map/ppermute | solution.py:50
  38.4 5.3 %collective-permute-start.27 = (bf16[256,256]{1,0:T(8,128)(2,1)S(1)}, bf16[256,256]{1,0:T(8,128)(2,1)S(1)}, u32[]{:S(2)}, u32[]{:S(2)}) collective-permute-start(bf16[256,256]{1,0:T(8,128)(2,1)S(1)} %collective-permute-done.25.refs_1_), channel_id=1, source_target_pairs={{0,1},{1,0},{2,3},{3,2},{4,5},{5,4},{6,7},{7,6},{8,9},{9,8},{10,11... | collective-permute-start | bytes 393224 | tf_op jit(solution)/shard_map/ppermute | solution.py:50
  43.1 4.2 %collective-permute-start.10 = (bf16[256,256]{1,0:T(8,128)(2,1)S(1)}, bf16[256,256]{1,0:T(8,128)(2,1)S(1)}, u32[]{:S(2)}, u32[]{:S(2)}) collective-permute-start(bf16[256,256]{1,0:T(8,128)(2,1)S(1)} %get-tuple-element.26.refs_0_), channel_id=1, source_target_pairs={{0,1},{1,0},{2,3},{3,2},{4,5},{5,4},{6,7},{7,6},{8,9},{9,8},{10,11... | collective-permute-start | bytes 393224 | tf_op jit(solution)/shard_map/ppermute | solution.py:50
  43.1 4.2 %collective-permute-start.11 = (bf16[256,256]{1,0:T(8,128)(2,1)S(1)}, bf16[256,256]{1,0:T(8,128)(2,1)S(1)}, u32[]{:S(2)}, u32[]{:S(2)}) collective-permute-start(bf16[256,256]{1,0:T(8,128)(2,1)S(1)} %collective-permute-done.9.refs_1_), channel_id=1, source_target_pairs={{0,1},{1,0},{2,3},{3,2},{4,5},{5,4},{6,7},{7,6},{8,9},{9,8},{10,11... | collective-permute-start | bytes 393224 | tf_op jit(solution)/shard_map/ppermute | solution.py:50
  43.6 5.7 %collective-permute-start.20 = (bf16[256,256]{1,0:T(8,128)(2,1)S(1)}, bf16[256,256]{1,0:T(8,128)(2,1)S(1)}, u32[]{:S(2)}, u32[]{:S(2)}) collective-permute-start(bf16[256,256]{1,0:T(8,128)(2,1)S(1)} %get-tuple-element.30.refs_0_), channel_id=1, source_target_pairs={{0,1},{1,0},{2,3},{3,2},{4,5},{5,4},{6,7},{7,6},{8,9},{9,8},{10,11... | collective-permute-start | bytes 393224 | tf_op jit(solution)/shard_map/ppermute | solution.py:50
  43.7 5.6 %collective-permute-start.21 = (bf16[256,256]{1,0:T(8,128)(2,1)S(1)}, bf16[256,256]{1,0:T(8,128)(2,1)S(1)}, u32[]{:S(2)}, u32[]{:S(2)}) collective-permute-start(bf16[256,256]{1,0:T(8,128)(2,1)S(1)} %collective-permute-done.19.refs_1_), channel_id=1, source_target_pairs={{0,1},{1,0},{2,3},{3,2},{4,5},{5,4},{6,7},{7,6},{8,9},{9,8},{10,11... | collective-permute-start | bytes 393224 | tf_op jit(solution)/shard_map/ppermute | solution.py:50
  44.1 1.6 %copy-start = (bf16[1024,1024]{1,0:T(8,128)(2,1)S(1)}, bf16[1024,1024]{1,0:T(8,128)(2,1)}, u32[]{:S(2)}) copy-start(bf16[1024,1024]{1,0:T(8,128)(2,1)} %up_ref.5) | copy-start | bytes 6291460
  49.3 2.0 %copy-start.3 = (bf16[1024,1024]{1,0:T(8,128)(2,1)S(1)}, bf16[1024,1024]{1,0:T(8,128)(2,1)}, u32[]{:S(2)}) copy-start(bf16[1024,1024]{1,0:T(8,128)(2,1)} %down_ref.1) | copy-start | bytes 6291460
  51.3 26.8 %copy-start.6 = (f32[2]{0:T(128)S(1)}, f32[2]{0:T(128)}, u32[]{:S(2)}) copy-start(f32[2]{0:T(128)} %params_ref.1) | copy-start | bytes 28
  51.3 27.6 %copy-start.4 = (bf16[1024,1024]{1,0:T(8,128)(2,1)S(1)}, bf16[1024,1024]{1,0:T(8,128)(2,1)}, u32[]{:S(2)}) copy-start(bf16[1024,1024]{1,0:T(8,128)(2,1)} %weight_ref.1) | copy-start | bytes 6291460
  51.7 1.2 %collective-permute-start.28 = (f32[3,1024]{1,0:T(4,128)S(1)}, f32[3,1024]{1,0:T(4,128)S(1)}, u32[]{:S(2)}, u32[]{:S(2)}) collective-permute-start(f32[3,1024]{1,0:T(4,128)S(1)} %reduce.1.own_ref), channel_id=1, source_target_pairs={{0,1},{1,0},{2,3},{3,2},{4,5},{5,4},{6,7},{7,6},{8,9},{9,8},{10,11... | collective-permute-start | bytes 36872 | tf_op jit(solution)/shard_map/ppermute | solution.py:50
  52.9 3.7 %collective-permute-start.29 = (f32[3,1024]{1,0:T(4,128)S(1)}, f32[3,1024]{1,0:T(4,128)S(1)}, u32[]{:S(2)}, u32[]{:S(2)}) collective-permute-start(f32[3,1024]{1,0:T(4,128)S(1)} %add.2.own_ref), channel_id=1, source_target_pairs={{0,2},{1,3},{2,0},{3,1},{4,6},{5,7},{6,4},{7,5},{8,10},{9,11},{10,... | collective-permute-start | bytes 36872 | tf_op jit(solution)/shard_map/ppermute | solution.py:50
  56.7 4.6 %collective-permute-start.30 = (f32[1,3,1024]{2,1,0:T(4,128)S(1)}, f32[1,3,1024]{2,1,0:T(4,128)S(1)}, u32[]{:S(2)}, u32[]{:S(2)}) collective-permute-start(f32[1,3,1024]{2,1,0:T(4,128)S(1)} %bitcast.1), channel_id=1, source_target_pairs={{0,16},{4,20},{8,24},{12,28},{16,0},{20,4},{24,8},{28,12},{1,17},{... | collective-permute-start | bytes 36872 | tf_op jit(solution)/shard_map/ppermute | solution.py:50
  61.3 3.9 %collective-permute-start.31 = (f32[2,3,1024]{2,1,0:T(4,128)S(1)}, f32[2,3,1024]{2,1,0:T(4,128)S(1)}, u32[]{:S(2)}, u32[]{:S(2)}) collective-permute-start(f32[2,3,1024]{2,1,0:T(4,128)S(1)} %shard_map.149.own_ref), channel_id=1, source_target_pairs={{0,8},{4,12},{8,0},{12,4},{16,24},{20,28},{24,16},{28,20},{1,9},{5... | collective-permute-start | bytes 73736 | tf_op jit(solution)/shard_map/ppermute | solution.py:50
  65.2 13.6 %collective-permute-start.32 = (f32[4,3,1024]{2,1,0:T(4,128)S(1)}, f32[4,3,1024]{2,1,0:T(4,128)S(1)}, u32[]{:S(2)}, u32[]{:S(2)}) collective-permute-start(f32[4,3,1024]{2,1,0:T(4,128)S(1)} %shard_map.150.refs_0_), channel_id=1, source_target_pairs={{0,4},{4,0},{8,12},{12,8},{16,20},{20,16},{24,28},{28,24},{1,5},{5... | collective-permute-start | bytes 147464 | tf_op jit(solution)/shard_map/ppermute | solution.py:50
  65.7 4.6 %collective-permute-start = (bf16[1,3,1152]{2,1,0:T(4,128)(2,1)S(1)}, bf16[1,3,1152]{2,1,0:T(4,128)(2,1)S(1)}, u32[]{:S(2)}, u32[]{:S(2)}) collective-permute-start(bf16[1,3,1152]{2,1,0:T(4,128)(2,1)S(1)} %get-tuple-element.18.own_ref), channel_id=1, source_target_pairs={{0,16},{4,20},{8,24},{12,28},{16,0},{20,4},{24,8},{28,12},{1,17},{... | collective-permute-start | bytes 20744 | tf_op jit(solution)/shard_map/ppermute | solution.py:50
  70.3 3.8 %collective-permute-start.1 = (bf16[2,3,1152]{2,1,0:T(4,128)(2,1)S(1)}, bf16[2,3,1152]{2,1,0:T(4,128)(2,1)S(1)}, u32[]{:S(2)}, u32[]{:S(2)}) collective-permute-start(bf16[2,3,1152]{2,1,0:T(4,128)(2,1)S(1)} %shard_map.140.own_ref), channel_id=1, source_target_pairs={{0,8},{4,12},{8,0},{12,4},{16,24},{20,28},{24,16},{28,20},{1,9},{5... | collective-permute-start | bytes 41480 | tf_op jit(solution)/shard_map/ppermute | solution.py:50
  74.1 4.0 %collective-permute-start.2 = (bf16[4,3,1152]{2,1,0:T(4,128)(2,1)S(1)}, bf16[4,3,1152]{2,1,0:T(4,128)(2,1)S(1)}, u32[]{:S(2)}, u32[]{:S(2)}) collective-permute-start(bf16[4,3,1152]{2,1,0:T(4,128)(2,1)S(1)} %shard_map.141.first_ref), channel_id=1, source_target_pairs={{0,4},{4,0},{8,12},{12,8},{16,20},{20,16},{24,28},{28,24},{1,5},{5... | collective-permute-start | bytes 82952 | tf_op jit(solution)/shard_map/ppermute | solution.py:50
